TPU v7x, 128 devices: a 2x2x16 block of a 8x8x16 slice. The times are simulated.
128 devices in a mesh: samples: 4 (over x, y), px: 16 (over z), py: 2 (over core).
Axes of the slice: x: 2, y: 2, z: 16, core: 2. Of those that a mesh axis runs over, the one named last changes fastest.
The devices are a block of a 8x8x16 slice.
Arguments:
- source: float32 [2, 1024, 256, 256], P(None, 'samples', 'px', 'py'), parts along dimension 1, may hold values from -6 to 6
- speed: float32 [1024, 256, 256], P('samples', 'px', 'py'), parts along dimension 0, may hold values from 0.5 to 3
Outputs:
- solution: float32 [2, 1024, 256, 256], P(None, 'samples', 'px', 'py'), parts along dimension 1
There are 4 independent parts, one for each index of `samples`. A program takes and returns all parts, laid end to end along the dimension named above; each array names one. Nothing has to cross between parts.
All inputs are finite; a program needn't handle non-finite values.
Results may differ from a plain program's by a relative error of at most 0.00024.
Values sent between devices are 32-bit elements; how exact they have to be, the bound alone decides.
No kernel may reach another device: no remote copies, remote signals or barrier semaphores. Data moves between devices by JAX's collectives and lax.ppermute only.
A program may use at most 192 MiB of HBM per device.

v0:
```python
import jax
import jax.numpy as jnp
from jax import lax
from jax.sharding import PartitionSpec as P

NX = 256
NY = 256
NZ = 256


wave_square = 0.25
damping = 0.5
epsilon = 1e-06
highest = lax.Precision.HIGHEST


def padded_2(shard, sides, width):
    edges = {}
    for axis, dim in sides:
        size, length = (lax.axis_size(axis), shard.shape[dim])
        up = [(i, (i + 1) % size) for i in range(size - 1)]
        last = lax.slice_in_dim(shard, length - width, length, axis=dim)
        first = lax.slice_in_dim(shard, 0, width, axis=dim)
        edges[dim] = (
            lax.ppermute(last, axis, up),
            lax.ppermute(first, axis, [(b, a) for a, b in up]),
        )
    done = []
    for _, dim in sides:
        low, high = edges[dim]
        around = [(width, width) if d in done else (0, 0) for d in range(shard.ndim)]
        shard = jnp.concatenate([jnp.pad(low, around), shard, jnp.pad(high, around)], axis=dim)
        done.append(dim)
    return shard


def copy_for_each(shard, axis):
    size = lax.axis_size(axis)
    return lax.all_to_all(
        jnp.broadcast_to(shard[None], (size, *shard.shape)), axis, 0, 0, tiled=True
    )


def of_everyone(shard, axis):
    everything = copy_for_each(shard, axis)
    return jnp.sum(everything, axis=0)


def in_one(arrays, axis):
    ends = [0]
    for a in arrays:
        ends.append(ends[-1] + a.size)
    total = of_everyone(jnp.concatenate([a.ravel() for a in arrays]), axis)
    return tuple((total[b:e].reshape(a.shape) for a, b, e in zip(arrays, ends, ends[1:])))


def sine_table(length):
    positions = jnp.arange(length, dtype=jnp.float32) + 1.0
    phases = jnp.pi * positions[:, None] * positions[None, :] / (length + 1.0)
    return jnp.sqrt(2.0 / (length + 1.0)) * jnp.sin(phases)


def eigen_line(length, offset, number):
    positions = (
        jnp.arange(number, dtype=jnp.float32) + jnp.asarray(offset).astype(jnp.float32) + 1.0
    )
    sine_half = jnp.sin(jnp.pi * positions / (2.0 * (length + 1.0)))
    return 4.0 * sine_half * sine_half


def divide(values, eigen_x, eigen_y, eigen_z):
    shifted = eigen_x[:, None, None] + eigen_y[None, :, None] + eigen_z[None, None, :] - wave_square
    damped = damping * wave_square
    modulus = shifted * shifted + damped * damped
    real_part = (values[0] * shifted + values[1] * damped) / modulus
    imag_part = (values[1] * shifted - values[0] * damped) / modulus
    return jnp.stack([real_part, imag_part])


def apply_x(matrix, values):
    return jnp.einsum("ak,ckyz->cayz", matrix, values, precision=highest)


def apply_y(matrix, values):
    return jnp.einsum("ak,cxkz->cxaz", matrix, values, precision=highest)


def apply_z(matrix, values):
    return jnp.einsum("ak,cxyk->cxya", matrix, values, precision=highest)


def precondition(vector):
    matrix_x = sine_table(NX)
    matrix_y = sine_table(NY)
    matrix_z = sine_table(NZ)
    section_x = apply_x(matrix_x, vector)
    swapped = (lambda pieces: apply_y(matrix_y, pieces))(
        lax.all_to_all(section_x, "px", split_axis=1, concat_axis=2, tiled=True)
    )
    spectral = (lambda pieces: apply_z(matrix_z, pieces))(
        lax.all_to_all(swapped, "py", split_axis=2, concat_axis=3, tiled=True)
    )
    eigen_x = eigen_line(NX, lax.axis_index("px") * spectral.shape[1], spectral.shape[1])
    eigen_y = eigen_line(NY, lax.axis_index("py") * spectral.shape[2], spectral.shape[2])
    scaled = apply_z(matrix_z, divide(spectral, eigen_x, eigen_y, eigen_line(NZ, 0, NZ)))
    swapped = (lambda pieces: apply_y(matrix_y, pieces))(
        lax.all_to_all(scaled, "py", split_axis=3, concat_axis=2, tiled=True)
    )
    result = (lambda pieces: apply_x(matrix_x, pieces))(
        lax.all_to_all(swapped, "px", split_axis=2, concat_axis=1, tiled=True)
    )
    return result


def operate(vector, wave_field):
    padded = padded_2(vector, (("px", 2), ("py", 3)), 1)
    padded = jnp.pad(padded, ((0, 0), (1, 1), (0, 0), (0, 0)))
    neighbours = padded[:, 2:, 1:-1, 1:-1] + padded[:, :-2, 1:-1, 1:-1]
    neighbours = neighbours + padded[:, 1:-1, 2:, 1:-1] + padded[:, 1:-1, :-2, 1:-1]
    neighbours = neighbours + padded[:, 1:-1, 1:-1, 2:] + padded[:, 1:-1, 1:-1, :-2]
    return (6.0 - wave_field) * vector - neighbours


def inner_sums(left, right):
    real_sum = jnp.sum(left[0] * right[0] + left[1] * right[1])
    imag_sum = jnp.sum(left[0] * right[1] - left[1] * right[0])
    return (real_sum, imag_sum)


def scaled_by(factor, vector):
    real_part = factor[0] * vector[0] - factor[1] * vector[1]
    imag_part = factor[0] * vector[1] + factor[1] * vector[0]
    return jnp.stack([real_part, imag_part])


def on_device(source, speed):
    wave_field = wave_square / (speed * speed)
    source_size = jnp.sqrt(of_everyone(jnp.sum(source * source), ("px", "py")) + epsilon)
    basis_one = source / source_size
    solved_one = precondition(basis_one)
    applied = operate(solved_one, wave_field)
    sum_re, sum_im = inner_sums(basis_one, applied)
    one_re, one_im, squares = in_one((sum_re, sum_im, jnp.sum(applied * applied)), ("px", "py"))
    two_one = jnp.sqrt(squares - one_re * one_re - one_im * one_im + epsilon)
    denominator = one_re * one_re + one_im * one_im + two_one * two_one
    weight = (source_size * one_re / denominator, -source_size * one_im / denominator)
    return scaled_by(weight, solved_one)


def solution(mesh):
    return jax.shard_map(
        on_device,
        mesh=mesh,
        in_specs=(P(None, "samples", "px", "py"), P("samples", "px", "py")),
        out_specs=P(None, "samples", "px", "py"),
        check_vma=False,
    )
```

profile of v0, /device:TPU:86, one launch (start us, length us, event | category | flops | bytes accessed | tf_op | source)
XLA Modules:
  0.0 616.6 jit_solution(10464155338639954215)
XLA Ops:
  0.0 3.9 multiply_reduce_fusion.1
  3.9 1.3 broadcast_in_dim.4
  5.1 17.8 %all-to-all-start = ((f32[32,1,1]{2,1,0:T(1,128)}), f32[32,1,1]{2,1,0:T(1,128)S(1)}, u32[]{:S(2)}, u32[]{:S(2)}) async-start(f32[32,1,1]{2,1,0:T(1,128)} %broadcast_in_dim.4), calls=%async_computation | async-start | bytes 32768 | tf_op jit(solution)/shard_map/all_to_all | solution.py:39
  22.9 5.2 copy.69
  28.2 6.5 %all-to-all-done = f32[32,1,1]{2,1,0:T(1,128)S(1)} async-done(((f32[32,1,1]{2,1,0:T(1,128)}), f32[32,1,1]{2,1,0:T(1,128)S(1)}, u32[]{:S(2)}, u32[]{:S(2)}) %all-to-all-start) | async-done | bytes 160 | tf_op jit(solution)/shard_map/all_to_all | solution.py:39
  34.7 0.6 reduce_sum.55
  36.0 2.6 broadcast_divide_fusion
  38.6 0.0 copy-start.2
  38.6 1.9 copy-done.2
  40.5 6.8 %convolution_bitcast_fusion.2 = f32[2,256,16,128]{1,3,2,0:T(8,128)} fusion(f32[2,256,16,128]{1,3,2,0:T(8,128)S(1)} %broadcast_divide_fusion, f32[256]{0:T(256)S(1)} %get-tuple-element.20, f32[256]{0:T(256)S(1)} %get-tuple-element.21), kind=kOutput, calls=%fused_computation.35 | convolution fusion | flops 3221422080 | bytes 8390656 | tf_op jit(solution)/shard_map/ak,ckyz->cayz/dot_general | solution.py:81
  47.4 5.4 copy.71
  52.8 5.1 all-to-all-start.1
  57.9 0.1 multiply_multiply_fusion.2
  58.1 0.1 broadcast_add_fusion
  58.2 182.2 %all-to-all-done.1 = f32[2,256,16,128]{3,2,0,1:T(8,128)} async-done(((f32[2,256,16,128]{3,2,0,1:T(8,128)}), f32[2,256,16,128]{3,2,0,1:T(8,128)}, u32[]{:S(2)}, u32[]{:S(2)}) %all-to-all-start.1) | async-done | bytes 4194336 | tf_op jit(solution)/shard_map/all_to_all | solution.py:98
  240.3 2.7 copy.73
  243.1 9.8 %convolution_bitcast_fusion.1 = f32[2,16,256,128]{2,3,1,0:T(8,128)} fusion(f32[2,16,256,128]{3,2,1,0:T(8,128)S(1)} %bitcast.52, f32[256]{0:T(256)S(1)} %get-tuple-element.20, f32[256]{0:T(256)S(1)} %get-tuple-element.21), kind=kOutput, calls=%fused_computation.34 | convolution fusion | flops 3221422080 | bytes 8390656 | tf_op jit(solution)/shard_map/ak,cxkz->cxaz/dot_general | solution.py:85
  252.9 5.5 copy.75
  258.4 9.0 %all_to_all.84 = f32[2,16,256,128]{3,1,0,2:T(8,128)S(1)} all-to-all(f32[2,16,256,128]{3,1,0,2:T(8,128)} %copy.75), channel_id=1, replica_groups=mesh['samples'=4,'px'=16,'py'=2] {'py'}, dimensions={2} | all-to-all | bytes 8388608 | tf_op jit(solution)/shard_map/all_to_all | solution.py:101
  267.4 5.2 copy.101
  272.6 6.5 %all_to_all.68 = f32[2,16,128,256]{3,2,1,0:T(8,128)} reshape(f32[2,16,128,2,128]{4,3,2,1,0:T(2,128)} %bitcast.54) | data formatting | bytes 8388608 | tf_op jit(solution)/shard_map/all_to_all | solution.py:101
  279.1 7.3 %fusion.19 = f32[2,16,128,256]{3,2,1,0:T(8,128)S(1)} fusion(f32[2,16,128,256]{3,2,1,0:T(8,128)} %all_to_all.68, f32[256]{0:T(256)S(1)} %get-tuple-element.20, f32[256]{0:T(256)S(1)} %get-tuple-element.21), kind=kOutput, calls=%fused_computation.49 | convolution fusion | flops 3221422080 | bytes 8390656 | tf_op jit(solution)/shard_map/ak,cxyk->cxya/dot_general | solution.py:89
  286.4 1.1 fusion.15
  287.4 6.9 %fusion.6 = f32[2,16,128,256]{3,2,1,0:T(8,128)} fusion(f32[1,16,128,256]{3,2,1,0:T(8,128)S(1)} %get-tuple-element.10, f32[1,16,128,256]{3,2,1,0:T(8,128)S(1)} %get-tuple-element.9, f32[256]{0:T(256)S(1)} %get-tuple-element.20, f32[256]{0:T(256)S(1)} %get-tuple-element.21), kind=kOutput, calls=%fused_computation.21 | convolution fusion | flops 3222470656 | bytes 8390656 | tf_op jit(solution)/shard_map/ak,cxyk->cxya/dot_general | solution.py:89
  294.3 5.5 copy.77
  299.8 8.7 %all_to_all.85 = f32[2,16,128,256]{2,1,0,3:T(8,128)S(1)} all-to-all(f32[2,16,128,256]{2,1,0,3:T(8,128)} %copy.77), channel_id=1, replica_groups=mesh['samples'=4,'px'=16,'py'=2] {'py'}, dimensions={3} | all-to-all | bytes 8388608 | tf_op jit(solution)/shard_map/all_to_all | solution.py:107
  308.5 5.2 copy.100
  313.7 6.5 %all_to_all.72 = f32[2,16,256,128]{2,3,1,0:T(8,128)} reshape(f32[2,16,2,128,128]{3,2,4,1,0:T(2,128)} %bitcast.56) | data formatting | bytes 8388608 | tf_op jit(solution)/shard_map/all_to_all | solution.py:107
  320.2 8.6 %convolution_bitcast_fusion = f32[2,16,256,128]{2,3,1,0:T(8,128)} fusion(f32[2,16,256,128]{2,3,1,0:T(8,128)} %all_to_all.72, f32[256]{0:T(256)S(1)} %get-tuple-element.20, f32[256]{0:T(256)S(1)} %get-tuple-element.21), kind=kOutput, calls=%fused_computation.33 | convolution fusion | flops 3221422080 | bytes 8390656 | tf_op jit(solution)/shard_map/ak,cxkz->cxaz/dot_general | solution.py:85
  328.7 5.5 copy.79
  334.2 197.4 %all_to_all.86 = f32[2,16,256,128]{3,1,0,2:T(8,128)S(1)} all-to-all(f32[2,16,256,128]{3,1,0,2:T(8,128)} %copy.79), channel_id=1, replica_groups=mesh['samples'=4,'px'=16,'py'=2] {'px'}, dimensions={2} | all-to-all | bytes 8388608 | tf_op jit(solution)/shard_map/all_to_all | solution.py:110
  531.7 2.4 copy.81
  534.1 0.0 copy-start.4
  534.1 8.6 %fusion.12 = f32[2,256,16,128]{1,3,2,0:T(8,128)S(1)} fusion(f32[2,256,16,128]{3,2,1,0:T(8,128)S(1)} %bitcast.51, f32[256]{0:T(256)S(1)} %get-tuple-element.20, f32[256]{0:T(256)S(1)} %get-tuple-element.21), kind=kOutput, calls=%fused_computation.32 | convolution fusion | flops 3221422080 | bytes 8390656 | tf_op jit(solution)/shard_map/ak,ckyz->cayz/dot_general | solution.py:81
  542.8 0.0 copy-start
  542.8 2.0 copy-done
  544.8 3.6 collective-permute-start.1
  548.4 1.3 collective-permute-start.2
  549.7 1.3 collective-permute-start
  551.1 1.6 collective-permute-start.3
  552.6 0.0 copy-done.4
  552.6 0.3 divide_subtract_fusion
  552.9 1.9 copy.70
  554.9 0.0 collective-permute-done
  554.9 0.0 collective-permute-done.3
  555.0 0.0 copy-start.1
  555.0 0.0 collective-permute-done.1
  555.0 1.8 collective-permute-done.2
  556.7 8.0 %select_maximum_fusion = f32[2,258,18,130]{1,3,2,0:T(8,128)} fusion(f32[2,256,18,1]{1,3,2,0:T(1,128)S(1)} %pad.12, f32[2,256,18,1]{1,3,2,0:T(1,128)S(1)} %pad.11, f32[2,256,1,128]{1,3,2,0:T(8,128)S(1)} %collective-permute-done.2, f32[2,256,16,128]{1,3,2,0:T(8,128)} %copy-done, f32[2,256,1,128]{1,3,2,0:T(8,128)S(1)} %collective-permute-done.1), kind=kLoop, calls=%fused_computation.2 | loop fusion | flops 14489280 | bytes 9622080 | tf_op jit(solution)/shard_map/concatenate | solution.py:32
  564.7 0.0 copy-done.1
  564.7 0.0 copy-start.3
  564.7 10.9 %multiply_reduce_fusion = (f32[]{:T(128)}, f32[2,256,16,128]{1,3,2,0:T(8,128)S(1)}) fusion(f32[2,256,1,128]{1,3,2,0:T(8,128)S(1)} %collective-permute-done.2, f32[2,256,16,128]{1,3,2,0:T(8,128)S(1)} %copy-done.1, f32[2,256,1,128]{1,3,2,0:T(8,128)S(1)} %collective-permute-done.1, f32[2,256,18,1]{1,3,2,0:T(1,128)S(1)} %pad.11, f32[2,256,18,1]{1,3,2,0:T(1,128)S(1)} %pad.12, ...), kind=kLoop, calls=%fused_computation.30 | loop fusion | flops 17825792 | bytes 19472388 | tf_op jit(solution)/shard_map/reduce_sum | solution.py:143
  575.6 0.0 copy-done.3
  575.6 1.8 add_reduce_fusion
  577.4 1.9 pad_maximum_fusion.9
  579.3 0.6 broadcast_in_dim.5
  579.9 8.8 %all-to-all-start.5 = ((f32[32,1,3]{2,1,0:T(1,128)}), f32[32,1,3]{2,1,0:T(1,128)S(1)}, u32[]{:S(2)}, u32[]{:S(2)}) async-start(f32[32,1,3]{2,1,0:T(1,128)} %broadcast_in_dim.5), calls=%async_computation.5 | async-start | bytes 32768 | tf_op jit(solution)/shard_map/all_to_all | solution.py:39
  588.7 11.8 %all-to-all-done.5 = f32[32,1,3]{2,1,0:T(1,128)S(1)} async-done(((f32[32,1,3]{2,1,0:T(1,128)}), f32[32,1,3]{2,1,0:T(1,128)S(1)}, u32[]{:S(2)}, u32[]{:S(2)}) %all-to-all-start.5) | async-done | bytes 416 | tf_op jit(solution)/shard_map/all_to_all | solution.py:39
  600.5 0.1 reduce_sum.59
  600.5 0.7 fusion.64
  605.6 2.8 multiply_subtract_fusion
  608.4 2.3 pad_maximum_fusion.8
  610.7 5.4 copy.84
  (7 shorter events, 0.2 us)
Async XLA Ops:
  5.1 29.6 %all-to-all-start = ((f32[32,1,1]{2,1,0:T(1,128)}), f32[32,1,1]{2,1,0:T(1,128)S(1)}, u32[]{:S(2)}, u32[]{:S(2)}) async-start(f32[32,1,1]{2,1,0:T(1,128)} %broadcast_in_dim.4), calls=%async_computation | async-start | bytes 32768 | tf_op jit(solution)/shard_map/all_to_all | solution.py:39
  38.6 1.9 copy-start.2
  52.8 187.5 %all-to-all-start.1 = ((f32[2,256,16,128]{3,2,0,1:T(8,128)}), f32[2,256,16,128]{3,2,0,1:T(8,128)}, u32[]{:S(2)}, u32[]{:S(2)}) async-start(f32[2,256,16,128]{3,2,0,1:T(8,128)} %copy.71), calls=%async_computation.1 | async-start | bytes 8388608 | tf_op jit(solution)/shard_map/all_to_all | solution.py:98
  534.1 18.5 %copy-start.4 = (f32[256,16,128]{2,1,0:T(8,128)S(1)}, f32[256,16,128]{2,1,0:T(8,128)}, u32[]{:S(2)}) copy-start(f32[256,16,128]{2,1,0:T(8,128)} %param.3) | copy-start | bytes 6291460
  542.8 2.0 copy-start
  544.8 10.1 %collective-permute-start.1 = (f32[2,256,1,128]{1,3,2,0:T(8,128)S(1)}, f32[2,256,1,128]{1,3,2,0:T(8,128)S(1)}, u32[]{:S(2)}, u32[]{:S(2)}) collective-permute-start(f32[2,256,1,128]{1,3,2,0:T(8,128)S(1)} %get-tuple-element.15), channel_id=1, source_target_pairs={{0,2},{2,4},{4,6},{6,8},{8,10},{10,12},{12,14},{14,16},{16,18},{18... | collective-permute-start | bytes 786440 | tf_op jit(solution)/shard_map/ppermute | solution.py:25
  548.4 8.3 %collective-permute-start.2 = (f32[2,256,1,128]{1,3,2,0:T(8,128)S(1)}, f32[2,256,1,128]{1,3,2,0:T(8,128)S(1)}, u32[]{:S(2)}, u32[]{:S(2)}) collective-permute-start(f32[2,256,1,128]{1,3,2,0:T(8,128)S(1)} %get-tuple-element.16), channel_id=1, source_target_pairs={{2,0},{4,2},{6,4},{8,6},{10,8},{12,10},{14,12},{16,14},{18,16},{20... | collective-permute-start | bytes 786440 | tf_op jit(solution)/shard_map/ppermute | solution.py:26
  549.7 5.1 collective-permute-start
  551.1 3.8 collective-permute-start.3
  555.0 9.8 %copy-start.1 = (f32[2,256,16,128]{1,3,2,0:T(8,128)S(1)}, f32[2,256,16,128]{1,3,2,0:T(8,128)}, u32[]{:S(2)}) copy-start(f32[2,256,16,128]{1,3,2,0:T(8,128)} %copy-done) | copy-start | bytes 12582916
  564.7 10.9 %copy-start.3 = (f32[2,256,16,128]{1,3,2,0:T(8,128)S(1)}, f32[2,256,16,128]{1,3,2,0:T(8,128)}, u32[]{:S(2)}) copy-start(f32[2,256,16,128]{1,3,2,0:T(8,128)} %copy-done.2) | copy-start | bytes 12582916
  579.9 20.6 %all-to-all-start.5 = ((f32[32,1,3]{2,1,0:T(1,128)}), f32[32,1,3]{2,1,0:T(1,128)S(1)}, u32[]{:S(2)}, u32[]{:S(2)}) async-start(f32[32,1,3]{2,1,0:T(1,128)} %broadcast_in_dim.5), calls=%async_computation.5 | async-start | bytes 32768 | tf_op jit(solution)/shard_map/all_to_all | solution.py:39
where the time goes:
time: 626 us; the launch traced here: 617 us
  blocking collectives  215 us (34%)
  waiting for transfers between devices  202 us (32%)
  local copies, waits for them, and re-layouts  69.6 us (11%)
  matrix products  48 us (8%)
  starting transfers between devices  39.5 us (6%)
  other arithmetic  36.4 us (6%)
    all_to_all x1, blocking collectives, precondition(): lax.all_to_all(swapped, 'px', split_axis=2, concat_axis=1, tiled=True)  197 us
    all_to_all x1, waiting for transfers between devices, precondition(): lax.all_to_all(section_x, 'px', split_axis=1, concat_axis=2, tiled=True)  182 us
    all_to_all x2, starting transfers between devices, copy_for_each(): lax.all_to_all(jnp.broadcast_to(shard[None], (size, *shard.shape)), axis,...  26.6 us
    dot_general x2, matrix products, apply_y(): return jnp.einsum('ak,cxkz->cxaz', matrix, values, precision=highest)  18.4 us
    all_to_all x2, waiting for transfers between devices, copy_for_each(): lax.all_to_all(jnp.broadcast_to(shard[None], (size, *shard.shape)), axis,...  18.3 us
    dot_general x2, matrix products, apply_x(): return jnp.einsum('ak,ckyz->cayz', matrix, values, precision=highest)  15.5 us
    dot_general x2, matrix products, apply_z(): return jnp.einsum('ak,cxyk->cxya', matrix, values, precision=highest)  14.1 us
  transfers between devices with their start and end apart: 7, of which 4 were waited for; matrix products, arithmetic and copies ran while one was open for 1% of the time, Pallas kernels for 0%

commit v1 on v0

v1 whole, which is shorter than its diff:
```python
import functools
import numpy as np
import jax
import jax.numpy as jnp
from jax import lax
from jax.experimental import pallas as pl
from jax.experimental.pallas import tpu as pltpu
from jax.sharding import PartitionSpec as P

wave_square = 0.25
damping = 0.5
epsilon = 1e-06
f32 = jnp.float32
bf16 = jnp.bfloat16
YB = 8
KB = 32


def sine_table(length):
    k = np.arange(1, length + 1, dtype=np.float64)
    phases = np.mod(np.outer(k, k), 2 * (length + 1)) * (np.pi / (length + 1))
    return np.sqrt(2.0 / (length + 1)) * np.sin(phases)


def halves_of(table):
    table = table.astype(np.float32)
    high = table.astype(bf16)
    low = (table - high.astype(np.float32)).astype(bf16)
    return high, low


def eigen_line(length):
    k = np.arange(1, length + 1, dtype=np.float64)
    return 4.0 * np.sin(np.pi * k / (2.0 * (length + 1))) ** 2


def root_tables(nx, nz):
    near = eigen_line(nx)[:, None] + eigen_line(nz)[None, :] - wave_square + 1j * damping * wave_square
    spread = np.sqrt(near) * np.sqrt(near + 4.0)
    lam = 2.0 / (near + 2.0 + spread)
    gam = 1.0 / spread
    return np.stack([lam.real, lam.imag, gam.real, gam.imag]).astype(np.float32)


def cmul(a, b):
    return a[0] * b[0] - a[1] * b[1], a[0] * b[1] + a[1] * b[0]


def cadd(a, b):
    return a[0] + b[0], a[1] + b[1]


def split(v):
    high = v.astype(bf16)
    return high, (v - high.astype(f32)).astype(bf16)


def dot(a, b):
    return lax.dot_general(a, b, (((1,), (0,)), ((), ())), preferred_element_type=f32)


def forward_x(s_ref, src, send, keep):
    me = lax.axis_index("py")
    nx = src.shape[1]
    flat = src.at[0].reshape(nx * YB, src.shape[3])
    cols = []
    for y in range(YB):
        high, low = split(flat[pl.ds(y, nx, stride=YB), :])
        cols.append(jnp.concatenate([high, low, high], axis=0))
    right = jnp.concatenate(cols, axis=1)
    for half, out in ((1 - me, send), (me, keep)):
        got = dot(s_ref[half], right)
        w = src.shape[3]
        for y in range(YB):
            out[0, y] = got[:, y * w : (y + 1) * w]


def forward_z(s_ref, root, keep, recv, f_out, pq):
    me = lax.axis_index("py")
    _, ny, kb, w = keep.shape
    total = None
    for half, ref in ((me, keep), (1 - me, recv)):
        high, low = split(ref[...].reshape(2 * ny * kb, w))
        part = dot(jnp.concatenate([high, low, high], axis=1), s_ref[half])
        total = part if total is None else total + part
    f_out[...] = total.reshape(f_out.shape)
    nk = root.shape[1] // 2
    rows = pl.ds(pl.multiple_of(me * nk + pl.program_id(0) * kb, kb), kb)
    lam = root[0, rows, :], root[1, rows, :]
    p = f_out[0, 0], f_out[1, 0]
    q = f_out[0, ny - 1], f_out[1, ny - 1]
    for j in range(1, ny):
        p = cadd(cmul(lam, p), (f_out[0, j], f_out[1, j]))
        q = cadd(cmul(lam, q), (f_out[0, ny - 1 - j], f_out[1, ny - 1 - j]))
    for i, part in enumerate((*p, *q)):
        pq[:, i] = part.reshape(pq.shape[0], pq.shape[2], pq.shape[3])


def local_solve(root, f_ref, w_out):
    me = lax.axis_index("py")
    _, ny, kb, _ = f_ref.shape
    nk = root.shape[1] // 2
    rows = pl.ds(pl.multiple_of(me * nk + pl.program_id(0) * kb, kb), kb)
    lam = root[0, rows, :], root[1, rows, :]
    gam = root[2, rows, :], root[3, rows, :]
    p = None
    for j in range(ny):
        f = f_ref[0, j], f_ref[1, j]
        p = f if p is None else cadd(cmul(lam, p), f)
        w_out[0, j], w_out[1, j] = p
    q = None
    for j in reversed(range(ny)):
        lq = None if q is None else cmul(lam, q)
        here = w_out[0, j], w_out[1, j]
        if lq is not None:
            here = cadd(here, lq)
            q = cadd(lq, (f_ref[0, j], f_ref[1, j]))
        else:
            q = f_ref[0, j], f_ref[1, j]
        w_out[0, j], w_out[1, j] = cmul(gam, here)


def carries(root, pq, fb):
    n, _, rows, _ = pq.shape
    first = (lax.axis_index("py") * n + lax.axis_index("px")) * rows
    own = pl.ds(pl.multiple_of(first, rows), rows)
    lam = root[0, own, :], root[1, own, :]
    gam = root[2, own, :], root[3, own, :]

    def power(base, exponent):
        result = None
        while exponent:
            if exponent & 1:
                result = base if result is None else cmul(result, base)
            exponent >>= 1
            if exponent:
                base = cmul(base, base)
        return result

    return lam, gam, power


def reduced_solve(ny, root, pq, fb):
    n = pq.shape[0]
    lam, gam, power = carries(root, pq, fb)
    block = power(lam, ny)
    whole = power(block, n)
    last_f = pq[0, 0], pq[0, 1]
    last_b = pq[n - 1, 2], pq[n - 1, 3]
    for i in range(1, n):
        last_f = cadd(cmul(block, last_f), (pq[i, 0], pq[i, 1]))
        last_b = cadd(cmul(block, last_b), (pq[n - 1 - i, 2], pq[n - 1 - i, 3]))
    around = cmul(whole, cmul(lam, lam))
    both = cmul(around, whole)
    det = 1.0 - both[0], -both[1]
    size = det[0] * det[0] + det[1] * det[1]
    inverse = det[0] / size, -det[1] / size
    minus = -lam[0], -lam[1]
    f = cmul(inverse, cadd(cmul(minus, last_b), cmul(around, last_f)))
    b = cmul(inverse, cadd(cmul(minus, last_f), cmul(around, last_b)))
    for i in range(n):
        fb[i, 0], fb[i, 1] = cmul(gam, f)
        k = n - 1 - i
        fb[k, 2], fb[k, 3] = cmul(gam, b)
        if i < n - 1:
            f = cadd(cmul(block, f), (pq[i, 0], pq[i, 1]))
            b = cadd(cmul(block, b), (pq[k, 2], pq[k, 3]))


def inverse_z(s_ref, root, w_ref, fb, send, keep, u):
    me = lax.axis_index("py")
    _, ny, kb, nz = w_ref.shape
    nk = root.shape[1] // 2
    rows = pl.ds(pl.multiple_of(me * nk + pl.program_id(0) * kb, kb), kb)
    lam = root[0, rows, :], root[1, rows, :]
    f = fb[:, 0].reshape(kb, nz), fb[:, 1].reshape(kb, nz)
    b = fb[:, 2].reshape(kb, nz), fb[:, 3].reshape(kb, nz)
    for j in range(ny):
        f = cmul(lam, f)
        u[0, j], u[1, j] = cadd((w_ref[0, j], w_ref[1, j]), f)
    for j in reversed(range(ny)):
        b = cmul(lam, b)
        u[0, j], u[1, j] = cadd((u[0, j], u[1, j]), b)
    high, low = split(u[...].reshape(2 * ny * kb, nz))
    left = jnp.concatenate([high, low, high], axis=1)
    got = dot(left, jnp.concatenate([s_ref[1 - me], s_ref[me]], axis=1))
    w = send.shape[3]
    send[...] = got[:, :w].reshape(send.shape)
    keep[...] = got[:, w:].reshape(keep.shape)


def inverse_x(s_ref, keep, recv, src, speed, out, sums):
    me = lax.axis_index("py")
    _, nx, _, w = out.shape
    left = jnp.concatenate([s_ref[me], s_ref[1 - me]], axis=1)
    for c in range(2):
        cols = []
        for y in range(YB):
            parts = []
            for ref in (keep, recv):
                high, low = split(ref[c, y])
                parts += [high, low, high]
            cols.append(jnp.concatenate(parts, axis=0))
        got = dot(left, jnp.concatenate(cols, axis=1))
        flat = out.at[c].reshape(nx * YB, w)
        for y in range(YB):
            flat[pl.ds(y, nx, stride=YB), :] = got[:, y * w : (y + 1) * w]

    @pl.when(pl.program_id(0) == 0)
    def _():
        sums[...] = jnp.zeros_like(sums)

    damped = damping * wave_square

    def step(i, acc):
        s0, s1 = src[0, i], src[1, i]
        p0, p1 = out[0, i], out[1, i]
        c = speed[i]
        factor = wave_square - wave_square / (c * c)
        a0 = s0 + factor * p0 + damped * p1
        a1 = s1 + factor * p1 - damped * p0
        new = (
            s0 * s0 + s1 * s1,
            s0 * a0 + s1 * a1,
            s0 * a1 - s1 * a0,
            a0 * a0 + a1 * a1,
        )
        return tuple(x + y for x, y in zip(acc, new))

    zero = jnp.zeros((YB, w), f32)
    acc = lax.fori_loop(0, nx, step, (zero,) * 4, unroll=8)
    for i, a in enumerate(acc):
        sums[i : i + 1, :] += jnp.sum(a, axis=0, keepdims=True)


def finish(total, ps, out):
    sums = jnp.sum(jnp.sum(total[...], axis=0), axis=1, keepdims=True)
    square, re, im, size = (sums[i : i + 1] for i in range(4))
    beta2 = square + epsilon
    re, im, size = re / beta2, im / beta2, size / beta2
    den = size - (re * re + im * im) * (epsilon / beta2) + epsilon
    a, b = re / den, -im / den
    shape = ps.shape[1:]
    a = jnp.broadcast_to(a[:, :, None], shape)
    b = jnp.broadcast_to(b[:, :, None], shape)
    out[0] = a * ps[0] - b * ps[1]
    out[1] = a * ps[1] + b * ps[0]


def params(parallel=1):
    return pltpu.CompilerParams(dimension_semantics=("arbitrary",) * parallel, vmem_limit_bytes=56 * 2**20)


def whole(a):
    return pl.BlockSpec(a.shape, lambda *_: (0,) * a.ndim)


def cost(flops, moved):
    return pl.CostEstimate(flops=flops, bytes_accessed=moved, transcendentals=0)


def on_device(source, speed):
    _, nx, ny, w = source.shape
    cores, ring = lax.axis_size("py"), lax.axis_size("px")
    nz, nk = w * cores, nx // cores
    other = [(i, cores - 1 - i) for i in range(cores)]
    sds = lambda *shape: jax.ShapeDtypeStruct(shape, f32)

    hx, lx = halves_of(sine_table(nx))
    hz, lz = halves_of(sine_table(nz))
    sx_in = jnp.asarray(np.concatenate([hx, hx, lx], 1).reshape(2, nk, 3 * nx))
    sz_in = jnp.asarray(np.stack([np.concatenate([hz[h * w : (h + 1) * w]] * 2 + [lz[h * w : (h + 1) * w]], 0) for h in (0, 1)]))
    sz_out = jnp.asarray(np.stack([np.concatenate([hz, hz, lz], 0)[:, h * w : (h + 1) * w] for h in (0, 1)]))
    sx_out = jnp.asarray(np.stack([np.concatenate([t[:, h * nk : (h + 1) * nk] for t in (hx, hx, lx)], 1) for h in (0, 1)]))
    root = jnp.asarray(root_tables(nx, nz))
    part = sds(2, ny, nk, w)
    flops = 2 * 2 * nx * ny * w * nx * 3

    spec = pl.BlockSpec((1, YB, nk, w), lambda c, y: (c, y, 0, 0))
    send, keep = pl.pallas_call(
        forward_x,
        grid=(2, ny // YB),
        in_specs=[whole(sx_in), pl.BlockSpec((1, nx, YB, w), lambda c, y: (c, 0, y, 0))],
        out_specs=[spec, spec],
        out_shape=[part, part],
        compiler_params=params(2),
        cost_estimate=cost(flops, 8 * 2**20),
        name="forward_x",
    )(sx_in, source)
    recv = lax.ppermute(send, "py", other)

    kspec = lambda width: pl.BlockSpec((2, ny, KB, width), lambda k: (0, 0, k, 0))
    rows = nk // ring
    pspec = pl.BlockSpec((KB // rows, 4, rows, nz), lambda k: (k, 0, 0, 0))
    f, pq = pl.pallas_call(
        forward_z,
        grid=(nk // KB,),
        in_specs=[whole(sz_in), whole(root), kspec(w), kspec(w)],
        out_specs=[kspec(nz), pspec],
        out_shape=[sds(2, ny, nk, nz), sds(ring, 4, rows, nz)],
        compiler_params=params(),
        cost_estimate=cost(flops, 8 * 2**20),
        name="forward_z",
    )(sz_in, root, keep, recv)
    pq = lax.all_to_all(pq, "px", 0, 0, tiled=True)
    local = pl.pallas_call(
        local_solve,
        grid=(nk // KB,),
        in_specs=[whole(root), kspec(nz)],
        out_specs=kspec(nz),
        out_shape=sds(2, ny, nk, nz),
        compiler_params=params(),
        cost_estimate=cost(flops, 8 * 2**20),
        name="local_solve",
    )(root, f)
    fb = pl.pallas_call(
        functools.partial(reduced_solve, ny),
        out_shape=sds(ring, 4, rows, nz),
        compiler_params=pltpu.CompilerParams(vmem_limit_bytes=16 * 2**20),
        cost_estimate=cost(10**7, 2**20),
        name="reduced_solve",
    )(root, pq)
    fb = lax.all_to_all(fb, "px", 0, 0, tiled=True)
    send, keep = pl.pallas_call(
        inverse_z,
        grid=(nk // KB,),
        in_specs=[whole(sz_out), whole(root), kspec(nz), pspec],
        out_specs=[kspec(w), kspec(w)],
        out_shape=[part, part],
        scratch_shapes=[pltpu.VMEM((2, ny, KB, nz), f32)],
        compiler_params=params(),
        cost_estimate=cost(flops, 8 * 2**20),
        name="inverse_z",
    )(sz_out, root, local, fb)
    recv = lax.ppermute(send, "py", other)
    yspec = pl.BlockSpec((2, YB, nk, w), lambda y: (0, y, 0, 0))
    block = pl.BlockSpec((2, nx, YB, w), lambda y: (0, 0, y, 0))
    solved, sums = pl.pallas_call(
        inverse_x,
        grid=(ny // YB,),
        in_specs=[whole(sx_out), yspec, yspec, block, pl.BlockSpec((nx, YB, w), lambda y: (0, y, 0))],
        out_specs=[block, pl.BlockSpec((4, w), lambda y: (0, 0))],
        out_shape=[sds(*source.shape), sds(4, w)],
        compiler_params=params(),
        cost_estimate=cost(flops, 16 * 2**20),
        name="inverse_x",
    )(sx_out, keep, recv, source, speed)
    sums = sums + lax.ppermute(sums, "py", other)
    every = lax.all_to_all(jnp.broadcast_to(sums[None], (ring, 4, w)), "px", 0, 0, tiled=True)
    xb = nx // 8
    xspec = pl.BlockSpec((2, xb, ny, w), lambda x: (0, x, 0, 0))
    return pl.pallas_call(
        finish,
        grid=(nx // xb,),
        in_specs=[whole(every), xspec],
        out_specs=xspec,
        out_shape=sds(*source.shape),
        compiler_params=params(),
        cost_estimate=cost(10**7, 8 * 2**20),
        name="finish",
    )(every, solved)


def solution(mesh):
    return jax.shard_map(
        on_device,
        mesh=mesh,
        in_specs=(P(None, "samples", "px", "py"), P("samples", "px", "py")),
        out_specs=P(None, "samples", "px", "py"),
        check_vma=False,
    )
```

time: 626 us -> 152 us (0.24); the launches traced: 617 us -> 152 us
  waiting for transfers between devices: 202 us -> 32.9 us
  blocking collectives: 215 us -> 64.9 us
  local copies, waits for them, and re-layouts: 69.6 us -> 3.45 us
  matrix products: 48 us -> 0 us
  Pallas kernels: 0 us -> 42.8 us
  other arithmetic: 36.4 us -> 0.67 us
  starting transfers between devices: 39.5 us -> 6.82 us
    all_to_all x3 -> x1, waiting for transfers between devices: 201 us -> 22.9 us  [on_device(): fb = lax.all_to_all(fb, 'px', 0, 0, tiled=True)]
    all_to_all x3 -> x2, blocking collectives: 215 us -> 64.9 us  [the longest x1 46 us: on_device(): pq = lax.all_to_all(pq, 'px', 0, 0, tiled=True)]
    dot_general x6 -> x0, matrix products: 48 us -> none  [the longest x2 18.4 us: apply_y(): return jnp.einsum('ak,cxkz->cxaz', matrix, values, precision=highest)]
    pallas_call x0 -> x7, Pallas kernels: none -> 42.8 us  [the longest x1 8.53 us: on_device(): pl.pallas_call(inverse_x, grid=(ny // YB,), in_specs=[whole(sx_out), yspe...]
    all_to_all x6 -> x0, local copies, waits for them, and re-layouts: 28.6 us -> none  [the longest x2 11.7 us: precondition(): lax.all_to_all(scaled, 'py', split_axis=3, concat_axis=2, tiled=True)]
    all_to_all x3 -> x1, starting transfers between devices: 31.7 us -> 6.69 us  [on_device(): fb = lax.all_to_all(fb, 'px', 0, 0, tiled=True)]
    reduce_sum x5 -> x0, other arithmetic: 17.2 us -> none  [the longest x1 10.9 us: on_device(): jnp.sum(applied * applied)]
    transpose x3 -> x0, local copies, waits for them, and re-layouts: 16.4 us -> none  [the longest x2 11 us: apply_y(): return jnp.einsum('ak,cxkz->cxaz', matrix, values, precision=highest)]
  transfers between devices with their start and end apart: 7 -> 4, of which waited for: 4 -> 4; matrix products, arithmetic and copies ran while one was open for 1% -> 0% of each run, Pallas kernels for 0% -> 4%
where the time goes in v1:
time: 152 us
  blocking collectives  64.9 us (43%)
  Pallas kernels  42.8 us (28%)
  waiting for transfers between devices  32.9 us (22%)
  starting transfers between devices  6.82 us (4%)
  local copies, waits for them, and re-layouts  3.45 us (2%)
    all_to_all x1, blocking collectives, on_device(): pq = lax.all_to_all(pq, 'px', 0, 0, tiled=True)  46 us
    all_to_all x1, waiting for transfers between devices, on_device(): fb = lax.all_to_all(fb, 'px', 0, 0, tiled=True)  22.9 us
    all_to_all x1, blocking collectives, on_device(): lax.all_to_all(jnp.broadcast_to(sums[None], (ring, 4, w)), 'px', 0, 0, ti...  18.9 us
    ppermute x2, waiting for transfers between devices, on_device(): recv = lax.ppermute(send, 'py', other)  8.73 us
    pallas_call x1, Pallas kernels, on_device(): pl.pallas_call(inverse_x, grid=(ny // YB,), in_specs=[whole(sx_out), yspe...  8.53 us
    pallas_call x1, Pallas kernels, on_device(): pl.pallas_call(finish, grid=(nx // xb,), in_specs=[whole(every), xspec],...  7.44 us
    pallas_call x1, Pallas kernels, on_device(): pl.pallas_call(forward_z, grid=(nk // KB,), in_specs=[whole(sz_in), whole...  7.43 us
    all_to_all x1, starting transfers between devices, on_device(): fb = lax.all_to_all(fb, 'px', 0, 0, tiled=True)  6.69 us
  transfers between devices with their start and end apart: 4, of which 4 were waited for; matrix products, arithmetic and copies ran while one was open for 0% of the time, Pallas kernels for 4%

profile of v1, /device:TPU:86, one launch (start us, length us, event | category | flops | bytes accessed | tf_op | source)
XLA Modules:
  0.0 151.6 jit_solution(15413133140173288367)
XLA Ops:
  0.0 5.7 %forward_x.1 = (f32[2,16,128,128]{3,2,1,0:T(8,128)}, f32[2,16,128,128]{3,2,1,0:T(8,128)}) custom-call(bf16[2,128,768]{2,1,0:T(8,128)(2,1)} %constant.10.clone.s_ref, f32[2,256,16,128]{3,2,1,0:T(8,128)} %src.3), custom_call_target="tpu_custom_call" | custom-call | flops 1610612736 | bytes 8388608 | tf_op jit(solution)/shard_map/forward_x/pallas_call | solution.py:280
  5.7 0.0 collective-permute-start
  5.7 4.4 %collective-permute-done.recv = f32[2,16,128,128]{3,2,1,0:T(8,128)S(1)} collective-permute-done((f32[2,16,128,128]{3,2,1,0:T(8,128)}, f32[2,16,128,128]{3,2,1,0:T(8,128)S(1)}, u32[]{:S(2)}, u32[]{:S(2)}) %collective-permute-start) | collective-permute-done | bytes 2097184 | tf_op jit(solution)/shard_map/ppermute | solution.py:290
  10.1 0.0 copy-start.3
  10.1 1.3 copy-done.3
  11.4 0.0 copy-start
  11.4 7.4 %forward_z.1 = (f32[2,16,128,256]{3,2,1,0:T(8,128)}, f32[16,4,8,256]{3,2,1,0:T(8,128)}) custom-call(bf16[2,384,256]{2,1,0:T(8,128)(2,1)} %constant.11.clone.s_ref, f32[4,256,256]{2,1,0:T(8,128)} %constant.14.clone.root, f32[2,16,128,128]{3,2,1,0:T(8,128)} %get-tuple-element.13.keep, f32[2,16,128,128]{3,2,1,0:T(8,128)} %copy-done.3), custom_call_target="tpu_custom_call" | custom-call | flops 1610612736 | bytes 8388608 | tf_op jit(solution)/shard_map/forward_z/pallas_call | solution.py:295
  18.9 46.0 %all_to_all.15.pq = f32[16,4,8,256]{3,2,1,0:T(8,128)S(1)} all-to-all(f32[16,4,8,256]{3,2,1,0:T(8,128)} %get-tuple-element.16), channel_id=1, replica_groups=mesh['samples'=4,'px'=16,'py'=2] {'px'}, dimensions={0} | all-to-all | bytes 1048576 | tf_op jit(solution)/shard_map/all_to_all | solution.py:305
  64.9 0.0 copy-done
  64.9 1.0 reduced_solve.1
  65.9 6.7 %all-to-all-start.1 = ((f32[16,4,8,256]{3,2,1,0:T(8,128)}), f32[16,4,8,256]{3,2,1,0:T(8,128)S(1)}, u32[]{:S(2)}, u32[]{:S(2)}) async-start(f32[16,4,8,256]{3,2,1,0:T(8,128)} %reduced_solve.1), calls=%async_computation.1 | async-start | bytes 1048576 | tf_op jit(solution)/shard_map/all_to_all | solution.py:323
  72.6 6.0 %local_solve.1.w_ref = f32[2,16,128,256]{3,2,1,0:T(8,128)} custom-call(f32[4,256,256]{2,1,0:T(8,128)} %constant.14.clone.root, f32[2,16,128,256]{3,2,1,0:T(8,128)} %get-tuple-element.15.f_ref), custom_call_target="tpu_custom_call" | custom-call | flops 1610612736 | bytes 8388608 | tf_op jit(solution)/shard_map/local_solve/pallas_call | solution.py:306
  78.6 22.9 %all-to-all-done.1.fb = f32[16,4,8,256]{3,2,1,0:T(8,128)S(1)} async-done(((f32[16,4,8,256]{3,2,1,0:T(8,128)}), f32[16,4,8,256]{3,2,1,0:T(8,128)S(1)}, u32[]{:S(2)}, u32[]{:S(2)}) %all-to-all-start.1) | async-done | bytes 524320 | tf_op jit(solution)/shard_map/all_to_all | solution.py:323
  101.5 0.0 copy-start.1
  101.5 0.8 copy-done.1
  102.3 6.7 %inverse_z.1 = (f32[2,16,128,128]{3,2,1,0:T(8,128)}, f32[2,16,128,128]{3,2,1,0:T(8,128)}) custom-call(bf16[2,768,128]{2,1,0:T(8,128)(2,1)} %constant.12.clone.s_ref, f32[4,256,256]{2,1,0:T(8,128)} %constant.14.clone.root, f32[2,16,128,256]{3,2,1,0:T(8,128)} %local_solve.1.w_ref, f32[16,4,8,256]{3,2,1,0:T(8,128)} %copy-done.1), custom_call_target="tpu_custom_call" | custom-call | flops 1610612736 | bytes 8388608 | tf_op jit(solution)/shard_map/inverse_z/pallas_call | solution.py:324
  109.0 0.0 collective-permute-start.1
  109.0 4.4 %collective-permute-done.1.recv = f32[2,16,128,128]{3,2,1,0:T(8,128)S(1)} collective-permute-done((f32[2,16,128,128]{3,2,1,0:T(8,128)}, f32[2,16,128,128]{3,2,1,0:T(8,128)S(1)}, u32[]{:S(2)}, u32[]{:S(2)}) %collective-permute-start.1) | collective-permute-done | bytes 2097184 | tf_op jit(solution)/shard_map/ppermute | solution.py:335
  113.4 0.0 copy-start.2
  113.4 1.3 copy-done.2
  114.7 8.5 %inverse_x.1 = (f32[2,256,16,128]{3,2,1,0:T(8,128)}, f32[4,128]{1,0:T(4,128)}) custom-call(bf16[2,256,384]{2,1,0:T(8,128)(2,1)} %constant.13.clone.s_ref, f32[2,16,128,128]{3,2,1,0:T(8,128)} %get-tuple-element.17.keep, f32[2,16,128,128]{3,2,1,0:T(8,128)} %copy-done.2, f32[2,256,16,128]{3,2,1,0:T(8,128)} %src.3, f32[256,16,128]{2,1,0:T(8,128)} %speed.1), custom_call_target="tpu_custom_call" | custom-call | flops 1610612736 | bytes 16777216 | tf_op jit(solution)/shard_map/inverse_x/pallas_call | solution.py:338
  123.2 0.1 collective-permute-start.2
  123.3 1.2 collective-permute-done.2
  124.6 0.7 add.3
  125.3 18.9 %all_to_all.16.total = f32[16,4,128]{2,1,0:T(4,128)} all-to-all(f32[16,4,128]{2,1,0:T(4,128)S(1)} %broadcast_in_dim.2), channel_id=1, replica_groups=mesh['samples'=4,'px'=16,'py'=2] {'px'}, dimensions={0} | all-to-all | bytes 65536 | tf_op jit(solution)/shard_map/all_to_all | solution.py:349
  144.2 7.4 %finish.1 = f32[2,256,16,128]{3,2,1,0:T(8,128)} custom-call(f32[16,4,128]{2,1,0:T(4,128)} %all_to_all.16.total, f32[2,256,16,128]{3,2,1,0:T(8,128)} %get-tuple-element.20.ps), custom_call_target="tpu_custom_call" | custom-call | flops 10000000 | bytes 8388608 | tf_op jit(solution)/shard_map/finish/pallas_call | solution.py:352
  (1 shorter events, 0.0 us)
Async XLA Ops:
  5.7 4.4 %collective-permute-start = (f32[2,16,128,128]{3,2,1,0:T(8,128)}, f32[2,16,128,128]{3,2,1,0:T(8,128)S(1)}, u32[]{:S(2)}, u32[]{:S(2)}) collective-permute-start(f32[2,16,128,128]{3,2,1,0:T(8,128)} %get-tuple-element.14), channel_id=1, source_target_pairs={{0,1},{1,0},{2,3},{3,2},{4,5},{5,4},{6,7},{7,6},{8,9},{9,8},{10,11... | collective-permute-start | bytes 6291464 | tf_op jit(solution)/shard_map/ppermute | solution.py:290
  10.1 1.3 copy-start.3
  11.4 53.5 %copy-start = (f32[4,256,256]{2,1,0:T(8,128)S(1)}, f32[4,256,256]{2,1,0:T(8,128)}, u32[]{:S(2)}) copy-start(f32[4,256,256]{2,1,0:T(8,128)} %constant.14.clone.root) | copy-start | bytes 3145732
  65.9 35.6 %all-to-all-start.1 = ((f32[16,4,8,256]{3,2,1,0:T(8,128)}), f32[16,4,8,256]{3,2,1,0:T(8,128)S(1)}, u32[]{:S(2)}, u32[]{:S(2)}) async-start(f32[16,4,8,256]{3,2,1,0:T(8,128)} %reduced_solve.1), calls=%async_computation.1 | async-start | bytes 1048576 | tf_op jit(solution)/shard_map/all_to_all | solution.py:323
  101.5 0.8 copy-start.1
  109.0 4.4 %collective-permute-start.1 = (f32[2,16,128,128]{3,2,1,0:T(8,128)}, f32[2,16,128,128]{3,2,1,0:T(8,128)S(1)}, u32[]{:S(2)}, u32[]{:S(2)}) collective-permute-start(f32[2,16,128,128]{3,2,1,0:T(8,128)} %get-tuple-element.18), channel_id=1, source_target_pairs={{0,1},{1,0},{2,3},{3,2},{4,5},{5,4},{6,7},{7,6},{8,9},{9,8},{10,11... | collective-permute-start | bytes 6291464 | tf_op jit(solution)/shard_map/ppermute | solution.py:335
  113.4 1.3 copy-start.2
  123.2 1.4 collective-permute-start.2

commit v2 on v1

v2 whole, which is shorter than its diff:
```python
import functools
import numpy as np
import jax
import jax.numpy as jnp
from jax import lax
from jax.experimental import pallas as pl
from jax.experimental.pallas import tpu as pltpu
from jax.sharding import PartitionSpec as P

wave_square = 0.25
damping = 0.5
epsilon = 1e-06
f32 = jnp.float32
bf16 = jnp.bfloat16
YB = 8
KB = 32
XC = 32


def sine_table(length):
    k = np.arange(1, length + 1, dtype=np.float64)
    phases = np.mod(np.outer(k, k), 2 * (length + 1)) * (np.pi / (length + 1))
    return np.sqrt(2.0 / (length + 1)) * np.sin(phases)


def halves_of(table):
    table = table.astype(np.float32)
    high = table.astype(bf16)
    low = (table - high.astype(np.float32)).astype(bf16)
    return high, low


def eigen_line(length):
    k = np.arange(1, length + 1, dtype=np.float64)
    return 4.0 * np.sin(np.pi * k / (2.0 * (length + 1))) ** 2


def root_tables(nx, nz):
    near = eigen_line(nx)[:, None] + eigen_line(nz)[None, :] - wave_square + 1j * damping * wave_square
    spread = np.sqrt(near) * np.sqrt(near + 4.0)
    lam = 2.0 / (near + 2.0 + spread)
    gam = 1.0 / spread
    return np.stack([lam.real, lam.imag, gam.real, gam.imag]).astype(np.float32)


def cmul(a, b):
    return a[0] * b[0] - a[1] * b[1], a[0] * b[1] + a[1] * b[0]


def cadd(a, b):
    return a[0] + b[0], a[1] + b[1]


def split(v):
    high = v.astype(bf16)
    return high, (v - high.astype(f32)).astype(bf16)


def dot(a, b):
    return lax.dot_general(a, b, (((1,), (0,)), ((), ())), preferred_element_type=f32)


def forward_x(s_ref, src, send, keep):
    me = lax.axis_index("py")
    nx = src.shape[1]
    flat = src.at[0].reshape(nx * YB, src.shape[3])
    cols = []
    for y in range(YB):
        high, low = split(flat[pl.ds(y, nx, stride=YB), :])
        cols.append(jnp.concatenate([high, low, high], axis=0))
    right = jnp.concatenate(cols, axis=1)
    for half, out in ((1 - me, send), (me, keep)):
        got = dot(s_ref[half], right)
        w = src.shape[3]
        for y in range(YB):
            out[0, y] = got[:, y * w : (y + 1) * w]


def own_rows(root, block, kb):
    nk = root.shape[1] // 2
    return pl.ds(pl.multiple_of(lax.axis_index("py") * nk + block * kb, kb), kb)


def power(base, exponent):
    result = None
    while exponent:
        if exponent & 1:
            result = base if result is None else cmul(result, base)
        exponent >>= 1
        if exponent:
            base = cmul(base, base)
    return result


def forward_z(first, s_ref, root, *refs):
    if first:
        keep, recv, f_out, pq = refs
    else:
        keep, recv, before, f_out, pq = refs
    me = lax.axis_index("py")
    _, ny, nk, w = keep.shape
    nz = f_out.shape[3]

    def block(i, carry):
        k = pl.ds(pl.multiple_of(i * KB, KB), KB)
        total = None
        for half, ref in ((me, keep), (1 - me, recv)):
            high, low = split(ref[:, :, k, :].reshape(2 * ny * KB, w))
            part = dot(jnp.concatenate([high, low, high], axis=1), s_ref[half])
            total = part if total is None else total + part
        total = total.reshape(2, ny, KB, nz)
        f_out[:, :, k, :] = total
        rows = own_rows(root, i, KB)
        lam = root[0, rows, :], root[1, rows, :]
        row = [(total[0, j], total[1, j]) for j in range(ny)]
        p = row[0] if first else cadd(cmul(lam, (before[0, k, :], before[1, k, :])), row[0])
        q = row[ny - 1]
        for j in range(1, ny):
            p = cadd(cmul(lam, p), row[j])
            q = cadd(cmul(lam, q), row[ny - 1 - j])
        if first:
            for c, part in enumerate((*p, *q)):
                pq[c, k, :] = part
        else:
            q = cadd(cmul(power(lam, ny), q), (before[2, k, :], before[3, k, :]))
            step = pq.shape[2]
            for c, part in enumerate((*p, *q)):
                pq[pl.ds(i * (KB // step), KB // step), c] = part.reshape(KB // step, step, nz)
        return carry

    lax.fori_loop(0, nk // KB, block, 0)


def local_solve(root, f0, f1, w0, w1):
    _, half, nk, _ = f0.shape
    ny = 2 * half

    def row(refs, j, k):
        ref = refs[j // half]
        return ref[0, j % half, k, :], ref[1, j % half, k, :]

    def block(i, carry):
        k = pl.ds(pl.multiple_of(i * KB, KB), KB)
        rows = own_rows(root, i, KB)
        lam = root[0, rows, :], root[1, rows, :]
        gam = root[2, rows, :], root[3, rows, :]

        def put(j, value):
            ref = (w0, w1)[j // half]
            ref[0, j % half, k, :], ref[1, j % half, k, :] = value

        p = None
        for j in range(ny):
            f = row((f0, f1), j, k)
            p = f if p is None else cadd(cmul(lam, p), f)
            put(j, p)
        q = None
        for j in reversed(range(ny)):
            here = row((w0, w1), j, k)
            if q is None:
                q = row((f0, f1), j, k)
            else:
                q = cmul(lam, q)
                here = cadd(here, q)
                q = cadd(q, row((f0, f1), j, k))
            put(j, cmul(gam, here))
        return carry

    lax.fori_loop(0, nk // KB, block, 0)


def reduced_solve(ny, root, pq, fb):
    n, _, rows, _ = pq.shape
    first = (lax.axis_index("py") * n + lax.axis_index("px")) * rows
    own = pl.ds(pl.multiple_of(first, rows), rows)
    lam = root[0, own, :], root[1, own, :]
    gam = root[2, own, :], root[3, own, :]
    block = power(lam, ny)
    whole = power(block, n)
    last_f = pq[0, 0], pq[0, 1]
    last_b = pq[n - 1, 2], pq[n - 1, 3]
    for i in range(1, n):
        last_f = cadd(cmul(block, last_f), (pq[i, 0], pq[i, 1]))
        last_b = cadd(cmul(block, last_b), (pq[n - 1 - i, 2], pq[n - 1 - i, 3]))
    around = cmul(whole, cmul(lam, lam))
    both = cmul(around, whole)
    det = 1.0 - both[0], -both[1]
    size = det[0] * det[0] + det[1] * det[1]
    inverse = det[0] / size, -det[1] / size
    minus = -lam[0], -lam[1]
    f = cmul(inverse, cadd(cmul(minus, last_b), cmul(around, last_f)))
    b = cmul(inverse, cadd(cmul(minus, last_f), cmul(around, last_b)))
    for i in range(n):
        fb[i, 0], fb[i, 1] = cmul(gam, f)
        k = n - 1 - i
        fb[k, 2], fb[k, 3] = cmul(gam, b)
        if i < n - 1:
            f = cadd(cmul(block, f), (pq[i, 0], pq[i, 1]))
            b = cadd(cmul(block, b), (pq[k, 2], pq[k, 3]))


def inverse_z(part, s_ref, root, w_ref, fb, send, keep, u):
    me = lax.axis_index("py")
    _, ny, nk, nz = w_ref.shape
    w = send.shape[3]

    def block(i, carry):
        k = pl.ds(pl.multiple_of(i * KB, KB), KB)
        rows = own_rows(root, i, KB)
        lam = root[0, rows, :], root[1, rows, :]
        step = fb.shape[2]
        got = pl.ds(i * (KB // step), KB // step)
        f = fb[got, 0].reshape(KB, nz), fb[got, 1].reshape(KB, nz)
        b = fb[got, 2].reshape(KB, nz), fb[got, 3].reshape(KB, nz)
        past = power(lam, ny)
        if part:
            f = cmul(past, f)
        else:
            b = cmul(past, b)
        for j in range(ny):
            f = cmul(lam, f)
            u[0, j], u[1, j] = cadd((w_ref[0, j, k, :], w_ref[1, j, k, :]), f)
        for j in reversed(range(ny)):
            b = cmul(lam, b)
            u[0, j], u[1, j] = cadd((u[0, j], u[1, j]), b)
        high, low = split(u[...].reshape(2 * ny * KB, nz))
        left = jnp.concatenate([high, low, high], axis=1)
        out = dot(left, jnp.concatenate([s_ref[1 - me], s_ref[me]], axis=1))
        send[:, :, k, :] = out[:, :w].reshape(2, ny, KB, w)
        keep[:, :, k, :] = out[:, w:].reshape(2, ny, KB, w)
        return carry

    lax.fori_loop(0, nk // KB, block, 0)


def inverse_x(part, s_ref, keep, recv, src_hbm, speed_hbm, out, sums, src, speed, sems):
    me = lax.axis_index("py")
    _, nx, _, w = out.shape
    rows = pl.ds(part * YB, YB)
    copies = [
        pltpu.make_async_copy(src_hbm.at[:, :, rows, :], src, sems.at[0]),
        pltpu.make_async_copy(speed_hbm.at[:, rows, :], speed, sems.at[1]),
    ]
    for copy in copies:
        copy.start()
    left = jnp.concatenate([s_ref[me], s_ref[1 - me]], axis=1)
    for c in range(2):
        cols = []
        for y in range(YB):
            parts = []
            for ref in (keep, recv):
                high, low = split(ref[c, y])
                parts += [high, low, high]
            cols.append(jnp.concatenate(parts, axis=0))
        got = dot(left, jnp.concatenate(cols, axis=1))
        flat = out.at[c].reshape(nx * YB, w)
        for y in range(YB):
            flat[pl.ds(y, nx, stride=YB), :] = got[:, y * w : (y + 1) * w]
    for copy in copies:
        copy.wait()
    damped = damping * wave_square

    def step(i, acc):
        s0, s1 = src[0, i], src[1, i]
        p0, p1 = out[0, i], out[1, i]
        c = speed[i]
        factor = wave_square - wave_square / (c * c)
        a0 = s0 + factor * p0 + damped * p1
        a1 = s1 + factor * p1 - damped * p0
        new = (
            s0 * s0 + s1 * s1,
            s0 * a0 + s1 * a1,
            s0 * a1 - s1 * a0,
            a0 * a0 + a1 * a1,
        )
        return tuple(x + y for x, y in zip(acc, new))

    zero = jnp.zeros((YB, w), f32)
    acc = lax.fori_loop(0, nx, step, (zero,) * 4, unroll=8)
    for i, a in enumerate(acc):
        sums[i : i + 1, :] = jnp.sum(a, axis=0, keepdims=True)


def finish(total, ps0, ps1, out_hbm, scaled, sems):
    sums = jnp.sum(jnp.sum(total[...], axis=0), axis=1, keepdims=True)
    square, re, im, size = (sums[i : i + 1] for i in range(4))
    beta2 = square + epsilon
    re, im, size = re / beta2, im / beta2, size / beta2
    den = size - (re * re + im * im) * (epsilon / beta2) + epsilon
    a, b = re / den, -im / den
    _, nx, _, w = ps0.shape
    a = jnp.broadcast_to(a, (YB, w))
    b = jnp.broadcast_to(b, (YB, w))
    copies = []
    for part, ps in enumerate((ps0, ps1)):
        for x in range(0, nx, XC):
            for i in range(x, x + XC):
                p0, p1 = ps[0, i], ps[1, i]
                scaled[part, 0, i] = a * p0 - b * p1
                scaled[part, 1, i] = a * p1 + b * p0
            copy = pltpu.make_async_copy(
                scaled.at[part, :, pl.ds(x, XC)],
                out_hbm.at[:, pl.ds(x, XC), pl.ds(part * YB, YB), :],
                sems.at[len(copies)],
            )
            copy.start()
            copies.append(copy)
    for copy in copies:
        copy.wait()


def params(mib, *dims):
    return pltpu.CompilerParams(dimension_semantics=dims or None, vmem_limit_bytes=mib * 2**20)


def whole(a):
    return pl.BlockSpec(a.shape, lambda *_: (0,) * a.ndim)


VM = pl.BlockSpec(memory_space=pltpu.VMEM)
ANY = pl.BlockSpec(memory_space=pl.ANY)


def cost(flops, moved):
    return pl.CostEstimate(flops=flops, bytes_accessed=moved, transcendentals=0)


def on_device(source, speed):
    _, nx, ny, w = source.shape
    cores, ring = lax.axis_size("py"), lax.axis_size("px")
    nz, nk = w * cores, nx // cores
    other = [(i, cores - 1 - i) for i in range(cores)]
    sds = lambda *shape: jax.ShapeDtypeStruct(shape, f32)

    hx, lx = halves_of(sine_table(nx))
    hz, lz = halves_of(sine_table(nz))
    sx_in = jnp.asarray(np.concatenate([hx, hx, lx], 1).reshape(2, nk, 3 * nx))
    sz_in = jnp.asarray(np.stack([np.concatenate([hz[h * w : (h + 1) * w]] * 2 + [lz[h * w : (h + 1) * w]], 0) for h in (0, 1)]))
    sz_out = jnp.asarray(np.stack([np.concatenate([hz, hz, lz], 0)[:, h * w : (h + 1) * w] for h in (0, 1)]))
    sx_out = jnp.asarray(np.stack([np.concatenate([t[:, h * nk : (h + 1) * nk] for t in (hx, hx, lx)], 1) for h in (0, 1)]))
    root = jnp.asarray(root_tables(nx, nz))
    piece = sds(2, YB, nk, w)
    modes = sds(2, YB, nk, nz)
    rows = nk // ring
    flops = 2 * 2 * nx * YB * w * nx * 3
    est = cost(flops, 4 * 2**20)

    spec = pl.BlockSpec((1, YB, nk, w), lambda c: (c, 0, 0, 0))
    moved = []
    for h in range(2):
        send, keep = pl.pallas_call(
            forward_x,
            grid=(2,),
            in_specs=[whole(sx_in), pl.BlockSpec((1, nx, YB, w), functools.partial(lambda h, c: (c, 0, h, 0), h))],
            out_specs=[spec, spec],
            out_shape=[piece, piece],
            compiler_params=params(12, "arbitrary"),
            cost_estimate=est,
            name="forward_x",
        )(sx_in, source)
        moved.append((keep, lax.ppermute(send, "py", other)))
    f, carry = [], ()
    for h in range(2):
        got, pq = pl.pallas_call(
            functools.partial(forward_z, h == 0),
            in_specs=[VM] * (4 + len(carry)),
            out_specs=[VM, VM],
            out_shape=[modes, sds(4, nk, nz) if h == 0 else sds(ring, 4, rows, nz)],
            compiler_params=params(12),
            cost_estimate=est,
            name="forward_z",
        )(sz_in, root, *moved[h], *carry)
        f.append(got)
        carry = (pq,)
    pq = lax.all_to_all(pq, "px", 0, 0, tiled=True)
    local = pl.pallas_call(
        local_solve,
        in_specs=[VM] * 3,
        out_specs=[VM, VM],
        out_shape=[modes, modes],
        compiler_params=params(8),
        cost_estimate=cost(2 * flops, 8 * 2**20),
        name="local_solve",
    )(root, *f)
    fb = pl.pallas_call(
        functools.partial(reduced_solve, ny),
        in_specs=[VM] * 2,
        out_specs=VM,
        out_shape=sds(ring, 4, rows, nz),
        compiler_params=params(8),
        cost_estimate=cost(10**7, 2**20),
        name="reduced_solve",
    )(root, pq)
    fb = lax.all_to_all(fb, "px", 0, 0, tiled=True)
    moved = []
    for h in range(2):
        send, keep = pl.pallas_call(
            functools.partial(inverse_z, h),
            in_specs=[VM] * 4,
            out_specs=[VM, VM],
            out_shape=[piece, piece],
            scratch_shapes=[pltpu.VMEM((2, YB, KB, nz), f32)],
            compiler_params=params(12),
            cost_estimate=est,
            name="inverse_z",
        )(sz_out, root, local[h], fb)
        moved.append((keep, lax.ppermute(send, "py", other)))
    solved, sums = [], []
    for h in range(2):
        got, part = pl.pallas_call(
            functools.partial(inverse_x, h),
            in_specs=[VM, VM, VM, ANY, ANY],
            out_specs=[VM, VM],
            out_shape=[sds(2, nx, YB, w), sds(4, w)],
            scratch_shapes=[pltpu.VMEM((2, nx, YB, w), f32), pltpu.VMEM((nx, YB, w), f32), pltpu.SemaphoreType.DMA((2,))],
            compiler_params=params(16),
            cost_estimate=est,
            name="inverse_x",
        )(sx_out, *moved[h], source, speed)
        solved.append(got)
        sums.append(part)
    sums = sums[0] + sums[1]
    sums = sums + lax.ppermute(sums, "py", other)
    every = lax.all_to_all(jnp.broadcast_to(sums[None], (ring, 4, w)), "px", 0, 0, tiled=True)
    return pl.pallas_call(
        finish,
        in_specs=[VM] * 3,
        out_specs=ANY,
        out_shape=sds(*source.shape),
        scratch_shapes=[pltpu.VMEM((2, 2, nx, YB, w), f32), pltpu.SemaphoreType.DMA((2 * nx // XC,))],
        compiler_params=params(16),
        cost_estimate=cost(10**7, 8 * 2**20),
        name="finish",
    )(every, *solved)


def solution(mesh):
    return jax.shard_map(
        on_device,
        mesh=mesh,
        in_specs=(P(None, "samples", "px", "py"), P("samples", "px", "py")),
        out_specs=P(None, "samples", "px", "py"),
        check_vma=False,
    )
```

time: 152 us -> 133 us (0.88)
  Pallas kernels: 42.8 us -> 21.7 us
  local copies, waits for them, and re-layouts: 3.45 us -> 15 us
  waiting for transfers between devices: 32.9 us -> 22.7 us
    pallas_call x7 -> x11, Pallas kernels: 42.8 us -> 21.7 us  [the longest x2 5.05 us: on_device(): pl.pallas_call(functools.partial(inverse_x, h), in_specs=[VM, VM, VM, ANY...]
    unnamed x8 -> x32, local copies, waits for them, and re-layouts: 3.44 us -> 15 us
    ppermute x2 -> x4, waiting for transfers between devices: 8.73 us -> 0.43 us  [on_device(): moved.append((keep, lax.ppermute(send, 'py', other)))]
    all_to_all x1, waiting for transfers between devices: 22.9 us -> 21.2 us  [on_device(): fb = lax.all_to_all(fb, 'px', 0, 0, tiled=True)]
  transfers between devices with their start and end apart: 4 -> 6, of which waited for: 4 -> 3; matrix products, arithmetic and copies ran while one was open for 0% -> 0% of each run, Pallas kernels for 4% -> 8%
where the time goes in v2:
time: 133 us; the launch traced here: 132 us
  blocking collectives  64.6 us (49%)
  waiting for transfers between devices  22.7 us (17%)
  Pallas kernels  21.7 us (16%)
  local copies, waits for them, and re-layouts  15 us (11%)
  starting transfers between devices  8.28 us (6%)
    all_to_all x1, blocking collectives, on_device(): pq = lax.all_to_all(pq, 'px', 0, 0, tiled=True)  45.8 us
    all_to_all x1, waiting for transfers between devices, on_device(): fb = lax.all_to_all(fb, 'px', 0, 0, tiled=True)  21.2 us
    all_to_all x1, blocking collectives, on_device(): lax.all_to_all(jnp.broadcast_to(sums[None], (ring, 4, w)), 'px', 0, 0, ti...  18.8 us
    unnamed x32, local copies, waits for them, and re-layouts  15 us
    all_to_all x1, starting transfers between devices, on_device(): fb = lax.all_to_all(fb, 'px', 0, 0, tiled=True)  6.68 us
    pallas_call x2, Pallas kernels, on_device(): pl.pallas_call(functools.partial(inverse_x, h), in_specs=[VM, VM, VM, ANY...  5.05 us
    pallas_call x2, Pallas kernels, on_device(): pl.pallas_call(functools.partial(forward_z, h == 0), in_specs=[VM] * (4 +...  4.47 us
    pallas_call x2, Pallas kernels, on_device(): pl.pallas_call(functools.partial(inverse_z, h), in_specs=[VM] * 4, out_sp...  3.76 us
  transfers between devices with their start and end apart: 6, of which 3 were waited for; matrix products, arithmetic and copies ran while one was open for 0% of the time, Pallas kernels for 8%

profile of v2, /device:TPU:86, one launch (start us, length us, event | category | flops | bytes accessed | tf_op | source)
XLA Modules:
  0.0 132.5 jit_solution(16687896329439819809)
XLA Ops:
  0.0 0.0 copy-start
  0.0 2.2 %copy-done = f32[2,256,16,128]{3,2,1,0:T(8,128)S(1)} copy-done((f32[2,256,16,128]{3,2,1,0:T(8,128)S(1)}, f32[2,256,16,128]{3,2,1,0:T(8,128)}, u32[]{:S(2)}) %copy-start) | copy-done | bytes 4194328
  2.2 0.0 copy-start.9
  2.2 1.0 copy-done.9
  3.2 1.6 %forward_x.2 = (f32[2,8,128,128]{3,2,1,0:T(8,128)S(1)}, f32[2,8,128,128]{3,2,1,0:T(8,128)S(1)}) custom-call(bf16[2,128,768]{2,1,0:T(8,128)(2,1)S(1)} %copy-done.9, f32[2,256,16,128]{3,2,1,0:T(8,128)S(1)} %copy-done), custom_call_target="tpu_custom_call" | custom-call | flops 805306368 | bytes 4194304 | tf_op jit(solution)/shard_map/forward_x/pallas_call | solution.py:351
  4.8 0.0 copy-start.2
  4.8 0.0 copy-start.10
  4.8 0.1 collective-permute-start
  5.0 1.6 %forward_x.3 = (f32[2,8,128,128]{3,2,1,0:T(8,128)S(1)}, f32[2,8,128,128]{3,2,1,0:T(8,128)S(1)}) custom-call(bf16[2,128,768]{2,1,0:T(8,128)(2,1)S(1)} %copy-done.9, f32[2,256,16,128]{3,2,1,0:T(8,128)S(1)} %copy-done), custom_call_target="tpu_custom_call" | custom-call | flops 805306368 | bytes 4194304 | tf_op jit(solution)/shard_map/forward_x/pallas_call | solution.py:351
  6.6 0.6 collective-permute-start.1
  7.2 0.4 collective-permute-done.refs_1_
  7.6 0.0 copy-done.2
  7.6 0.0 copy-done.10
  7.6 2.2 %forward_z.2 = (f32[2,8,128,256]{3,2,1,0:T(8,128)S(1)}, f32[4,128,256]{2,1,0:T(8,128)S(1)}) custom-call(bf16[2,384,256]{2,1,0:T(8,128)(2,1)S(1)} %copy-done.10, f32[4,256,256]{2,1,0:T(8,128)S(1)} %copy-done.2, f32[2,8,128,128]{3,2,1,0:T(8,128)S(1)} %get-tuple-element.23.refs_0_, f32[2,8,128,128]{3,2,1,0:T(8,128)S(1)} %collective-permute-done.refs_1_), custom_call_target="tpu_custom_call" | custom-call | flops 805306368 | bytes 4194304 | tf_op jit(solution)/shard_map/forward_z/pallas_call | solution.py:364
  9.8 0.0 copy-start.12
  9.8 1.3 copy-done.12
  11.1 0.0 collective-permute-done.1.refs_1_
  11.1 2.3 %forward_z.3 = (f32[2,8,128,256]{3,2,1,0:T(8,128)S(1)}, f32[16,4,8,256]{3,2,1,0:T(8,128)S(1)}) custom-call(bf16[2,384,256]{2,1,0:T(8,128)(2,1)S(1)} %copy-done.10, f32[4,256,256]{2,1,0:T(8,128)S(1)} %copy-done.2, f32[2,8,128,128]{3,2,1,0:T(8,128)S(1)} %get-tuple-element.26.refs_0_, f32[2,8,128,128]{3,2,1,0:T(8,128)S(1)} %collective-permute-done.1.refs_1_, ...), custom_call_target="tpu_custom_call" | custom-call | flops 805306368 | bytes 4194304 | tf_op jit(solution)/shard_map/forward_z/pallas_call | solution.py:364
  13.4 0.0 copy-start.14
  13.4 1.3 %copy-done.14 = f32[2,8,128,256]{3,2,1,0:T(8,128)} copy-done((f32[2,8,128,256]{3,2,1,0:T(8,128)}, f32[2,8,128,256]{3,2,1,0:T(8,128)S(1)}, u32[]{:S(2)}) %copy-start.14) | copy-done | bytes 2097176
  14.8 45.8 %all_to_all.15.pq = f32[16,4,8,256]{3,2,1,0:T(8,128)S(1)} all-to-all(f32[16,4,8,256]{3,2,1,0:T(8,128)S(1)} %get-tuple-element.31), channel_id=1, replica_groups=mesh['samples'=4,'px'=16,'py'=2] {'px'}, dimensions={0} | all-to-all | bytes 1048576 | tf_op jit(solution)/shard_map/all_to_all | solution.py:375
  60.6 1.0 reduced_solve.1
  61.6 6.7 %all-to-all-start.1 = ((f32[16,4,8,256]{3,2,1,0:T(8,128)}), f32[16,4,8,256]{3,2,1,0:T(8,128)S(1)}, u32[]{:S(2)}, u32[]{:S(2)}) async-start(f32[16,4,8,256]{3,2,1,0:T(8,128)} %reduced_solve.1), calls=%async_computation.1 | async-start | bytes 1048576 | tf_op jit(solution)/shard_map/all_to_all | solution.py:394
  68.3 0.0 copy-start.13
  68.3 1.6 %copy-done.13 = f32[2,8,128,256]{3,2,1,0:T(8,128)S(1)} copy-done((f32[2,8,128,256]{3,2,1,0:T(8,128)S(1)}, f32[2,8,128,256]{3,2,1,0:T(8,128)}, u32[]{:S(2)}) %copy-start.13) | copy-done | bytes 2097176
  69.9 0.0 copy-start.15
  69.9 1.6 %copy-done.15 = f32[2,8,128,256]{3,2,1,0:T(8,128)S(1)} copy-done((f32[2,8,128,256]{3,2,1,0:T(8,128)S(1)}, f32[2,8,128,256]{3,2,1,0:T(8,128)}, u32[]{:S(2)}) %copy-start.15) | copy-done | bytes 2097176
  71.5 0.0 copy-start.11
  71.5 1.9 %local_solve.1 = (f32[2,8,128,256]{3,2,1,0:T(8,128)S(1)}, f32[2,8,128,256]{3,2,1,0:T(8,128)S(1)}) custom-call(f32[4,256,256]{2,1,0:T(8,128)S(1)} %copy-done.2, f32[2,8,128,256]{3,2,1,0:T(8,128)S(1)} %copy-done.13, f32[2,8,128,256]{3,2,1,0:T(8,128)S(1)} %copy-done.15), custom_call_target="tpu_custom_call" | custom-call | flops 1610612736 | bytes 8388608 | tf_op jit(solution)/shard_map/local_solve/pallas_call | solution.py:376
  73.4 0.0 copy-start.4
  73.4 1.3 copy-done.4
  74.7 0.0 copy-start.6
  74.7 1.3 %copy-done.6 = f32[2,8,128,256]{3,2,1,0:T(8,128)} copy-done((f32[2,8,128,256]{3,2,1,0:T(8,128)}, f32[2,8,128,256]{3,2,1,0:T(8,128)S(1)}, u32[]{:S(2)}) %copy-start.6) | copy-done | bytes 2097176
  76.0 21.2 %all-to-all-done.1.fb = f32[16,4,8,256]{3,2,1,0:T(8,128)S(1)} async-done(((f32[16,4,8,256]{3,2,1,0:T(8,128)}), f32[16,4,8,256]{3,2,1,0:T(8,128)S(1)}, u32[]{:S(2)}, u32[]{:S(2)}) %all-to-all-start.1) | async-done | bytes 524320 | tf_op jit(solution)/shard_map/all_to_all | solution.py:394
  97.2 0.0 copy-done.11
  97.3 0.0 copy-start.7
  97.3 1.6 %copy-done.7 = f32[2,8,128,256]{3,2,1,0:T(8,128)S(1)} copy-done((f32[2,8,128,256]{3,2,1,0:T(8,128)S(1)}, f32[2,8,128,256]{3,2,1,0:T(8,128)}, u32[]{:S(2)}) %copy-start.7) | copy-done | bytes 2097176
  98.8 0.0 copy-start.1
  98.8 1.9 %inverse_z.3 = (f32[2,8,128,128]{3,2,1,0:T(8,128)S(1)}, f32[2,8,128,128]{3,2,1,0:T(8,128)S(1)}) custom-call(bf16[2,768,128]{2,1,0:T(8,128)(2,1)S(1)} %copy-done.11, f32[4,256,256]{2,1,0:T(8,128)S(1)} %copy-done.2, f32[2,8,128,256]{3,2,1,0:T(8,128)S(1)} %copy-done.7, f32[16,4,8,256]{3,2,1,0:T(8,128)S(1)} %all-to-all-done.1.fb), custom_call_target="tpu_custom_call" | custom-call | flops 805306368 | bytes 4194304 | tf_op jit(solution)/shard_map/inverse_z/pallas_call | solution.py:397
  100.7 0.0 copy-start.3
  100.7 0.1 collective-permute-start.3
  100.9 0.0 copy-start.5
  100.9 1.7 %copy-done.5 = f32[2,8,128,256]{3,2,1,0:T(8,128)S(1)} copy-done((f32[2,8,128,256]{3,2,1,0:T(8,128)S(1)}, f32[2,8,128,256]{3,2,1,0:T(8,128)}, u32[]{:S(2)}) %copy-start.5) | copy-done | bytes 2097176
  102.6 0.0 copy-start.8
  102.6 1.9 %inverse_z.2 = (f32[2,8,128,128]{3,2,1,0:T(8,128)S(1)}, f32[2,8,128,128]{3,2,1,0:T(8,128)S(1)}) custom-call(bf16[2,768,128]{2,1,0:T(8,128)(2,1)S(1)} %copy-done.11, f32[4,256,256]{2,1,0:T(8,128)S(1)} %copy-done.2, f32[2,8,128,256]{3,2,1,0:T(8,128)S(1)} %copy-done.5, f32[16,4,8,256]{3,2,1,0:T(8,128)S(1)} %all-to-all-done.1.fb), custom_call_target="tpu_custom_call" | custom-call | flops 805306368 | bytes 4194304 | tf_op jit(solution)/shard_map/inverse_z/pallas_call | solution.py:397
  104.5 0.5 collective-permute-start.2
  105.0 0.0 collective-permute-done.3.recv
  105.0 0.0 copy-done.1
  105.0 0.0 copy-done.3
  105.0 0.0 copy-done.8
  105.0 2.6 %inverse_x.3 = (f32[2,256,8,128]{3,2,1,0:T(8,128)S(1)}, f32[4,128]{1,0:T(4,128)S(1)}) custom-call(bf16[2,256,384]{2,1,0:T(8,128)(2,1)S(1)} %copy-done.8, f32[2,8,128,128]{3,2,1,0:T(8,128)S(1)} %get-tuple-element.36.keep, f32[2,8,128,128]{3,2,1,0:T(8,128)S(1)} %collective-permute-done.3.recv, f32[2,256,16,128]{3,2,1,0:T(8,128)S(1)} %copy-done.1, ...), custom_call_target="tpu_custom_call" | custom-call | flops 805306368 | bytes 4194304 | tf_op jit(solution)/shard_map/inverse_x/pallas_call | solution.py:410
  107.6 0.0 collective-permute-done.2.recv
  107.6 2.5 %inverse_x.2 = (f32[2,256,8,128]{3,2,1,0:T(8,128)S(1)}, f32[4,128]{1,0:T(4,128)S(1)}) custom-call(bf16[2,256,384]{2,1,0:T(8,128)(2,1)S(1)} %copy-done.8, f32[2,8,128,128]{3,2,1,0:T(8,128)S(1)} %get-tuple-element.32.keep, f32[2,8,128,128]{3,2,1,0:T(8,128)S(1)} %collective-permute-done.2.recv, f32[2,256,16,128]{3,2,1,0:T(8,128)S(1)} %copy-done.1, ...), custom_call_target="tpu_custom_call" | custom-call | flops 805306368 | bytes 4194304 | tf_op jit(solution)/shard_map/inverse_x/pallas_call | solution.py:410
  110.1 0.3 collective-permute-start.4
  110.3 1.0 collective-permute-done.4
  111.4 18.8 %all_to_all.16.total = f32[16,4,128]{2,1,0:T(4,128)S(1)} all-to-all(f32[16,4,128]{2,1,0:T(4,128)S(1)} %broadcast_in_dim.2), channel_id=1, replica_groups=mesh['samples'=4,'px'=16,'py'=2] {'px'}, dimensions={0} | all-to-all | bytes 65536 | tf_op jit(solution)/shard_map/all_to_all | solution.py:424
  130.2 2.3 %finish.1 = f32[2,256,16,128]{3,2,1,0:T(8,128)} custom-call(f32[16,4,128]{2,1,0:T(4,128)S(1)} %all_to_all.16.total, f32[2,256,8,128]{3,2,1,0:T(8,128)S(1)} %get-tuple-element.39.ps0, f32[2,256,8,128]{3,2,1,0:T(8,128)S(1)} %get-tuple-element.40.ps1), custom_call_target="tpu_custom_call" | custom-call | flops 10000000 | bytes 8388608 | tf_op jit(solution)/shard_map/finish/pallas_call | solution.py:425
  (3 shorter events, 0.0 us)
Async XLA Ops:
  0.0 2.2 %copy-start = (f32[2,256,16,128]{3,2,1,0:T(8,128)S(1)}, f32[2,256,16,128]{3,2,1,0:T(8,128)}, u32[]{:S(2)}) copy-start(f32[2,256,16,128]{3,2,1,0:T(8,128)} %src_hbm.3) | copy-start | bytes 12582916
  2.2 1.0 copy-start.9
  4.8 2.8 %copy-start.2 = (f32[4,256,256]{2,1,0:T(8,128)S(1)}, f32[4,256,256]{2,1,0:T(8,128)}, u32[]{:S(2)}) copy-start(f32[4,256,256]{2,1,0:T(8,128)} %constant.14.clone.root) | copy-start | bytes 3145732
  4.8 2.8 %copy-start.10 = (bf16[2,384,256]{2,1,0:T(8,128)(2,1)S(1)}, bf16[2,384,256]{2,1,0:T(8,128)(2,1)}, u32[]{:S(2)}) copy-start(bf16[2,384,256]{2,1,0:T(8,128)(2,1)} %constant.11.clone.s_ref) | copy-start | bytes 1179652
  4.8 2.8 %collective-permute-start = (f32[2,8,128,128]{3,2,1,0:T(8,128)S(1)}, f32[2,8,128,128]{3,2,1,0:T(8,128)S(1)}, u32[]{:S(2)}, u32[]{:S(2)}) collective-permute-start(f32[2,8,128,128]{3,2,1,0:T(8,128)S(1)} %get-tuple-element.24), channel_id=1, source_target_pairs={{0,1},{1,0},{2,3},{3,2},{4,5},{5,4},{6,7},{7,6},{8,9},{9,8},{10,11... | collective-permute-start | bytes 3145736 | tf_op jit(solution)/shard_map/ppermute | solution.py:361
  6.6 4.6 %collective-permute-start.1 = (f32[2,8,128,128]{3,2,1,0:T(8,128)S(1)}, f32[2,8,128,128]{3,2,1,0:T(8,128)S(1)}, u32[]{:S(2)}, u32[]{:S(2)}) collective-permute-start(f32[2,8,128,128]{3,2,1,0:T(8,128)S(1)} %get-tuple-element.27), channel_id=1, source_target_pairs={{0,1},{1,0},{2,3},{3,2},{4,5},{5,4},{6,7},{7,6},{8,9},{9,8},{10,11... | collective-permute-start | bytes 3145736 | tf_op jit(solution)/shard_map/ppermute | solution.py:361
  9.8 1.3 copy-start.12
  13.4 1.3 %copy-start.14 = (f32[2,8,128,256]{3,2,1,0:T(8,128)}, f32[2,8,128,256]{3,2,1,0:T(8,128)S(1)}, u32[]{:S(2)}) copy-start(f32[2,8,128,256]{3,2,1,0:T(8,128)S(1)} %get-tuple-element.29.f1) | copy-start | bytes 6291460
  61.6 35.6 %all-to-all-start.1 = ((f32[16,4,8,256]{3,2,1,0:T(8,128)}), f32[16,4,8,256]{3,2,1,0:T(8,128)S(1)}, u32[]{:S(2)}, u32[]{:S(2)}) async-start(f32[16,4,8,256]{3,2,1,0:T(8,128)} %reduced_solve.1), calls=%async_computation.1 | async-start | bytes 1048576 | tf_op jit(solution)/shard_map/all_to_all | solution.py:394
  68.3 1.6 %copy-start.13 = (f32[2,8,128,256]{3,2,1,0:T(8,128)S(1)}, f32[2,8,128,256]{3,2,1,0:T(8,128)}, u32[]{:S(2)}) copy-start(f32[2,8,128,256]{3,2,1,0:T(8,128)} %copy-done.12) | copy-start | bytes 6291460
  69.9 1.6 %copy-start.15 = (f32[2,8,128,256]{3,2,1,0:T(8,128)S(1)}, f32[2,8,128,256]{3,2,1,0:T(8,128)}, u32[]{:S(2)}) copy-start(f32[2,8,128,256]{3,2,1,0:T(8,128)} %copy-done.14) | copy-start | bytes 6291460
  71.5 25.7 %copy-start.11 = (bf16[2,768,128]{2,1,0:T(8,128)(2,1)S(1)}, bf16[2,768,128]{2,1,0:T(8,128)(2,1)}, u32[]{:S(2)}) copy-start(bf16[2,768,128]{2,1,0:T(8,128)(2,1)} %constant.12.clone.s_ref) | copy-start | bytes 1179652
  73.4 1.3 copy-start.4
  74.7 1.3 %copy-start.6 = (f32[2,8,128,256]{3,2,1,0:T(8,128)}, f32[2,8,128,256]{3,2,1,0:T(8,128)S(1)}, u32[]{:S(2)}) copy-start(f32[2,8,128,256]{3,2,1,0:T(8,128)S(1)} %get-tuple-element.35.w_ref) | copy-start | bytes 6291460
  97.3 1.6 %copy-start.7 = (f32[2,8,128,256]{3,2,1,0:T(8,128)S(1)}, f32[2,8,128,256]{3,2,1,0:T(8,128)}, u32[]{:S(2)}) copy-start(f32[2,8,128,256]{3,2,1,0:T(8,128)} %copy-done.6) | copy-start | bytes 6291460
  98.8 6.1 %copy-start.1 = (f32[2,256,16,128]{3,2,1,0:T(8,128)S(1)}, f32[2,256,16,128]{3,2,1,0:T(8,128)}, u32[]{:S(2)}) copy-start(f32[2,256,16,128]{3,2,1,0:T(8,128)} %src_hbm.3) | copy-start | bytes 12582916
  100.7 4.2 %copy-start.3 = (f32[256,16,128]{2,1,0:T(8,128)S(1)}, f32[256,16,128]{2,1,0:T(8,128)}, u32[]{:S(2)}) copy-start(f32[256,16,128]{2,1,0:T(8,128)} %speed_hbm.3) | copy-start | bytes 6291460
  100.7 4.2 %collective-permute-start.3 = (f32[2,8,128,128]{3,2,1,0:T(8,128)S(1)}, f32[2,8,128,128]{3,2,1,0:T(8,128)S(1)}, u32[]{:S(2)}, u32[]{:S(2)}) collective-permute-start(f32[2,8,128,128]{3,2,1,0:T(8,128)S(1)} %get-tuple-element.37), channel_id=1, source_target_pairs={{0,1},{1,0},{2,3},{3,2},{4,5},{5,4},{6,7},{7,6},{8,9},{9,8},{10,11... | collective-permute-start | bytes 3145736 | tf_op jit(solution)/shard_map/ppermute | solution.py:407
  100.9 1.7 %copy-start.5 = (f32[2,8,128,256]{3,2,1,0:T(8,128)S(1)}, f32[2,8,128,256]{3,2,1,0:T(8,128)}, u32[]{:S(2)}) copy-start(f32[2,8,128,256]{3,2,1,0:T(8,128)} %copy-done.4) | copy-start | bytes 6291460
  102.6 2.4 %copy-start.8 = (bf16[2,256,384]{2,1,0:T(8,128)(2,1)S(1)}, bf16[2,256,384]{2,1,0:T(8,128)(2,1)}, u32[]{:S(2)}) copy-start(bf16[2,256,384]{2,1,0:T(8,128)(2,1)} %constant.13.clone.s_ref) | copy-start | bytes 1179652
  104.5 3.1 %collective-permute-start.2 = (f32[2,8,128,128]{3,2,1,0:T(8,128)S(1)}, f32[2,8,128,128]{3,2,1,0:T(8,128)S(1)}, u32[]{:S(2)}, u32[]{:S(2)}) collective-permute-start(f32[2,8,128,128]{3,2,1,0:T(8,128)S(1)} %get-tuple-element.33), channel_id=1, source_target_pairs={{0,1},{1,0},{2,3},{3,2},{4,5},{5,4},{6,7},{7,6},{8,9},{9,8},{10,11... | collective-permute-start | bytes 3145736 | tf_op jit(solution)/shard_map/ppermute | solution.py:407
  110.1 1.3 collective-permute-start.4

commit v3 on v2

v3 whole, which is shorter than its diff:
```python
import functools
import numpy as np
import jax
import jax.numpy as jnp
from jax import lax
from jax.experimental import pallas as pl
from jax.experimental.pallas import tpu as pltpu
from jax.sharding import PartitionSpec as P

wave_square = 0.25
damping = 0.5
epsilon = 1e-06
f32 = jnp.float32
bf16 = jnp.bfloat16
YB = 8
KB = 32
XC = 32
CHUNKS = 2


def sine_table(length):
    k = np.arange(1, length + 1, dtype=np.float64)
    phases = np.mod(np.outer(k, k), 2 * (length + 1)) * (np.pi / (length + 1))
    return np.sqrt(2.0 / (length + 1)) * np.sin(phases)


def halves_of(table):
    table = table.astype(np.float32)
    high = table.astype(bf16)
    low = (table - high.astype(np.float32)).astype(bf16)
    return high, low


def eigen_line(length):
    k = np.arange(1, length + 1, dtype=np.float64)
    return 4.0 * np.sin(np.pi * k / (2.0 * (length + 1))) ** 2


def root_tables(nx, nz):
    near = eigen_line(nx)[:, None] + eigen_line(nz)[None, :] - wave_square + 1j * damping * wave_square
    spread = np.sqrt(near) * np.sqrt(near + 4.0)
    lam = 2.0 / (near + 2.0 + spread)
    gam = 1.0 / spread
    return np.stack([lam.real, lam.imag, gam.real, gam.imag]).astype(np.float32)


def cmul(a, b):
    return a[0] * b[0] - a[1] * b[1], a[0] * b[1] + a[1] * b[0]


def cadd(a, b):
    return a[0] + b[0], a[1] + b[1]


def split(v):
    high = v.astype(bf16)
    return high, (v - high.astype(f32)).astype(bf16)


def dot(a, b):
    return lax.dot_general(a, b, (((1,), (0,)), ((), ())), preferred_element_type=f32)


def stack(s_ref, axis):
    return jnp.concatenate([s_ref[0], s_ref[0], s_ref[1]], axis=axis)


def by_half(me, keep, recv):
    first = me == 0
    return jnp.where(first, keep, recv), jnp.where(first, recv, keep)


def forward_x(part, s_ref, src, send, keep):
    me = lax.axis_index("py")
    _, nx, ny, w = src.shape
    nk = nx // 2
    for c in range(2):
        flat = src.at[c].reshape(nx * ny, w)
        cols = []
        for y in range(YB):
            high, low = split(flat[pl.ds(part * YB + y, nx, stride=ny), :])
            cols.append(jnp.concatenate([high, low, high], axis=0))
        right = jnp.concatenate(cols, axis=1)
        for half, out in ((1 - me, send), (me, keep)):
            rows = pl.ds(pl.multiple_of(half * nk, nk), nk)
            high, low = s_ref[0, rows, :], s_ref[1, rows, :]
            got = dot(jnp.concatenate([high, high, low], axis=1), right)
            for y in range(YB):
                out[c, y] = got[:, y * w : (y + 1) * w]


def own_rows(root, block, kb):
    nk = root.shape[1] // 2
    return pl.ds(pl.multiple_of(lax.axis_index("py") * nk + block * kb, kb), kb)


def power(base, exponent):
    result = None
    while exponent:
        if exponent & 1:
            result = base if result is None else cmul(result, base)
        exponent >>= 1
        if exponent:
            base = cmul(base, base)
    return result


def forward_z(first, s_ref, root, *refs):
    if first:
        keep, recv, f_out, pq = refs
    else:
        keep, recv, before, f_out, pq, *sends = refs
    me = lax.axis_index("py")
    ring, place = lax.axis_size("px"), lax.axis_index("px")
    _, ny, nk, w = keep.shape
    nz = f_out.shape[3]

    def block(send, base, i):
        k = pl.ds(pl.multiple_of((base + i) * KB, KB), KB)
        shape = 2 * ny * KB, w
        both = by_half(me, keep[:, :, k, :].reshape(shape), recv[:, :, k, :].reshape(shape))
        high, low = split(jnp.concatenate(both, axis=1))
        total = dot(jnp.concatenate([high, low, high], axis=1), stack(s_ref, 0))
        total = total.reshape(2, ny, KB, nz)
        f_out[:, :, k, :] = total
        rows = own_rows(root, base + i, KB)
        lam = root[0, rows, :], root[1, rows, :]
        row = [(total[0, j], total[1, j]) for j in range(ny)]
        p = row[0] if first else cadd(cmul(lam, (before[0, k, :], before[1, k, :])), row[0])
        q = row[ny - 1]
        for j in range(1, ny):
            p = cadd(cmul(lam, p), row[j])
            q = cadd(cmul(lam, q), row[ny - 1 - j])
        if not first:
            q = cadd(cmul(power(lam, ny), q), (before[2, k, :], before[3, k, :]))
            wide = 2 * ny
            left, right = images(lam, 2 * wide, ring, place)
            edge = power(lam, wide + 1)
            p, q = (
                csub(p, cmul(cmul(left, edge), q)),
                csub(q, cmul(cmul(right, edge), p)),
            )
            even = place % 2 == 0
            to = pl.ds(pl.multiple_of(i * KB, KB), KB)
            for c in range(2):
                send[c, to, :] = jnp.where(even, p[c], q[c])
        for c, part in enumerate((*p, *q)):
            pq[c, k, :] = part

    over_blocks(block, nk, (None,) if first else sends)


def over_blocks(block, nk, refs):
    number = nk // KB // len(refs)
    for c, ref in enumerate(refs):

        def step(i, carry, c=c, ref=ref):
            block(ref, c * number, i)
            return carry

        lax.fori_loop(0, number, step, 0)


def csub(a, b):
    return a[0] - b[0], a[1] - b[1]


def images(lam, step, ring, place):
    one, base = (jnp.ones_like(lam[0]), jnp.zeros_like(lam[0])), power(lam, step)
    found = [one, one]
    bit = 1
    while bit < ring:
        for i, number in enumerate((place, ring - 1 - place)):
            taken = (number // bit) % 2 == 1
            more = cmul(found[i], base)
            found[i] = tuple(jnp.where(taken, m, f) for m, f in zip(more, found[i]))
        base, bit = cmul(base, base), 2 * bit
    return found


def fold(chunk, exponent, root, now, recv, out):
    kc = out.shape[1]
    rows = own_rows(root, chunk, kc)
    far = power((root[0, rows, :], root[1, rows, :]), exponent)
    out[0], out[1] = cadd((now[0], now[1]), cmul(far, (recv[0], recv[1])))


def fold_pair(chunk, exponent, root, pq, recv, out):
    kc = out.shape[1]
    rows = own_rows(root, chunk, kc)
    k = pl.ds(chunk * kc, kc)
    far = power((root[0, rows, :], root[1, rows, :]), exponent)
    even = lax.axis_index("px") % 2 == 0
    now = tuple(jnp.where(even, pq[2 + c, k, :], pq[c, k, :]) for c in range(2))
    out[0], out[1] = cadd(now, cmul(far, (recv[0], recv[1])))


def carries(chunk, ny, root, pq, near, one, two, fb):
    kc, ring, place = fb.shape[1], lax.axis_size("px"), lax.axis_index("px")
    rows = own_rows(root, chunk, kc)
    k = pl.ds(chunk * kc, kc)
    lam = root[0, rows, :], root[1, rows, :]
    gam = root[2, rows, :], root[3, rows, :]
    block = power(lam, ny)
    direct = one[0], one[1]
    joined = cadd(cmul(block, (two[0], two[1])), (near[0], near[1]))
    even = place % 2 == 0
    f = tuple(jnp.where(even, a, b) for a, b in zip(direct, joined))
    b = tuple(jnp.where(even, b, a) for a, b in zip(direct, joined))
    p, q = (pq[0, k, :], pq[1, k, :]), (pq[2, k, :], pq[3, k, :])
    left, right = images(lam, 2 * ny, ring, place)
    whole = power(lam, 2 * (ny * ring + 1))
    det = 1.0 - whole[0], -whole[1]
    size = det[0] * det[0] + det[1] * det[1]
    scale = cmul(gam, (det[0] / size, -det[1] / size))
    f, b = (
        csub(f, cmul(cmul(left, lam), cadd(cmul(block, b), q))),
        csub(b, cmul(cmul(right, lam), cadd(cmul(block, f), p))),
    )
    fb[0], fb[1] = cmul(scale, f)
    fb[2], fb[3] = cmul(scale, b)


def local_solve(root, f0, f1, w0, w1):
    _, half, nk, _ = f0.shape
    ny = 2 * half

    def row(refs, j, k):
        ref = refs[j // half]
        return ref[0, j % half, k, :], ref[1, j % half, k, :]

    def block(i, carry):
        k = pl.ds(pl.multiple_of(i * KB, KB), KB)
        rows = own_rows(root, i, KB)
        lam = root[0, rows, :], root[1, rows, :]
        gam = root[2, rows, :], root[3, rows, :]

        def put(j, value):
            ref = (w0, w1)[j // half]
            ref[0, j % half, k, :], ref[1, j % half, k, :] = value

        p = None
        for j in range(ny):
            f = row((f0, f1), j, k)
            p = f if p is None else cadd(cmul(lam, p), f)
            put(j, p)
        q = None
        for j in reversed(range(ny)):
            here = row((w0, w1), j, k)
            if q is None:
                q = row((f0, f1), j, k)
            else:
                q = cmul(lam, q)
                here = cadd(here, q)
                q = cadd(q, row((f0, f1), j, k))
            put(j, cmul(gam, here))
        return carry

    lax.fori_loop(0, nk // KB, block, 0)


def inverse_z(part, s_ref, root, w_ref, *refs):
    *fbs, send, keep, u = refs
    me = lax.axis_index("py")
    _, ny, nk, nz = w_ref.shape
    w = send.shape[3]

    def block(fb, base, i):
        k = pl.ds(pl.multiple_of((base + i) * KB, KB), KB)
        rows = own_rows(root, base + i, KB)
        lam = root[0, rows, :], root[1, rows, :]
        at = pl.ds(pl.multiple_of(i * KB, KB), KB)
        f = fb[0, at, :], fb[1, at, :]
        b = fb[2, at, :], fb[3, at, :]
        past = power(lam, ny)
        if part:
            f = cmul(past, f)
        else:
            b = cmul(past, b)
        for j in range(ny):
            f = cmul(lam, f)
            u[0, j], u[1, j] = cadd((w_ref[0, j, k, :], w_ref[1, j, k, :]), f)
        for j in reversed(range(ny)):
            b = cmul(lam, b)
            u[0, j], u[1, j] = cadd((u[0, j], u[1, j]), b)
        high, low = split(u[...].reshape(2 * ny * KB, nz))
        left = jnp.concatenate([high, low, high], axis=1)
        out = dot(left, stack(s_ref, 0))
        own, away = by_half(me, out[:, :w], out[:, w:])
        send[:, :, k, :] = away.reshape(2, ny, KB, w)
        keep[:, :, k, :] = own.reshape(2, ny, KB, w)

    over_blocks(block, nk, fbs)


def inverse_x(part, s_ref, keep, recv, src, speed, out, sums):
    me = lax.axis_index("py")
    _, nx, _, w = out.shape
    left = stack(s_ref, 1)
    for c in range(2):
        cols = []
        for y in range(YB):
            high, low = split(jnp.concatenate(by_half(me, keep[c, y], recv[c, y]), axis=0))
            cols.append(jnp.concatenate([high, low, high], axis=0))
        got = dot(left, jnp.concatenate(cols, axis=1))
        flat = out.at[c].reshape(nx * YB, w)
        for y in range(YB):
            flat[pl.ds(y, nx, stride=YB), :] = got[:, y * w : (y + 1) * w]
    here = pl.ds(part * YB, YB)
    damped = damping * wave_square

    def step(i, acc):
        s0, s1 = src[0, i, here, :], src[1, i, here, :]
        p0, p1 = out[0, i], out[1, i]
        c = speed[i, here, :]
        factor = wave_square - wave_square / (c * c)
        a0 = s0 + factor * p0 + damped * p1
        a1 = s1 + factor * p1 - damped * p0
        new = (
            s0 * s0 + s1 * s1,
            s0 * a0 + s1 * a1,
            s0 * a1 - s1 * a0,
            a0 * a0 + a1 * a1,
        )
        return tuple(x + y for x, y in zip(acc, new))

    zero = jnp.zeros((YB, w), f32)
    acc = lax.fori_loop(0, nx, step, (zero,) * 4, unroll=8)
    for i, a in enumerate(acc):
        sums[i : i + 1, :] = jnp.sum(a, axis=0, keepdims=True)


def finish(total, ps0, ps1, out_hbm, scaled, sems):
    sums = jnp.sum(jnp.sum(total[...], axis=0), axis=1, keepdims=True)
    square, re, im, size = (sums[i : i + 1] for i in range(4))
    beta2 = square + epsilon
    re, im, size = re / beta2, im / beta2, size / beta2
    den = size - (re * re + im * im) * (epsilon / beta2) + epsilon
    a, b = re / den, -im / den
    _, nx, _, w = ps0.shape
    a = jnp.broadcast_to(a, (YB, w))
    b = jnp.broadcast_to(b, (YB, w))
    copies = []
    for part, ps in enumerate((ps0, ps1)):
        for x in range(0, nx, XC):

            def step(i, carry, part=part, ps=ps):
                p0, p1 = ps[0, i], ps[1, i]
                scaled[part, 0, i] = a * p0 - b * p1
                scaled[part, 1, i] = a * p1 + b * p0
                return carry

            lax.fori_loop(x, x + XC, step, 0, unroll=8)
            copy = pltpu.make_async_copy(
                scaled.at[part, :, pl.ds(x, XC)],
                out_hbm.at[:, pl.ds(x, XC), pl.ds(part * YB, YB), :],
                sems.at[len(copies)],
            )
            copy.start()
            copies.append(copy)
    for copy in copies:
        copy.wait()


def params(mib, *dims):
    return pltpu.CompilerParams(dimension_semantics=dims or None, vmem_limit_bytes=mib * 2**20)


def whole(a):
    return pl.BlockSpec(a.shape, lambda *_: (0,) * a.ndim)


VM = pl.BlockSpec(memory_space=pltpu.VMEM)
ANY = pl.BlockSpec(memory_space=pl.ANY)


def cost(flops, moved):
    return pl.CostEstimate(flops=flops, bytes_accessed=moved, transcendentals=0)


def on_device(source, speed):
    _, nx, ny, w = source.shape
    cores, ring = lax.axis_size("py"), lax.axis_size("px")
    nz, nk = w * cores, nx // cores
    other = [(i, cores - 1 - i) for i in range(cores)]
    sds = lambda *shape: jax.ShapeDtypeStruct(shape, f32)

    table_x = jnp.asarray(np.stack(halves_of(sine_table(nx))))
    table_z = table_x if nz == nx else jnp.asarray(np.stack(halves_of(sine_table(nz))))
    root = jnp.asarray(root_tables(nx, nz))
    piece = sds(2, YB, nk, w)
    modes = sds(2, YB, nk, nz)
    flops = 2 * 2 * nx * YB * w * nx * 3
    est = cost(flops, 4 * 2**20)

    moved = []
    for h in range(2):
        send, keep = pl.pallas_call(
            functools.partial(forward_x, h),
            in_specs=[VM] * 2,
            out_specs=[VM] * 2,
            out_shape=[piece, piece],
            compiler_params=params(12),
            cost_estimate=est,
            name="forward_x",
        )(table_x, source)
        moved.append((keep, lax.ppermute(send, "py", other)))
    f, before = [], ()
    kc = nk // CHUNKS
    plane = sds(2, kc, nz)
    for h in range(2):
        got, pq, *sends = pl.pallas_call(
            functools.partial(forward_z, h == 0),
            in_specs=[VM] * (4 + len(before)),
            out_specs=[VM] * (2 + h * CHUNKS),
            out_shape=[modes, sds(4, nk, nz)] + [plane] * (h * CHUNKS),
            compiler_params=params(12),
            cost_estimate=est,
            name="forward_z",
        )(table_z, root, *moved[h], *before)
        f.append(got)
        before = (pq,)

    def small(body, n_in, out, name):
        return pl.pallas_call(
            body,
            in_specs=[VM] * n_in,
            out_specs=VM,
            out_shape=out,
            compiler_params=params(4),
            cost_estimate=cost(2 * 10**6, 2**19),
            name=name,
        )

    def mirrored(pairs):
        return pairs + [(ring - 1 - a, ring - 1 - b) for a, b in pairs]

    pair = mirrored([(i, i + 1) for i in range(0, ring, 2)])
    quad = mirrored([(i, i + 2) for i in range(1, ring, 4)])
    hops = [mirrored([(i, i + 4)]) for i in range(3, ring - 5, 4)]
    down = mirrored([(i, i + 2) for i in range(3, ring - 2, 4)])
    sums = [lax.ppermute(s, "px", pair) for s in sends]
    near = sums
    now = [small(functools.partial(fold_pair, c, ny), 3, plane, "fold")(root, pq, r) for c, r in enumerate(near)]
    for route, blocks in [(quad, 2)] + [(hop, 4) for hop in hops] + [(down, 2)]:
        sums = [lax.ppermute(s, "px", route) for s in now]
        now = [
            small(functools.partial(fold, c, blocks * ny), 3, plane, "fold")(root, s, r)
            for c, (s, r) in enumerate(zip(now, sums))
        ]
    two = [lax.ppermute(s, "px", mirrored([(i, i + 2) for i in range(1, ring - 2, 2)])) for s in now]
    one = [lax.ppermute(s, "px", mirrored([(i, i + 1) for i in range(1, ring - 2, 2)])) for s in now]
    fb = [
        small(functools.partial(carries, c, ny), 5, sds(4, kc, nz), "carries")(root, pq, near[c], one[c], two[c])
        for c in range(CHUNKS)
    ]
    local = pl.pallas_call(
        local_solve,
        in_specs=[VM] * 3,
        out_specs=[VM, VM],
        out_shape=[modes, modes],
        compiler_params=params(8),
        cost_estimate=cost(2 * flops, 8 * 2**20),
        name="local_solve",
    )(root, *f)
    moved = []
    for h in range(2):
        send, keep = pl.pallas_call(
            functools.partial(inverse_z, h),
            in_specs=[VM] * (3 + CHUNKS),
            out_specs=[VM, VM],
            out_shape=[piece, piece],
            scratch_shapes=[pltpu.VMEM((2, YB, KB, nz), f32)],
            compiler_params=params(12),
            cost_estimate=est,
            name="inverse_z",
        )(table_z, root, local[h], *fb)
        moved.append((keep, lax.ppermute(send, "py", other)))
    solved, sums = [], []
    for h in range(2):
        got, part = pl.pallas_call(
            functools.partial(inverse_x, h),
            in_specs=[VM] * 5,
            out_specs=[VM, VM],
            out_shape=[sds(2, nx, YB, w), sds(4, w)],
            compiler_params=params(16),
            cost_estimate=est,
            name="inverse_x",
        )(table_x, *moved[h], source, speed)
        solved.append(got)
        sums.append(part)
    sums = sums[0] + sums[1]
    sums = sums + lax.ppermute(sums, "py", other)
    every = lax.all_to_all(jnp.broadcast_to(sums[None], (ring, 4, w)), "px", 0, 0, tiled=True)
    return pl.pallas_call(
        finish,
        in_specs=[VM] * 3,
        out_specs=ANY,
        out_shape=sds(*source.shape),
        scratch_shapes=[pltpu.VMEM((2, 2, nx, YB, w), f32), pltpu.SemaphoreType.DMA((2 * nx // XC,))],
        compiler_params=params(16),
        cost_estimate=cost(10**7, 8 * 2**20),
        name="finish",
    )(every, *solved)


def solution(mesh):
    return jax.shard_map(
        on_device,
        mesh=mesh,
        in_specs=(P(None, "samples", "px", "py"), P("samples", "px", "py")),
        out_specs=P(None, "samples", "px", "py"),
        check_vma=False,
    )
```

time: 133 us -> 112 us (0.84)
  blocking collectives: 64.6 us -> 19.9 us
  waiting for transfers between devices: 22.7 us -> 51.6 us
  local copies, waits for them, and re-layouts: 15 us -> 3.17 us
  starting transfers between devices: 8.28 us -> 15 us
    ppermute x0 -> x14, waiting for transfers between devices: none -> 50.2 us  [the longest x2 38.5 us: on_device(): lax.ppermute(s, 'px', mirrored([(i, i + 2) for i in range(1, ring - 2, 2)]))]
    all_to_all x1 -> x0, blocking collectives: 45.8 us -> none  [on_device(): pq = lax.all_to_all(pq, 'px', 0, 0, tiled=True)]
    all_to_all x1 -> x0, waiting for transfers between devices: 21.2 us -> none  [on_device(): fb = lax.all_to_all(fb, 'px', 0, 0, tiled=True)]
    ppermute x0 -> x14, starting transfers between devices: none -> 13 us  [the longest x8 6.63 us: on_device(): sums = [lax.ppermute(s, 'px', route) for s in now]]
    unnamed x32 -> x12, local copies, waits for them, and re-layouts: 15 us -> 3.16 us
    all_to_all x1 -> x0, starting transfers between devices: 6.68 us -> none  [on_device(): fb = lax.all_to_all(fb, 'px', 0, 0, tiled=True)]
    pallas_call x7 -> x18, Pallas kernels: 13.1 us -> 13.3 us  [the longest x2 4.71 us: on_device(): pl.pallas_call(functools.partial(inverse_x, h), in_specs=[VM] * 5, out_sp...]
  transfers between devices with their start and end apart: 6 -> 19, of which waited for: 3 -> 9; matrix products, arithmetic and copies ran while one was open for 0% -> 0% of each run, Pallas kernels for 8% -> 10%
where the time goes in v3:
time: 112 us
  waiting for transfers between devices  51.6 us (46%)
  Pallas kernels  21.6 us (19%)
  blocking collectives  19.9 us (18%)
  starting transfers between devices  15 us (13%)
  local copies, waits for them, and re-layouts  3.17 us (3%)
    ppermute x2, waiting for transfers between devices, on_device(): lax.ppermute(s, 'px', mirrored([(i, i + 2) for i in range(1, ring - 2, 2)]))  38.5 us
    all_to_all x1, blocking collectives, on_device(): lax.all_to_all(jnp.broadcast_to(sums[None], (ring, 4, w)), 'px', 0, 0, ti...  19.9 us
    ppermute x8, starting transfers between devices, on_device(): sums = [lax.ppermute(s, 'px', route) for s in now]  6.63 us
    ppermute x8, waiting for transfers between devices, on_device(): sums = [lax.ppermute(s, 'px', route) for s in now]  6.36 us
    ppermute x2, waiting for transfers between devices, on_device(): sums = [lax.ppermute(s, 'px', pair) for s in sends]  5.33 us
    pallas_call x2, Pallas kernels, on_device(): pl.pallas_call(functools.partial(inverse_x, h), in_specs=[VM] * 5, out_sp...  4.71 us
    pallas_call x2, Pallas kernels, on_device(): pl.pallas_call(functools.partial(forward_z, h == 0), in_specs=[VM] * (4 +...  4.1 us
    pallas_call x2, Pallas kernels, on_device(): pl.pallas_call(functools.partial(inverse_z, h), in_specs=[VM] * (3 + CHUN...  3.7 us
  transfers between devices with their start and end apart: 19, of which 9 were waited for; matrix products, arithmetic and copies ran while one was open for 0% of the time, Pallas kernels for 10%

profile of v3, /device:TPU:86, one launch (start us, length us, event | category | flops | bytes accessed | tf_op | source)
XLA Modules:
  0.0 111.7 jit_solution(8333691431100400183)
XLA Ops:
  0.0 2.2 %copy-done.1 = f32[2,256,16,128]{3,2,1,0:T(8,128)S(1)} copy-done((f32[2,256,16,128]{3,2,1,0:T(8,128)S(1)}, f32[2,256,16,128]{3,2,1,0:T(8,128)}, u32[]{:S(2)}) %copy-start.1) | copy-done | bytes 4194328
  2.2 0.9 copy-done.3
  3.1 1.6 %forward_x.2 = (f32[2,8,128,128]{3,2,1,0:T(8,128)S(1)}, f32[2,8,128,128]{3,2,1,0:T(8,128)S(1)}) custom-call(bf16[2,256,256]{2,1,0:T(8,128)(2,1)S(1)} %copy-done.3, f32[2,256,16,128]{3,2,1,0:T(8,128)S(1)} %copy-done.1), custom_call_target="tpu_custom_call" | custom-call | flops 805306368 | bytes 4194304 | tf_op jit(solution)/shard_map/forward_x/pallas_call | solution.py:398
  4.8 0.0 copy-start
  4.8 0.1 collective-permute-start
  4.9 1.6 %forward_x.3 = (f32[2,8,128,128]{3,2,1,0:T(8,128)S(1)}, f32[2,8,128,128]{3,2,1,0:T(8,128)S(1)}) custom-call(bf16[2,256,256]{2,1,0:T(8,128)(2,1)S(1)} %copy-done.3, f32[2,256,16,128]{3,2,1,0:T(8,128)S(1)} %copy-done.1), custom_call_target="tpu_custom_call" | custom-call | flops 805306368 | bytes 4194304 | tf_op jit(solution)/shard_map/forward_x/pallas_call | solution.py:398
  6.5 0.6 collective-permute-start.1
  7.1 0.4 collective-permute-done.refs_1_
  7.5 1.8 %forward_z.2 = (f32[2,8,128,256]{3,2,1,0:T(8,128)S(1)}, f32[4,128,256]{2,1,0:T(8,128)S(1)}) custom-call(bf16[2,256,256]{2,1,0:T(8,128)(2,1)S(1)} %copy-done.3, f32[4,256,256]{2,1,0:T(8,128)S(1)} %copy-done, f32[2,8,128,128]{3,2,1,0:T(8,128)S(1)} %get-tuple-element.25.refs_0_, f32[2,8,128,128]{3,2,1,0:T(8,128)S(1)} %collective-permute-done.refs_1_), custom_call_target="tpu_custom_call" | custom-call | flops 805306368 | bytes 4194304 | tf_op jit(solution)/shard_map/forward_z/pallas_call | solution.py:412
  9.3 0.1 collective-permute-done.1.refs_1_
  9.4 2.3 %forward_z.3 = (f32[2,8,128,256]{3,2,1,0:T(8,128)S(1)}, f32[4,128,256]{2,1,0:T(8,128)S(1)}, f32[2,64,256]{2,1,0:T(8,128)S(1)}, f32[2,64,256]{2,1,0:T(8,128)S(1)}) custom-call(bf16[2,256,256]{2,1,0:T(8,128)(2,1)S(1)} %copy-done.3, f32[4,256,256]{2,1,0:T(8,128)S(1)} %copy-done, f32[2,8,128,128]{3,2,1,0:T(8,128)S(1)} %get-tuple-element.28.refs_0_, ...), custom_call_target="tpu_custom_call" | custom-call | flops 805306368 | bytes 4194304 | tf_op jit(solution)/shard_map/forward_z/pallas_call | solution.py:412
  11.7 2.2 %collective-permute-start.9 = (f32[2,64,256]{2,1,0:T(8,128)S(1)}, f32[2,64,256]{2,1,0:T(8,128)S(1)}, u32[]{:S(2)}, u32[]{:S(2)}) collective-permute-start(f32[2,64,256]{2,1,0:T(8,128)S(1)} %get-tuple-element.35), channel_id=1, source_target_pairs={{0,2},{4,6},{8,10},{12,14},{16,18},{20,22},{24,26},{28,30},{30,28}... | collective-permute-start | bytes 393224 | tf_op jit(solution)/shard_map/ppermute | solution.py:442
  14.0 0.1 collective-permute-start.2
  14.1 4.2 %collective-permute-done.9.recv.near = f32[2,64,256]{2,1,0:T(8,128)S(1)} collective-permute-done((f32[2,64,256]{2,1,0:T(8,128)S(1)}, f32[2,64,256]{2,1,0:T(8,128)S(1)}, u32[]{:S(2)}, u32[]{:S(2)}) %collective-permute-start.9) | collective-permute-done | bytes 131104 | tf_op jit(solution)/shard_map/ppermute | solution.py:442
  18.3 0.1 fold.15.now
  18.4 1.3 %collective-permute-start.10 = (f32[2,64,256]{2,1,0:T(8,128)S(1)}, f32[2,64,256]{2,1,0:T(8,128)S(1)}, u32[]{:S(2)}, u32[]{:S(2)}) collective-permute-start(f32[2,64,256]{2,1,0:T(8,128)S(1)} %fold.15.now), channel_id=1, source_target_pairs={{2,6},{10,14},{18,22},{26,30},{28,24},{20,16},{12,8},{4,0},{3,7},{... | collective-permute-start | bytes 393224 | tf_op jit(solution)/shard_map/ppermute | solution.py:446
  19.7 1.1 collective-permute-done.2.recv.near
  20.8 0.1 fold.10.now
  20.9 1.3 %collective-permute-start.3 = (f32[2,64,256]{2,1,0:T(8,128)S(1)}, f32[2,64,256]{2,1,0:T(8,128)S(1)}, u32[]{:S(2)}, u32[]{:S(2)}) collective-permute-start(f32[2,64,256]{2,1,0:T(8,128)S(1)} %fold.10.now), channel_id=1, source_target_pairs={{2,6},{10,14},{18,22},{26,30},{28,24},{20,16},{12,8},{4,0},{3,7},{... | collective-permute-start | bytes 393224 | tf_op jit(solution)/shard_map/ppermute | solution.py:446
  22.2 4.3 %collective-permute-done.10.recv = f32[2,64,256]{2,1,0:T(8,128)S(1)} collective-permute-done((f32[2,64,256]{2,1,0:T(8,128)S(1)}, f32[2,64,256]{2,1,0:T(8,128)S(1)}, u32[]{:S(2)}, u32[]{:S(2)}) %collective-permute-start.10) | collective-permute-done | bytes 131104 | tf_op jit(solution)/shard_map/ppermute | solution.py:446
  26.5 0.1 fold.16.now
  26.6 0.7 collective-permute-start.11
  27.3 2.1 %collective-permute-done.3.recv = f32[2,64,256]{2,1,0:T(8,128)S(1)} collective-permute-done((f32[2,64,256]{2,1,0:T(8,128)S(1)}, f32[2,64,256]{2,1,0:T(8,128)S(1)}, u32[]{:S(2)}, u32[]{:S(2)}) %collective-permute-start.3) | collective-permute-done | bytes 131104 | tf_op jit(solution)/shard_map/ppermute | solution.py:446
  29.3 0.1 fold.11.now
  29.4 0.7 collective-permute-start.4
  30.1 0.0 collective-permute-done.11.recv
  30.1 0.1 fold.17.now
  30.2 0.7 collective-permute-start.12
  30.9 0.0 collective-permute-done.4.recv
  30.9 0.1 fold.12.now
  31.0 0.7 collective-permute-start.5
  31.7 0.0 collective-permute-done.12.recv
  31.7 0.1 fold.18.now
  31.8 0.7 collective-permute-start.13
  32.4 0.0 collective-permute-done.5.recv
  32.5 0.1 fold.13.now
  32.6 0.7 collective-permute-start.6
  33.2 0.0 collective-permute-done.13.recv
  33.2 0.1 fold.19
  33.3 0.7 collective-permute-start.14
  34.0 1.3 %collective-permute-start.15 = (f32[2,64,256]{2,1,0:T(8,128)S(1)}, f32[2,64,256]{2,1,0:T(8,128)S(1)}, u32[]{:S(2)}, u32[]{:S(2)}) collective-permute-start(f32[2,64,256]{2,1,0:T(8,128)S(1)} %fold.19), channel_id=1, source_target_pairs={{2,6},{6,10},{10,14},{14,18},{18,22},{22,26},{26,30},{28,24},{24,2... | collective-permute-start | bytes 393224 | tf_op jit(solution)/shard_map/ppermute | solution.py:451
  35.3 0.0 collective-permute-done.6.recv
  35.3 0.1 fold.14
  35.4 0.7 collective-permute-start.7
  36.1 1.3 %collective-permute-start.8 = (f32[2,64,256]{2,1,0:T(8,128)S(1)}, f32[2,64,256]{2,1,0:T(8,128)S(1)}, u32[]{:S(2)}, u32[]{:S(2)}) collective-permute-start(f32[2,64,256]{2,1,0:T(8,128)S(1)} %fold.14), channel_id=1, source_target_pairs={{2,6},{6,10},{10,14},{14,18},{18,22},{22,26},{26,30},{28,24},{24,2... | collective-permute-start | bytes 393224 | tf_op jit(solution)/shard_map/ppermute | solution.py:451
  37.4 1.9 %local_solve.1 = (f32[2,8,128,256]{3,2,1,0:T(8,128)S(1)}, f32[2,8,128,256]{3,2,1,0:T(8,128)S(1)}) custom-call(f32[4,256,256]{2,1,0:T(8,128)S(1)} %copy-done, f32[2,8,128,256]{3,2,1,0:T(8,128)S(1)} %get-tuple-element.27.f0, f32[2,8,128,256]{3,2,1,0:T(8,128)S(1)} %get-tuple-element.31.f1), custom_call_target="tpu_custom_call" | custom-call | flops 1610612736 | bytes 8388608 | tf_op jit(solution)/shard_map/local_solve/pallas_call | solution.py:457
  39.3 0.0 copy-start.4
  39.3 34.7 %collective-permute-done.15.two = f32[2,64,256]{2,1,0:T(8,128)S(1)} collective-permute-done((f32[2,64,256]{2,1,0:T(8,128)S(1)}, f32[2,64,256]{2,1,0:T(8,128)S(1)}, u32[]{:S(2)}, u32[]{:S(2)}) %collective-permute-start.15) | collective-permute-done | bytes 131104 | tf_op jit(solution)/shard_map/ppermute | solution.py:451
  74.1 0.4 carries.3.refs_1_
  74.5 3.7 %collective-permute-done.8.two = f32[2,64,256]{2,1,0:T(8,128)S(1)} collective-permute-done((f32[2,64,256]{2,1,0:T(8,128)S(1)}, f32[2,64,256]{2,1,0:T(8,128)S(1)}, u32[]{:S(2)}, u32[]{:S(2)}) %collective-permute-start.8) | collective-permute-done | bytes 131104 | tf_op jit(solution)/shard_map/ppermute | solution.py:451
  78.2 0.4 carries.2.refs_0_
  78.7 0.0 copy-start.2
  78.7 1.8 %inverse_z.3 = (f32[2,8,128,128]{3,2,1,0:T(8,128)S(1)}, f32[2,8,128,128]{3,2,1,0:T(8,128)S(1)}) custom-call(bf16[2,256,256]{2,1,0:T(8,128)(2,1)S(1)} %copy-done.4, f32[4,256,256]{2,1,0:T(8,128)S(1)} %copy-done, f32[2,8,128,256]{3,2,1,0:T(8,128)S(1)} %get-tuple-element.39.w_ref, f32[4,64,256]{2,1,0:T(8,128)S(1)} %carries.2.refs_0_, ...), custom_call_target="tpu_custom_call" | custom-call | flops 805306368 | bytes 4194304 | tf_op jit(solution)/shard_map/inverse_z/pallas_call | solution.py:468
  80.5 0.0 copy-start.5
  80.5 0.1 collective-permute-start.17
  80.7 1.8 %inverse_z.2 = (f32[2,8,128,128]{3,2,1,0:T(8,128)S(1)}, f32[2,8,128,128]{3,2,1,0:T(8,128)S(1)}) custom-call(bf16[2,256,256]{2,1,0:T(8,128)(2,1)S(1)} %copy-done.4, f32[4,256,256]{2,1,0:T(8,128)S(1)} %copy-done, f32[2,8,128,256]{3,2,1,0:T(8,128)S(1)} %get-tuple-element.32.w_ref, f32[4,64,256]{2,1,0:T(8,128)S(1)} %carries.2.refs_0_, ...), custom_call_target="tpu_custom_call" | custom-call | flops 805306368 | bytes 4194304 | tf_op jit(solution)/shard_map/inverse_z/pallas_call | solution.py:468
  82.5 0.8 collective-permute-start.16
  83.3 0.0 collective-permute-done.17.recv
  83.3 2.3 %inverse_x.3 = (f32[2,256,8,128]{3,2,1,0:T(8,128)S(1)}, f32[4,128]{1,0:T(4,128)S(1)}) custom-call(bf16[2,256,256]{2,1,0:T(8,128)(2,1)S(1)} %copy-done.4, f32[2,8,128,128]{3,2,1,0:T(8,128)S(1)} %get-tuple-element.40.keep, f32[2,8,128,128]{3,2,1,0:T(8,128)S(1)} %collective-permute-done.17.recv, f32[2,256,16,128]{3,2,1,0:T(8,128)S(1)} %copy-done.2, ...), custom_call_target="tpu_custom_call" | custom-call | flops 805306368 | bytes 4194304 | tf_op jit(solution)/shard_map/inverse_x/pallas_call | solution.py:481
  85.7 2.4 %inverse_x.2 = (f32[2,256,8,128]{3,2,1,0:T(8,128)S(1)}, f32[4,128]{1,0:T(4,128)S(1)}) custom-call(bf16[2,256,256]{2,1,0:T(8,128)(2,1)S(1)} %copy-done.4, f32[2,8,128,128]{3,2,1,0:T(8,128)S(1)} %get-tuple-element.36.keep, f32[2,8,128,128]{3,2,1,0:T(8,128)S(1)} %collective-permute-done.16.recv, f32[2,256,16,128]{3,2,1,0:T(8,128)S(1)} %copy-done.2, ...), custom_call_target="tpu_custom_call" | custom-call | flops 805306368 | bytes 4194304 | tf_op jit(solution)/shard_map/inverse_x/pallas_call | solution.py:481
  88.1 0.4 collective-permute-start.18
  88.5 0.9 collective-permute-done.18
  89.4 19.9 %all_to_all.5.total = f32[16,4,128]{2,1,0:T(4,128)S(1)} all-to-all(f32[16,4,128]{2,1,0:T(4,128)S(1)} %broadcast_in_dim.2), channel_id=1, replica_groups=mesh['samples'=4,'px'=16,'py'=2] {'px'}, dimensions={0} | all-to-all | bytes 65536 | tf_op jit(solution)/shard_map/all_to_all | solution.py:494
  109.3 2.3 %finish.1 = f32[2,256,16,128]{3,2,1,0:T(8,128)} custom-call(f32[16,4,128]{2,1,0:T(4,128)S(1)} %all_to_all.5.total, f32[2,256,8,128]{3,2,1,0:T(8,128)S(1)} %get-tuple-element.43.ps0, f32[2,256,8,128]{3,2,1,0:T(8,128)S(1)} %get-tuple-element.44.ps1), custom_call_target="tpu_custom_call" | custom-call | flops 10000000 | bytes 8388608 | tf_op jit(solution)/shard_map/finish/pallas_call | solution.py:495
  (12 shorter events, 0.0 us)
Async XLA Ops:
  0.0 2.2 %copy-start.1 = (f32[2,256,16,128]{3,2,1,0:T(8,128)S(1)}, f32[2,256,16,128]{3,2,1,0:T(8,128)}, u32[]{:S(2)}) copy-start(f32[2,256,16,128]{3,2,1,0:T(8,128)} %src.7) | copy-start | bytes 12582916
  2.2 0.9 copy-start.3
  4.8 2.8 %copy-start = (f32[4,256,256]{2,1,0:T(8,128)S(1)}, f32[4,256,256]{2,1,0:T(8,128)}, u32[]{:S(2)}) copy-start(f32[4,256,256]{2,1,0:T(8,128)} %constant.5.clone.root) | copy-start | bytes 3145732
  4.8 2.8 %collective-permute-start = (f32[2,8,128,128]{3,2,1,0:T(8,128)S(1)}, f32[2,8,128,128]{3,2,1,0:T(8,128)S(1)}, u32[]{:S(2)}, u32[]{:S(2)}) collective-permute-start(f32[2,8,128,128]{3,2,1,0:T(8,128)S(1)} %get-tuple-element.26), channel_id=1, source_target_pairs={{0,1},{1,0},{2,3},{3,2},{4,5},{5,4},{6,7},{7,6},{8,9},{9,8},{10,11... | collective-permute-start | bytes 3145736 | tf_op jit(solution)/shard_map/ppermute | solution.py:407
  6.5 2.9 %collective-permute-start.1 = (f32[2,8,128,128]{3,2,1,0:T(8,128)S(1)}, f32[2,8,128,128]{3,2,1,0:T(8,128)S(1)}, u32[]{:S(2)}, u32[]{:S(2)}) collective-permute-start(f32[2,8,128,128]{3,2,1,0:T(8,128)S(1)} %get-tuple-element.29), channel_id=1, source_target_pairs={{0,1},{1,0},{2,3},{3,2},{4,5},{5,4},{6,7},{7,6},{8,9},{9,8},{10,11... | collective-permute-start | bytes 3145736 | tf_op jit(solution)/shard_map/ppermute | solution.py:407
  11.7 6.6 %collective-permute-start.9 = (f32[2,64,256]{2,1,0:T(8,128)S(1)}, f32[2,64,256]{2,1,0:T(8,128)S(1)}, u32[]{:S(2)}, u32[]{:S(2)}) collective-permute-start(f32[2,64,256]{2,1,0:T(8,128)S(1)} %get-tuple-element.35), channel_id=1, source_target_pairs={{0,2},{4,6},{8,10},{12,14},{16,18},{20,22},{24,26},{28,30},{30,28}... | collective-permute-start | bytes 393224 | tf_op jit(solution)/shard_map/ppermute | solution.py:442
  14.0 6.9 %collective-permute-start.2 = (f32[2,64,256]{2,1,0:T(8,128)S(1)}, f32[2,64,256]{2,1,0:T(8,128)S(1)}, u32[]{:S(2)}, u32[]{:S(2)}) collective-permute-start(f32[2,64,256]{2,1,0:T(8,128)S(1)} %get-tuple-element.34), channel_id=1, source_target_pairs={{0,2},{4,6},{8,10},{12,14},{16,18},{20,22},{24,26},{28,30},{30,28}... | collective-permute-start | bytes 393224 | tf_op jit(solution)/shard_map/ppermute | solution.py:442
  18.4 8.1 %collective-permute-start.10 = (f32[2,64,256]{2,1,0:T(8,128)S(1)}, f32[2,64,256]{2,1,0:T(8,128)S(1)}, u32[]{:S(2)}, u32[]{:S(2)}) collective-permute-start(f32[2,64,256]{2,1,0:T(8,128)S(1)} %fold.15.now), channel_id=1, source_target_pairs={{2,6},{10,14},{18,22},{26,30},{28,24},{20,16},{12,8},{4,0},{3,7},{... | collective-permute-start | bytes 393224 | tf_op jit(solution)/shard_map/ppermute | solution.py:446
  20.9 8.4 %collective-permute-start.3 = (f32[2,64,256]{2,1,0:T(8,128)S(1)}, f32[2,64,256]{2,1,0:T(8,128)S(1)}, u32[]{:S(2)}, u32[]{:S(2)}) collective-permute-start(f32[2,64,256]{2,1,0:T(8,128)S(1)} %fold.10.now), channel_id=1, source_target_pairs={{2,6},{10,14},{18,22},{26,30},{28,24},{20,16},{12,8},{4,0},{3,7},{... | collective-permute-start | bytes 393224 | tf_op jit(solution)/shard_map/ppermute | solution.py:446
  26.6 3.5 %collective-permute-start.11 = (f32[2,64,256]{2,1,0:T(8,128)S(1)}, f32[2,64,256]{2,1,0:T(8,128)S(1)}, u32[]{:S(2)}, u32[]{:S(2)}) collective-permute-start(f32[2,64,256]{2,1,0:T(8,128)S(1)} %fold.16.now), channel_id=1, source_target_pairs={{6,14},{24,16},{7,15},{25,17},{38,46},{56,48},{39,47},{57,49},{70,... | collective-permute-start | bytes 393224 | tf_op jit(solution)/shard_map/ppermute | solution.py:446
  29.4 1.5 %collective-permute-start.4 = (f32[2,64,256]{2,1,0:T(8,128)S(1)}, f32[2,64,256]{2,1,0:T(8,128)S(1)}, u32[]{:S(2)}, u32[]{:S(2)}) collective-permute-start(f32[2,64,256]{2,1,0:T(8,128)S(1)} %fold.11.now), channel_id=1, source_target_pairs={{6,14},{24,16},{7,15},{25,17},{38,46},{56,48},{39,47},{57,49},{70,... | collective-permute-start | bytes 393224 | tf_op jit(solution)/shard_map/ppermute | solution.py:446
  30.2 1.5 %collective-permute-start.12 = (f32[2,64,256]{2,1,0:T(8,128)S(1)}, f32[2,64,256]{2,1,0:T(8,128)S(1)}, u32[]{:S(2)}, u32[]{:S(2)}) collective-permute-start(f32[2,64,256]{2,1,0:T(8,128)S(1)} %fold.17.now), channel_id=1, source_target_pairs={{14,22},{16,8},{15,23},{17,9},{46,54},{48,40},{47,55},{49,41},{78,... | collective-permute-start | bytes 393224 | tf_op jit(solution)/shard_map/ppermute | solution.py:446
  31.0 1.5 %collective-permute-start.5 = (f32[2,64,256]{2,1,0:T(8,128)S(1)}, f32[2,64,256]{2,1,0:T(8,128)S(1)}, u32[]{:S(2)}, u32[]{:S(2)}) collective-permute-start(f32[2,64,256]{2,1,0:T(8,128)S(1)} %fold.12.now), channel_id=1, source_target_pairs={{14,22},{16,8},{15,23},{17,9},{46,54},{48,40},{47,55},{49,41},{78,... | collective-permute-start | bytes 393224 | tf_op jit(solution)/shard_map/ppermute | solution.py:446
  31.8 1.5 %collective-permute-start.13 = (f32[2,64,256]{2,1,0:T(8,128)S(1)}, f32[2,64,256]{2,1,0:T(8,128)S(1)}, u32[]{:S(2)}, u32[]{:S(2)}) collective-permute-start(f32[2,64,256]{2,1,0:T(8,128)S(1)} %fold.18.now), channel_id=1, source_target_pairs={{6,10},{14,18},{22,26},{24,20},{16,12},{8,4},{7,11},{15,19},{23,27... | collective-permute-start | bytes 393224 | tf_op jit(solution)/shard_map/ppermute | solution.py:446
  32.6 2.8 %collective-permute-start.6 = (f32[2,64,256]{2,1,0:T(8,128)S(1)}, f32[2,64,256]{2,1,0:T(8,128)S(1)}, u32[]{:S(2)}, u32[]{:S(2)}) collective-permute-start(f32[2,64,256]{2,1,0:T(8,128)S(1)} %fold.13.now), channel_id=1, source_target_pairs={{6,10},{14,18},{22,26},{24,20},{16,12},{8,4},{7,11},{15,19},{23,27... | collective-permute-start | bytes 393224 | tf_op jit(solution)/shard_map/ppermute | solution.py:446
  33.3 6.0 %collective-permute-start.14 = (f32[2,64,256]{2,1,0:T(8,128)S(1)}, f32[2,64,256]{2,1,0:T(8,128)S(1)}, u32[]{:S(2)}, u32[]{:S(2)}) collective-permute-start(f32[2,64,256]{2,1,0:T(8,128)S(1)} %fold.19), channel_id=1, source_target_pairs={{2,4},{6,8},{10,12},{14,16},{18,20},{22,24},{26,28},{28,26},{24,22... | collective-permute-start | bytes 393224 | tf_op jit(solution)/shard_map/ppermute | solution.py:452
  34.0 40.1 %collective-permute-start.15 = (f32[2,64,256]{2,1,0:T(8,128)S(1)}, f32[2,64,256]{2,1,0:T(8,128)S(1)}, u32[]{:S(2)}, u32[]{:S(2)}) collective-permute-start(f32[2,64,256]{2,1,0:T(8,128)S(1)} %fold.19), channel_id=1, source_target_pairs={{2,6},{6,10},{10,14},{14,18},{18,22},{22,26},{26,30},{28,24},{24,2... | collective-permute-start | bytes 393224 | tf_op jit(solution)/shard_map/ppermute | solution.py:451
  35.4 39.1 %collective-permute-start.7 = (f32[2,64,256]{2,1,0:T(8,128)S(1)}, f32[2,64,256]{2,1,0:T(8,128)S(1)}, u32[]{:S(2)}, u32[]{:S(2)}) collective-permute-start(f32[2,64,256]{2,1,0:T(8,128)S(1)} %fold.14), channel_id=1, source_target_pairs={{2,4},{6,8},{10,12},{14,16},{18,20},{22,24},{26,28},{28,26},{24,22... | collective-permute-start | bytes 393224 | tf_op jit(solution)/shard_map/ppermute | solution.py:452
  36.1 42.1 %collective-permute-start.8 = (f32[2,64,256]{2,1,0:T(8,128)S(1)}, f32[2,64,256]{2,1,0:T(8,128)S(1)}, u32[]{:S(2)}, u32[]{:S(2)}) collective-permute-start(f32[2,64,256]{2,1,0:T(8,128)S(1)} %fold.14), channel_id=1, source_target_pairs={{2,6},{6,10},{10,14},{14,18},{18,22},{22,26},{26,30},{28,24},{24,2... | collective-permute-start | bytes 393224 | tf_op jit(solution)/shard_map/ppermute | solution.py:451
  39.3 39.4 %copy-start.4 = (bf16[2,256,256]{2,1,0:T(8,128)(2,1)S(1)}, bf16[2,256,256]{2,1,0:T(8,128)(2,1)}, u32[]{:S(2)}) copy-start(bf16[2,256,256]{2,1,0:T(8,128)(2,1)} %constant.4.clone.s_ref) | copy-start | bytes 786436
  78.7 4.7 %copy-start.2 = (f32[2,256,16,128]{3,2,1,0:T(8,128)S(1)}, f32[2,256,16,128]{3,2,1,0:T(8,128)}, u32[]{:S(2)}) copy-start(f32[2,256,16,128]{3,2,1,0:T(8,128)} %src.7) | copy-start | bytes 12582916
  80.5 2.8 %copy-start.5 = (f32[256,16,128]{2,1,0:T(8,128)S(1)}, f32[256,16,128]{2,1,0:T(8,128)}, u32[]{:S(2)}) copy-start(f32[256,16,128]{2,1,0:T(8,128)} %speed.3) | copy-start | bytes 6291460
  80.5 2.8 %collective-permute-start.17 = (f32[2,8,128,128]{3,2,1,0:T(8,128)S(1)}, f32[2,8,128,128]{3,2,1,0:T(8,128)S(1)}, u32[]{:S(2)}, u32[]{:S(2)}) collective-permute-start(f32[2,8,128,128]{3,2,1,0:T(8,128)S(1)} %get-tuple-element.41), channel_id=1, source_target_pairs={{0,1},{1,0},{2,3},{3,2},{4,5},{5,4},{6,7},{7,6},{8,9},{9,8},{10,11... | collective-permute-start | bytes 3145736 | tf_op jit(solution)/shard_map/ppermute | solution.py:478
  82.5 3.1 %collective-permute-start.16 = (f32[2,8,128,128]{3,2,1,0:T(8,128)S(1)}, f32[2,8,128,128]{3,2,1,0:T(8,128)S(1)}, u32[]{:S(2)}, u32[]{:S(2)}) collective-permute-start(f32[2,8,128,128]{3,2,1,0:T(8,128)S(1)} %get-tuple-element.37), channel_id=1, source_target_pairs={{0,1},{1,0},{2,3},{3,2},{4,5},{5,4},{6,7},{7,6},{8,9},{9,8},{10,11... | collective-permute-start | bytes 3145736 | tf_op jit(solution)/shard_map/ppermute | solution.py:478
  88.1 1.3 %collective-permute-start.18 = (f32[4,128]{1,0:T(4,128)S(1)}, f32[4,128]{1,0:T(4,128)S(1)}, u32[]{:S(2)}, u32[]{:S(2)}) collective-permute-start(f32[4,128]{1,0:T(4,128)S(1)} %add.6), channel_id=1, source_target_pairs={{0,1},{1,0},{2,3},{3,2},{4,5},{5,4},{6,7},{7,6},{8,9},{9,8},{10,11... | collective-permute-start | bytes 6152 | tf_op jit(solution)/shard_map/ppermute | solution.py:493

commit v4 on v3

--- a/solution.py
+++ b/solution.py
@@ -105,25 +105,26 @@
     return result
 
 
-def forward_z(first, s_ref, root, *refs):
+def forward_z(chunk, first, s_ref, root, keep, recv, *refs):
     if first:
-        keep, recv, f_out, pq = refs
+        f_out, pq = refs
     else:
-        keep, recv, before, f_out, pq, *sends = refs
+        before, f_out, pq, send = refs
     me = lax.axis_index("py")
     ring, place = lax.axis_size("px"), lax.axis_index("px")
-    _, ny, nk, w = keep.shape
-    nz = f_out.shape[3]
-
-    def block(send, base, i):
-        k = pl.ds(pl.multiple_of((base + i) * KB, KB), KB)
+    _, ny, _, w = keep.shape
+    _, _, kc, nz = f_out.shape
+
+    def block(i, carry):
+        k = pl.ds(pl.multiple_of(i * KB, KB), KB)
+        here = pl.ds(pl.multiple_of(chunk * kc + i * KB, KB), KB)
         shape = 2 * ny * KB, w
-        both = by_half(me, keep[:, :, k, :].reshape(shape), recv[:, :, k, :].reshape(shape))
+        both = by_half(me, keep[:, :, here, :].reshape(shape), recv[:, :, here, :].reshape(shape))
         high, low = split(jnp.concatenate(both, axis=1))
         total = dot(jnp.concatenate([high, low, high], axis=1), stack(s_ref, 0))
         total = total.reshape(2, ny, KB, nz)
         f_out[:, :, k, :] = total
-        rows = own_rows(root, base + i, KB)
+        rows = own_rows(root, chunk * (kc // KB) + i, KB)
         lam = root[0, rows, :], root[1, rows, :]
         row = [(total[0, j], total[1, j]) for j in range(ny)]
         p = row[0] if first else cadd(cmul(lam, (before[0, k, :], before[1, k, :])), row[0])
@@ -141,24 +142,13 @@
                 csub(q, cmul(cmul(right, edge), p)),
             )
             even = place % 2 == 0
-            to = pl.ds(pl.multiple_of(i * KB, KB), KB)
             for c in range(2):
-                send[c, to, :] = jnp.where(even, p[c], q[c])
+                send[c, k, :] = jnp.where(even, p[c], q[c])
         for c, part in enumerate((*p, *q)):
             pq[c, k, :] = part
-
-    over_blocks(block, nk, (None,) if first else sends)
-
-
-def over_blocks(block, nk, refs):
-    number = nk // KB // len(refs)
-    for c, ref in enumerate(refs):
-
-        def step(i, carry, c=c, ref=ref):
-            block(ref, c * number, i)
-            return carry
-
-        lax.fori_loop(0, number, step, 0)
+        return carry
+
+    lax.fori_loop(0, kc // KB, block, 0)
 
 
 def csub(a, b):
@@ -178,27 +168,29 @@
     return found
 
 
-def fold(chunk, exponent, root, now, recv, out):
+def fold(chunk, exponents, root, now, *refs):
+    *recv, out = refs
+    kc = out.shape[1]
+    rows = own_rows(root, chunk, kc)
+    total = now[0], now[1]
+    for exponent, r in zip(exponents, recv):
+        far = power((root[0, rows, :], root[1, rows, :]), exponent)
+        total = cadd(total, cmul(far, (r[0], r[1])))
+    out[0], out[1] = total
+
+
+def fold_pair(chunk, exponent, root, pq, recv, out):
     kc = out.shape[1]
     rows = own_rows(root, chunk, kc)
     far = power((root[0, rows, :], root[1, rows, :]), exponent)
-    out[0], out[1] = cadd((now[0], now[1]), cmul(far, (recv[0], recv[1])))
-
-
-def fold_pair(chunk, exponent, root, pq, recv, out):
-    kc = out.shape[1]
-    rows = own_rows(root, chunk, kc)
-    k = pl.ds(chunk * kc, kc)
-    far = power((root[0, rows, :], root[1, rows, :]), exponent)
     even = lax.axis_index("px") % 2 == 0
-    now = tuple(jnp.where(even, pq[2 + c, k, :], pq[c, k, :]) for c in range(2))
+    now = tuple(jnp.where(even, pq[2 + c], pq[c]) for c in range(2))
     out[0], out[1] = cadd(now, cmul(far, (recv[0], recv[1])))
 
 
 def carries(chunk, ny, root, pq, near, one, two, fb):
     kc, ring, place = fb.shape[1], lax.axis_size("px"), lax.axis_index("px")
     rows = own_rows(root, chunk, kc)
-    k = pl.ds(chunk * kc, kc)
     lam = root[0, rows, :], root[1, rows, :]
     gam = root[2, rows, :], root[3, rows, :]
     block = power(lam, ny)
@@ -207,7 +199,7 @@
     even = place % 2 == 0
     f = tuple(jnp.where(even, a, b) for a, b in zip(direct, joined))
     b = tuple(jnp.where(even, b, a) for a, b in zip(direct, joined))
-    p, q = (pq[0, k, :], pq[1, k, :]), (pq[2, k, :], pq[3, k, :])
+    p, q = (pq[0], pq[1]), (pq[2], pq[3])
     left, right = images(lam, 2 * ny, ring, place)
     whole = power(lam, 2 * (ny * ring + 1))
     det = 1.0 - whole[0], -whole[1]
@@ -221,8 +213,8 @@
     fb[2], fb[3] = cmul(scale, b)
 
 
-def local_solve(root, f0, f1, w0, w1):
-    _, half, nk, _ = f0.shape
+def local_solve(chunk, root, f0, f1, w0, w1):
+    _, half, kc, _ = f0.shape
     ny = 2 * half
 
     def row(refs, j, k):
@@ -231,7 +223,7 @@
 
     def block(i, carry):
         k = pl.ds(pl.multiple_of(i * KB, KB), KB)
-        rows = own_rows(root, i, KB)
+        rows = own_rows(root, chunk * (kc // KB) + i, KB)
         lam = root[0, rows, :], root[1, rows, :]
         gam = root[2, rows, :], root[3, rows, :]
 
@@ -256,22 +248,20 @@
             put(j, cmul(gam, here))
         return carry
 
-    lax.fori_loop(0, nk // KB, block, 0)
-
-
-def inverse_z(part, s_ref, root, w_ref, *refs):
-    *fbs, send, keep, u = refs
+    lax.fori_loop(0, kc // KB, block, 0)
+
+
+def inverse_z(chunk, part, s_ref, root, w_ref, fb, send, keep, u):
     me = lax.axis_index("py")
-    _, ny, nk, nz = w_ref.shape
+    _, ny, kc, nz = w_ref.shape
     w = send.shape[3]
 
-    def block(fb, base, i):
-        k = pl.ds(pl.multiple_of((base + i) * KB, KB), KB)
-        rows = own_rows(root, base + i, KB)
+    def block(i, carry):
+        k = pl.ds(pl.multiple_of(i * KB, KB), KB)
+        rows = own_rows(root, chunk * (kc // KB) + i, KB)
         lam = root[0, rows, :], root[1, rows, :]
-        at = pl.ds(pl.multiple_of(i * KB, KB), KB)
-        f = fb[0, at, :], fb[1, at, :]
-        b = fb[2, at, :], fb[3, at, :]
+        f = fb[0, k, :], fb[1, k, :]
+        b = fb[2, k, :], fb[3, k, :]
         past = power(lam, ny)
         if part:
             f = cmul(past, f)
@@ -289,18 +279,22 @@
         own, away = by_half(me, out[:, :w], out[:, w:])
         send[:, :, k, :] = away.reshape(2, ny, KB, w)
         keep[:, :, k, :] = own.reshape(2, ny, KB, w)
-
-    over_blocks(block, nk, fbs)
-
-
-def inverse_x(part, s_ref, keep, recv, src, speed, out, sums):
+        return carry
+
+    lax.fori_loop(0, kc // KB, block, 0)
+
+
+def inverse_x(part, s_ref, *refs):
+    *moved, src, speed, out, sums = refs
+    number = len(moved) // 2
     me = lax.axis_index("py")
     _, nx, _, w = out.shape
     left = stack(s_ref, 1)
     for c in range(2):
         cols = []
         for y in range(YB):
-            high, low = split(jnp.concatenate(by_half(me, keep[c, y], recv[c, y]), axis=0))
+            keep, recv = (jnp.concatenate([r[c, y] for r in rs], axis=0) for rs in (moved[:number], moved[number:]))
+            high, low = split(jnp.concatenate(by_half(me, keep, recv), axis=0))
             cols.append(jnp.concatenate([high, low, high], axis=0))
         got = dot(left, jnp.concatenate(cols, axis=1))
         flat = out.at[c].reshape(nx * YB, w)
@@ -389,7 +383,6 @@
     table_z = table_x if nz == nx else jnp.asarray(np.stack(halves_of(sine_table(nz))))
     root = jnp.asarray(root_tables(nx, nz))
     piece = sds(2, YB, nk, w)
-    modes = sds(2, YB, nk, nz)
     flops = 2 * 2 * nx * YB * w * nx * 3
     est = cost(flops, 4 * 2**20)
 
@@ -405,21 +398,22 @@
             name="forward_x",
         )(table_x, source)
         moved.append((keep, lax.ppermute(send, "py", other)))
-    f, before = [], ()
     kc = nk // CHUNKS
-    plane = sds(2, kc, nz)
+    plane, block = sds(2, kc, nz), sds(2, YB, kc, nz)
+    f, pq, sends = {}, [()] * CHUNKS, []
     for h in range(2):
-        got, pq, *sends = pl.pallas_call(
-            functools.partial(forward_z, h == 0),
-            in_specs=[VM] * (4 + len(before)),
-            out_specs=[VM] * (2 + h * CHUNKS),
-            out_shape=[modes, sds(4, nk, nz)] + [plane] * (h * CHUNKS),
-            compiler_params=params(12),
-            cost_estimate=est,
-            name="forward_z",
-        )(table_z, root, *moved[h], *before)
-        f.append(got)
-        before = (pq,)
+        for c in range(CHUNKS):
+            before = () if h == 0 else (pq[c],)
+            f[h, c], pq[c], *send = pl.pallas_call(
+                functools.partial(forward_z, c, h == 0),
+                in_specs=[VM] * (4 + h),
+                out_specs=[VM] * (2 + h),
+                out_shape=[block, sds(4, kc, nz)] + [plane] * h,
+                compiler_params=params(12),
+                cost_estimate=est,
+                name="forward_z",
+            )(table_z, root, *moved[h], *before)
+            sends += send
 
     def small(body, n_in, out, name):
         return pl.pallas_call(
@@ -437,56 +431,61 @@
 
     pair = mirrored([(i, i + 1) for i in range(0, ring, 2)])
     quad = mirrored([(i, i + 2) for i in range(1, ring, 4)])
-    hops = [mirrored([(i, i + 4)]) for i in range(3, ring - 5, 4)]
+    steps = range(1, ring // 4 - 1)
+    hops = [mirrored([(4 * m - 1, 4 * m + 3)]) for m in steps]
     down = mirrored([(i, i + 2) for i in range(3, ring - 2, 4)])
-    sums = [lax.ppermute(s, "px", pair) for s in sends]
-    near = sums
-    now = [small(functools.partial(fold_pair, c, ny), 3, plane, "fold")(root, pq, r) for c, r in enumerate(near)]
-    for route, blocks in [(quad, 2)] + [(hop, 4) for hop in hops] + [(down, 2)]:
-        sums = [lax.ppermute(s, "px", route) for s in now]
-        now = [
-            small(functools.partial(fold, c, blocks * ny), 3, plane, "fold")(root, s, r)
-            for c, (s, r) in enumerate(zip(now, sums))
-        ]
-    two = [lax.ppermute(s, "px", mirrored([(i, i + 2) for i in range(1, ring - 2, 2)])) for s in now]
-    one = [lax.ppermute(s, "px", mirrored([(i, i + 1) for i in range(1, ring - 2, 2)])) for s in now]
-    fb = [
-        small(functools.partial(carries, c, ny), 5, sds(4, kc, nz), "carries")(root, pq, near[c], one[c], two[c])
+    local = [
+        pl.pallas_call(
+            functools.partial(local_solve, c),
+            in_specs=[VM] * 3,
+            out_specs=[VM, VM],
+            out_shape=[block, block],
+            compiler_params=params(8),
+            cost_estimate=cost(flops // 8, 8 * 2**20),
+            name="local_solve",
+        )(root, f[0, c], f[1, c])
         for c in range(CHUNKS)
     ]
-    local = pl.pallas_call(
-        local_solve,
-        in_specs=[VM] * 3,
-        out_specs=[VM, VM],
-        out_shape=[modes, modes],
-        compiler_params=params(8),
-        cost_estimate=cost(2 * flops, 8 * 2**20),
-        name="local_solve",
-    )(root, *f)
-    moved = []
+    near = [lax.ppermute(s, "px", pair) for s in sends]
+    now = [small(functools.partial(fold_pair, c, ny), 3, plane, "fold")(root, pq[c], r) for c, r in enumerate(near)]
+    for level, (route, blocks) in enumerate([(quad, 2)] + [(hop, 4) for hop in hops] + [(down, 2)]):
+        for c, s in enumerate(now):
+            recv = lax.ppermute(s, "px", route)
+            if level == 1:
+                recv, local[c] = lax.optimization_barrier((recv, local[c]))
+            now[c] = small(functools.partial(fold, c, [ny * blocks]), 3, plane, "fold")(root, s, recv)
+    one = [lax.ppermute(s, "px", mirrored([(i, i + 1) for i in range(1, ring - 2, 2)])) for s in now]
+    two = [lax.ppermute(s, "px", pair) for s in one]
+    fb = [
+        small(functools.partial(carries, c, ny), 5, sds(4, kc, nz), "carries")(root, pq[c], near[c], one[c], two[c])
+        for c in range(CHUNKS)
+    ]
+    kept, sent = {}, {}
+    half = sds(2, YB, kc, w)
     for h in range(2):
-        send, keep = pl.pallas_call(
-            functools.partial(inverse_z, h),
-            in_specs=[VM] * (3 + CHUNKS),
-            out_specs=[VM, VM],
-            out_shape=[piece, piece],
-            scratch_shapes=[pltpu.VMEM((2, YB, KB, nz), f32)],
-            compiler_params=params(12),
-            cost_estimate=est,
-            name="inverse_z",
-        )(table_z, root, local[h], *fb)
-        moved.append((keep, lax.ppermute(send, "py", other)))
+        for c in range(CHUNKS):
+            send, kept[h, c] = pl.pallas_call(
+                functools.partial(inverse_z, c, h),
+                in_specs=[VM] * 4,
+                out_specs=[VM, VM],
+                out_shape=[half, half],
+                scratch_shapes=[pltpu.VMEM((2, YB, KB, nz), f32)],
+                compiler_params=params(12),
+                cost_estimate=est,
+                name="inverse_z",
+            )(table_z, root, local[c][h], fb[c])
+            sent[h, c] = lax.ppermute(send, "py", other)
     solved, sums = [], []
     for h in range(2):
         got, part = pl.pallas_call(
             functools.partial(inverse_x, h),
-            in_specs=[VM] * 5,
+            in_specs=[VM] * (3 + 2 * CHUNKS),
             out_specs=[VM, VM],
             out_shape=[sds(2, nx, YB, w), sds(4, w)],
             compiler_params=params(16),
             cost_estimate=est,
             name="inverse_x",
-        )(table_x, *moved[h], source, speed)
+        )(table_x, *(kept[h, c] for c in range(CHUNKS)), *(sent[h, c] for c in range(CHUNKS)), source, speed)
         solved.append(got)
         sums.append(part)
     sums = sums[0] + sums[1]

time: 112 us -> 106 us (0.946)
  waiting for transfers between devices: 51.6 us -> 11.9 us
  starting transfers between devices: 15 us -> 51.1 us
  blocking collectives: 19.9 us -> 17.4 us
    ppermute x12 -> x16, waiting for transfers between devices: 50.2 us -> 9.54 us  [the longest x8 4.91 us: on_device(): recv = lax.ppermute(s, 'px', route)]
    ppermute x12 -> x16, starting transfers between devices: 11.6 us -> 48.8 us  [the longest x2 38.4 us: on_device(): two = [lax.ppermute(s, 'px', pair) for s in one]]
    all_to_all x1, blocking collectives: 19.9 us -> 17.4 us  [on_device(): lax.all_to_all(jnp.broadcast_to(sums[None], (ring, 4, w)), 'px', 0, 0, ti...]
    pallas_call x17 -> x22, Pallas kernels: 15.2 us -> 15.1 us  [the longest x2 4.66 us: on_device(): pl.pallas_call(functools.partial(inverse_x, h), in_specs=[VM] * (3 + 2 *...]
  transfers between devices with their start and end apart: 19 -> 21, of which waited for: 9 -> 9; matrix products, arithmetic and copies ran while one was open for 0% -> 0% of each run, Pallas kernels for 10% -> 13%
where the time goes in v4:
time: 106 us
  starting transfers between devices  51.1 us (48%)
  Pallas kernels  21.5 us (20%)
  blocking collectives  17.4 us (16%)
  waiting for transfers between devices  11.9 us (11%)
  local copies, waits for them, and re-layouts  3.17 us (3%)
    ppermute x2, starting transfers between devices, on_device(): two = [lax.ppermute(s, 'px', pair) for s in one]  38.4 us
    all_to_all x1, blocking collectives, on_device(): lax.all_to_all(jnp.broadcast_to(sums[None], (ring, 4, w)), 'px', 0, 0, ti...  17.4 us
    ppermute x8, starting transfers between devices, on_device(): recv = lax.ppermute(s, 'px', route)  6.76 us
    ppermute x8, waiting for transfers between devices, on_device(): recv = lax.ppermute(s, 'px', route)  4.91 us
    pallas_call x2, Pallas kernels, on_device(): pl.pallas_call(functools.partial(inverse_x, h), in_specs=[VM] * (3 + 2 *...  4.66 us
    pallas_call x4, Pallas kernels, on_device(): pl.pallas_call(functools.partial(forward_z, c, h == 0), in_specs=[VM] * (...  4.11 us
    ppermute x2, waiting for transfers between devices, on_device(): near = [lax.ppermute(s, 'px', pair) for s in sends]  4.07 us
    pallas_call x4, Pallas kernels, on_device(): pl.pallas_call(functools.partial(inverse_z, c, h), in_specs=[VM] * 4, out...  3.65 us
  transfers between devices with their start and end apart: 21, of which 9 were waited for; matrix products, arithmetic and copies ran while one was open for 0% of the time, Pallas kernels for 13%

profile of v4, /device:TPU:86, one launch (start us, length us, event | category | flops | bytes accessed | tf_op | source)
XLA Modules:
  0.0 105.7 jit_solution(7123006227805367070)
XLA Ops:
  0.0 2.2 %copy-done.1 = f32[2,256,16,128]{3,2,1,0:T(8,128)S(1)} copy-done((f32[2,256,16,128]{3,2,1,0:T(8,128)S(1)}, f32[2,256,16,128]{3,2,1,0:T(8,128)}, u32[]{:S(2)}) %copy-start.1) | copy-done | bytes 4194328
  2.2 0.9 copy-done.3
  3.1 1.6 %forward_x.3 = (f32[2,8,128,128]{3,2,1,0:T(8,128)S(1)}, f32[2,8,128,128]{3,2,1,0:T(8,128)S(1)}) custom-call(bf16[2,256,256]{2,1,0:T(8,128)(2,1)S(1)} %copy-done.3, f32[2,256,16,128]{3,2,1,0:T(8,128)S(1)} %copy-done.1), custom_call_target="tpu_custom_call" | custom-call | flops 805306368 | bytes 4194304 | tf_op jit(solution)/shard_map/forward_x/pallas_call | solution.py:391
  4.8 0.0 copy-start
  4.8 0.1 collective-permute-start.1
  4.9 1.6 %forward_x.2 = (f32[2,8,128,128]{3,2,1,0:T(8,128)S(1)}, f32[2,8,128,128]{3,2,1,0:T(8,128)S(1)}) custom-call(bf16[2,256,256]{2,1,0:T(8,128)(2,1)S(1)} %copy-done.3, f32[2,256,16,128]{3,2,1,0:T(8,128)S(1)} %copy-done.1), custom_call_target="tpu_custom_call" | custom-call | flops 805306368 | bytes 4194304 | tf_op jit(solution)/shard_map/forward_x/pallas_call | solution.py:391
  6.5 0.6 collective-permute-start
  7.1 0.4 collective-permute-done.1.recv
  7.5 0.9 forward_z.4
  8.4 1.0 collective-permute-done.recv
  9.4 1.2 %forward_z.5 = (f32[2,8,64,256]{3,2,1,0:T(8,128)S(1)}, f32[4,64,256]{2,1,0:T(8,128)S(1)}, f32[2,64,256]{2,1,0:T(8,128)S(1)}) custom-call(bf16[2,256,256]{2,1,0:T(8,128)(2,1)S(1)} %copy-done.3, f32[4,256,256]{2,1,0:T(8,128)S(1)} %copy-done, f32[2,8,128,128]{3,2,1,0:T(8,128)S(1)} %get-tuple-element.41.keep, f32[2,8,128,128]{3,2,1,0:T(8,128)S(1)} %collective-permute-done.recv, ...), custom_call_target="tpu_custom_call" | custom-call | flops 805306368 | bytes 4194304 | tf_op jit(solution)/shard_map/forward_z/pallas_call | solution.py:407
  10.6 2.2 %collective-permute-start.2 = (f32[2,64,256]{2,1,0:T(8,128)S(1)}, f32[2,64,256]{2,1,0:T(8,128)S(1)}, u32[]{:S(2)}, u32[]{:S(2)}) collective-permute-start(f32[2,64,256]{2,1,0:T(8,128)S(1)} %get-tuple-element.47), channel_id=1, source_target_pairs={{0,2},{4,6},{8,10},{12,14},{16,18},{20,22},{24,26},{28,30},{30,28}... | collective-permute-start | bytes 393224 | tf_op jit(solution)/shard_map/ppermute | solution.py:449
  12.8 0.9 forward_z.6
  13.7 1.2 %forward_z.7 = (f32[2,8,64,256]{3,2,1,0:T(8,128)S(1)}, f32[4,64,256]{2,1,0:T(8,128)S(1)}, f32[2,64,256]{2,1,0:T(8,128)S(1)}) custom-call(bf16[2,256,256]{2,1,0:T(8,128)(2,1)S(1)} %copy-done.3, f32[4,256,256]{2,1,0:T(8,128)S(1)} %copy-done, f32[2,8,128,128]{3,2,1,0:T(8,128)S(1)} %get-tuple-element.41.keep, f32[2,8,128,128]{3,2,1,0:T(8,128)S(1)} %collective-permute-done.recv, ...), custom_call_target="tpu_custom_call" | custom-call | flops 805306368 | bytes 4194304 | tf_op jit(solution)/shard_map/forward_z/pallas_call | solution.py:407
  14.9 0.1 collective-permute-start.9
  15.0 1.8 %collective-permute-done.2.recv.near = f32[2,64,256]{2,1,0:T(8,128)S(1)} collective-permute-done((f32[2,64,256]{2,1,0:T(8,128)S(1)}, f32[2,64,256]{2,1,0:T(8,128)S(1)}, u32[]{:S(2)}, u32[]{:S(2)}) %collective-permute-start.2) | collective-permute-done | bytes 131104 | tf_op jit(solution)/shard_map/ppermute | solution.py:449
  16.9 0.1 fold.10.now
  16.9 1.3 %collective-permute-start.3 = (f32[2,64,256]{2,1,0:T(8,128)S(1)}, f32[2,64,256]{2,1,0:T(8,128)S(1)}, u32[]{:S(2)}, u32[]{:S(2)}) collective-permute-start(f32[2,64,256]{2,1,0:T(8,128)S(1)} %fold.10.now), channel_id=1, source_target_pairs={{2,6},{10,14},{18,22},{26,30},{28,24},{20,16},{12,8},{4,0},{3,7},{... | collective-permute-start | bytes 393224 | tf_op jit(solution)/shard_map/ppermute | solution.py:453
  18.2 2.2 %collective-permute-done.9.recv.near = f32[2,64,256]{2,1,0:T(8,128)S(1)} collective-permute-done((f32[2,64,256]{2,1,0:T(8,128)S(1)}, f32[2,64,256]{2,1,0:T(8,128)S(1)}, u32[]{:S(2)}, u32[]{:S(2)}) %collective-permute-start.9) | collective-permute-done | bytes 131104 | tf_op jit(solution)/shard_map/ppermute | solution.py:449
  20.5 0.1 fold.15.now
  20.6 1.3 %collective-permute-start.10 = (f32[2,64,256]{2,1,0:T(8,128)S(1)}, f32[2,64,256]{2,1,0:T(8,128)S(1)}, u32[]{:S(2)}, u32[]{:S(2)}) collective-permute-start(f32[2,64,256]{2,1,0:T(8,128)S(1)} %fold.15.now), channel_id=1, source_target_pairs={{2,6},{10,14},{18,22},{26,30},{28,24},{20,16},{12,8},{4,0},{3,7},{... | collective-permute-start | bytes 393224 | tf_op jit(solution)/shard_map/ppermute | solution.py:453
  21.9 3.5 %collective-permute-done.3.refs_0_ = f32[2,64,256]{2,1,0:T(8,128)S(1)} collective-permute-done((f32[2,64,256]{2,1,0:T(8,128)S(1)}, f32[2,64,256]{2,1,0:T(8,128)S(1)}, u32[]{:S(2)}, u32[]{:S(2)}) %collective-permute-start.3) | collective-permute-done | bytes 131104 | tf_op jit(solution)/shard_map/ppermute | solution.py:453
  25.3 0.1 fold.11.now
  25.4 0.7 collective-permute-start.4
  26.1 0.9 local_solve.2
  27.0 1.4 %collective-permute-done.10.refs_0_ = f32[2,64,256]{2,1,0:T(8,128)S(1)} collective-permute-done((f32[2,64,256]{2,1,0:T(8,128)S(1)}, f32[2,64,256]{2,1,0:T(8,128)S(1)}, u32[]{:S(2)}, u32[]{:S(2)}) %collective-permute-start.10) | collective-permute-done | bytes 131104 | tf_op jit(solution)/shard_map/ppermute | solution.py:453
  28.5 0.1 fold.16.now
  28.5 0.7 collective-permute-start.11
  29.2 0.0 collective-permute-done.4.refs_0_
  29.2 0.1 fold.12.now
  29.3 0.7 collective-permute-start.5
  30.0 0.9 local_solve.3
  31.0 0.1 fold.17.now
  31.1 0.7 collective-permute-start.12
  31.8 0.1 fold.13.now
  31.9 0.7 collective-permute-start.6
  32.5 0.1 fold.18.now
  32.6 0.0 copy-start.4
  32.7 0.8 collective-permute-start.13
  33.5 0.1 fold.14
  33.6 0.7 collective-permute-start.7
  34.3 0.1 fold.19
  34.4 0.7 collective-permute-start.14
  35.0 34.4 %collective-permute-start.8 = (f32[2,64,256]{2,1,0:T(8,128)S(1)}, f32[2,64,256]{2,1,0:T(8,128)S(1)}, u32[]{:S(2)}, u32[]{:S(2)}) collective-permute-start(f32[2,64,256]{2,1,0:T(8,128)S(1)} %collective-permute-done.7.one), channel_id=1, source_target_pairs={{0,2},{4,6},{8,10},{12,14},{16,18},{20,22},{24,26},{28,30},{30,28}... | collective-permute-start | bytes 393224 | tf_op jit(solution)/shard_map/ppermute | solution.py:458
  69.4 4.1 %collective-permute-start.15 = (f32[2,64,256]{2,1,0:T(8,128)S(1)}, f32[2,64,256]{2,1,0:T(8,128)S(1)}, u32[]{:S(2)}, u32[]{:S(2)}) collective-permute-start(f32[2,64,256]{2,1,0:T(8,128)S(1)} %collective-permute-done.14.one), channel_id=1, source_target_pairs={{0,2},{4,6},{8,10},{12,14},{16,18},{20,22},{24,26},{28,30},{30,28}... | collective-permute-start | bytes 393224 | tf_op jit(solution)/shard_map/ppermute | solution.py:458
  73.5 0.4 carries.2.fb
  73.9 0.9 inverse_z.6
  74.8 0.3 collective-permute-start.18
  75.1 0.9 inverse_z.4
  76.1 0.3 collective-permute-done.15.two
  76.4 0.4 carries.3.fb
  76.8 0.0 copy-start.2
  76.8 0.9 inverse_z.7
  77.8 0.3 collective-permute-start.19
  78.0 0.3 collective-permute-start.16
  78.4 0.9 inverse_z.5
  79.3 0.3 collective-permute-start.17
  79.6 0.2 collective-permute-done.19.refs_3_
  79.8 2.3 %inverse_x.3 = (f32[2,256,8,128]{3,2,1,0:T(8,128)S(1)}, f32[4,128]{1,0:T(4,128)S(1)}) custom-call(bf16[2,256,256]{2,1,0:T(8,128)(2,1)S(1)} %copy-done.4, f32[2,8,64,128]{3,2,1,0:T(8,128)S(1)} %get-tuple-element.69.refs_0_, f32[2,8,64,128]{3,2,1,0:T(8,128)S(1)} %get-tuple-element.71.refs_1_, f32[2,8,64,128]{3,2,1,0:T(8,128)S(1)} %collective-permute-done.18.refs_2_, ...), custom_call_target="tpu_custom_call" | custom-call | flops 805306368 | bytes 4194304 | tf_op jit(solution)/shard_map/inverse_x/pallas_call | solution.py:480
  82.1 2.3 %inverse_x.2 = (f32[2,256,8,128]{3,2,1,0:T(8,128)S(1)}, f32[4,128]{1,0:T(4,128)S(1)}) custom-call(bf16[2,256,256]{2,1,0:T(8,128)(2,1)S(1)} %copy-done.4, f32[2,8,64,128]{3,2,1,0:T(8,128)S(1)} %get-tuple-element.54.refs_0_, f32[2,8,64,128]{3,2,1,0:T(8,128)S(1)} %get-tuple-element.64.refs_1_, f32[2,8,64,128]{3,2,1,0:T(8,128)S(1)} %collective-permute-done.16.refs_2_, ...), custom_call_target="tpu_custom_call" | custom-call | flops 805306368 | bytes 4194304 | tf_op jit(solution)/shard_map/inverse_x/pallas_call | solution.py:480
  84.5 0.3 collective-permute-start.20
  84.8 1.0 collective-permute-done.20
  85.8 17.4 %all_to_all.5.total = f32[16,4,128]{2,1,0:T(4,128)S(1)} all-to-all(f32[16,4,128]{2,1,0:T(4,128)S(1)} %broadcast_in_dim.2), channel_id=1, replica_groups=mesh['samples'=4,'px'=16,'py'=2] {'px'}, dimensions={0} | all-to-all | bytes 65536 | tf_op jit(solution)/shard_map/all_to_all | solution.py:493
  103.2 2.3 %finish.1 = f32[2,256,16,128]{3,2,1,0:T(8,128)} custom-call(f32[16,4,128]{2,1,0:T(4,128)S(1)} %all_to_all.5.total, f32[2,256,8,128]{3,2,1,0:T(8,128)S(1)} %get-tuple-element.75.ps0, f32[2,256,8,128]{3,2,1,0:T(8,128)S(1)} %get-tuple-element.76.ps1), custom_call_target="tpu_custom_call" | custom-call | flops 10000000 | bytes 8388608 | tf_op jit(solution)/shard_map/finish/pallas_call | solution.py:494
  (21 shorter events, 0.1 us)
Async XLA Ops:
  0.0 2.2 %copy-start.1 = (f32[2,256,16,128]{3,2,1,0:T(8,128)S(1)}, f32[2,256,16,128]{3,2,1,0:T(8,128)}, u32[]{:S(2)}) copy-start(f32[2,256,16,128]{3,2,1,0:T(8,128)} %refs_4_.3) | copy-start | bytes 12582916
  2.2 0.9 copy-start.3
  4.8 2.8 %copy-start = (f32[4,256,256]{2,1,0:T(8,128)S(1)}, f32[4,256,256]{2,1,0:T(8,128)}, u32[]{:S(2)}) copy-start(f32[4,256,256]{2,1,0:T(8,128)} %constant.5.clone.root) | copy-start | bytes 3145732
  4.8 2.8 %collective-permute-start.1 = (f32[2,8,128,128]{3,2,1,0:T(8,128)S(1)}, f32[2,8,128,128]{3,2,1,0:T(8,128)S(1)}, u32[]{:S(2)}, u32[]{:S(2)}) collective-permute-start(f32[2,8,128,128]{3,2,1,0:T(8,128)S(1)} %get-tuple-element.44), channel_id=1, source_target_pairs={{0,1},{1,0},{2,3},{3,2},{4,5},{5,4},{6,7},{7,6},{8,9},{9,8},{10,11... | collective-permute-start | bytes 3145736 | tf_op jit(solution)/shard_map/ppermute | solution.py:400
  6.5 2.9 %collective-permute-start = (f32[2,8,128,128]{3,2,1,0:T(8,128)S(1)}, f32[2,8,128,128]{3,2,1,0:T(8,128)S(1)}, u32[]{:S(2)}, u32[]{:S(2)}) collective-permute-start(f32[2,8,128,128]{3,2,1,0:T(8,128)S(1)} %get-tuple-element.42), channel_id=1, source_target_pairs={{0,1},{1,0},{2,3},{3,2},{4,5},{5,4},{6,7},{7,6},{8,9},{9,8},{10,11... | collective-permute-start | bytes 3145736 | tf_op jit(solution)/shard_map/ppermute | solution.py:400
  10.6 6.3 %collective-permute-start.2 = (f32[2,64,256]{2,1,0:T(8,128)S(1)}, f32[2,64,256]{2,1,0:T(8,128)S(1)}, u32[]{:S(2)}, u32[]{:S(2)}) collective-permute-start(f32[2,64,256]{2,1,0:T(8,128)S(1)} %get-tuple-element.47), channel_id=1, source_target_pairs={{0,2},{4,6},{8,10},{12,14},{16,18},{20,22},{24,26},{28,30},{30,28}... | collective-permute-start | bytes 393224 | tf_op jit(solution)/shard_map/ppermute | solution.py:449
  14.9 5.6 %collective-permute-start.9 = (f32[2,64,256]{2,1,0:T(8,128)S(1)}, f32[2,64,256]{2,1,0:T(8,128)S(1)}, u32[]{:S(2)}, u32[]{:S(2)}) collective-permute-start(f32[2,64,256]{2,1,0:T(8,128)S(1)} %get-tuple-element.57), channel_id=1, source_target_pairs={{0,2},{4,6},{8,10},{12,14},{16,18},{20,22},{24,26},{28,30},{30,28}... | collective-permute-start | bytes 393224 | tf_op jit(solution)/shard_map/ppermute | solution.py:449
  16.9 8.4 %collective-permute-start.3 = (f32[2,64,256]{2,1,0:T(8,128)S(1)}, f32[2,64,256]{2,1,0:T(8,128)S(1)}, u32[]{:S(2)}, u32[]{:S(2)}) collective-permute-start(f32[2,64,256]{2,1,0:T(8,128)S(1)} %fold.10.now), channel_id=1, source_target_pairs={{2,6},{10,14},{18,22},{26,30},{28,24},{20,16},{12,8},{4,0},{3,7},{... | collective-permute-start | bytes 393224 | tf_op jit(solution)/shard_map/ppermute | solution.py:453
  20.6 7.9 %collective-permute-start.10 = (f32[2,64,256]{2,1,0:T(8,128)S(1)}, f32[2,64,256]{2,1,0:T(8,128)S(1)}, u32[]{:S(2)}, u32[]{:S(2)}) collective-permute-start(f32[2,64,256]{2,1,0:T(8,128)S(1)} %fold.15.now), channel_id=1, source_target_pairs={{2,6},{10,14},{18,22},{26,30},{28,24},{20,16},{12,8},{4,0},{3,7},{... | collective-permute-start | bytes 393224 | tf_op jit(solution)/shard_map/ppermute | solution.py:453
  25.4 3.8 %collective-permute-start.4 = (f32[2,64,256]{2,1,0:T(8,128)S(1)}, f32[2,64,256]{2,1,0:T(8,128)S(1)}, u32[]{:S(2)}, u32[]{:S(2)}) collective-permute-start(f32[2,64,256]{2,1,0:T(8,128)S(1)} %fold.11.now), channel_id=1, source_target_pairs={{6,14},{24,16},{7,15},{25,17},{38,46},{56,48},{39,47},{57,49},{70,... | collective-permute-start | bytes 393224 | tf_op jit(solution)/shard_map/ppermute | solution.py:453
  28.5 2.4 %collective-permute-start.11 = (f32[2,64,256]{2,1,0:T(8,128)S(1)}, f32[2,64,256]{2,1,0:T(8,128)S(1)}, u32[]{:S(2)}, u32[]{:S(2)}) collective-permute-start(f32[2,64,256]{2,1,0:T(8,128)S(1)} %fold.16.now), channel_id=1, source_target_pairs={{6,14},{24,16},{7,15},{25,17},{38,46},{56,48},{39,47},{57,49},{70,... | collective-permute-start | bytes 393224 | tf_op jit(solution)/shard_map/ppermute | solution.py:453
  29.3 2.4 %collective-permute-start.5 = (f32[2,64,256]{2,1,0:T(8,128)S(1)}, f32[2,64,256]{2,1,0:T(8,128)S(1)}, u32[]{:S(2)}, u32[]{:S(2)}) collective-permute-start(f32[2,64,256]{2,1,0:T(8,128)S(1)} %fold.12.now), channel_id=1, source_target_pairs={{14,22},{16,8},{15,23},{17,9},{46,54},{48,40},{47,55},{49,41},{78,... | collective-permute-start | bytes 393224 | tf_op jit(solution)/shard_map/ppermute | solution.py:453
  31.1 1.5 %collective-permute-start.12 = (f32[2,64,256]{2,1,0:T(8,128)S(1)}, f32[2,64,256]{2,1,0:T(8,128)S(1)}, u32[]{:S(2)}, u32[]{:S(2)}) collective-permute-start(f32[2,64,256]{2,1,0:T(8,128)S(1)} %fold.17.now), channel_id=1, source_target_pairs={{14,22},{16,8},{15,23},{17,9},{46,54},{48,40},{47,55},{49,41},{78,... | collective-permute-start | bytes 393224 | tf_op jit(solution)/shard_map/ppermute | solution.py:453
  31.9 1.6 %collective-permute-start.6 = (f32[2,64,256]{2,1,0:T(8,128)S(1)}, f32[2,64,256]{2,1,0:T(8,128)S(1)}, u32[]{:S(2)}, u32[]{:S(2)}) collective-permute-start(f32[2,64,256]{2,1,0:T(8,128)S(1)} %fold.13.now), channel_id=1, source_target_pairs={{6,10},{14,18},{22,26},{24,20},{16,12},{8,4},{7,11},{15,19},{23,27... | collective-permute-start | bytes 393224 | tf_op jit(solution)/shard_map/ppermute | solution.py:453
  32.6 41.2 %copy-start.4 = (bf16[2,256,256]{2,1,0:T(8,128)(2,1)S(1)}, bf16[2,256,256]{2,1,0:T(8,128)(2,1)}, u32[]{:S(2)}) copy-start(bf16[2,256,256]{2,1,0:T(8,128)(2,1)} %constant.4.clone.s_ref) | copy-start | bytes 786436
  32.7 1.6 %collective-permute-start.13 = (f32[2,64,256]{2,1,0:T(8,128)S(1)}, f32[2,64,256]{2,1,0:T(8,128)S(1)}, u32[]{:S(2)}, u32[]{:S(2)}) collective-permute-start(f32[2,64,256]{2,1,0:T(8,128)S(1)} %fold.18.now), channel_id=1, source_target_pairs={{6,10},{14,18},{22,26},{24,20},{16,12},{8,4},{7,11},{15,19},{23,27... | collective-permute-start | bytes 393224 | tf_op jit(solution)/shard_map/ppermute | solution.py:453
  33.6 1.5 %collective-permute-start.7 = (f32[2,64,256]{2,1,0:T(8,128)S(1)}, f32[2,64,256]{2,1,0:T(8,128)S(1)}, u32[]{:S(2)}, u32[]{:S(2)}) collective-permute-start(f32[2,64,256]{2,1,0:T(8,128)S(1)} %fold.14), channel_id=1, source_target_pairs={{2,4},{6,8},{10,12},{14,16},{18,20},{22,24},{26,28},{28,26},{24,22... | collective-permute-start | bytes 393224 | tf_op jit(solution)/shard_map/ppermute | solution.py:457
  34.4 35.0 %collective-permute-start.14 = (f32[2,64,256]{2,1,0:T(8,128)S(1)}, f32[2,64,256]{2,1,0:T(8,128)S(1)}, u32[]{:S(2)}, u32[]{:S(2)}) collective-permute-start(f32[2,64,256]{2,1,0:T(8,128)S(1)} %fold.19), channel_id=1, source_target_pairs={{2,4},{6,8},{10,12},{14,16},{18,20},{22,24},{26,28},{28,26},{24,22... | collective-permute-start | bytes 393224 | tf_op jit(solution)/shard_map/ppermute | solution.py:457
  35.0 38.4 %collective-permute-start.8 = (f32[2,64,256]{2,1,0:T(8,128)S(1)}, f32[2,64,256]{2,1,0:T(8,128)S(1)}, u32[]{:S(2)}, u32[]{:S(2)}) collective-permute-start(f32[2,64,256]{2,1,0:T(8,128)S(1)} %collective-permute-done.7.one), channel_id=1, source_target_pairs={{0,2},{4,6},{8,10},{12,14},{16,18},{20,22},{24,26},{28,30},{30,28}... | collective-permute-start | bytes 393224 | tf_op jit(solution)/shard_map/ppermute | solution.py:458
  69.4 7.0 %collective-permute-start.15 = (f32[2,64,256]{2,1,0:T(8,128)S(1)}, f32[2,64,256]{2,1,0:T(8,128)S(1)}, u32[]{:S(2)}, u32[]{:S(2)}) collective-permute-start(f32[2,64,256]{2,1,0:T(8,128)S(1)} %collective-permute-done.14.one), channel_id=1, source_target_pairs={{0,2},{4,6},{8,10},{12,14},{16,18},{20,22},{24,26},{28,30},{30,28}... | collective-permute-start | bytes 393224 | tf_op jit(solution)/shard_map/ppermute | solution.py:458
  74.8 4.8 %collective-permute-start.18 = (f32[2,8,64,128]{3,2,1,0:T(8,128)S(1)}, f32[2,8,64,128]{3,2,1,0:T(8,128)S(1)}, u32[]{:S(2)}, u32[]{:S(2)}) collective-permute-start(f32[2,8,64,128]{3,2,1,0:T(8,128)S(1)} %get-tuple-element.72), channel_id=1, source_target_pairs={{0,1},{1,0},{2,3},{3,2},{4,5},{5,4},{6,7},{7,6},{8,9},{9,8},{10,11... | collective-permute-start | bytes 1572872 | tf_op jit(solution)/shard_map/ppermute | solution.py:477
  76.4 3.4 %copy-start.5 = (f32[256,16,128]{2,1,0:T(8,128)S(1)}, f32[256,16,128]{2,1,0:T(8,128)}, u32[]{:S(2)}) copy-start(f32[256,16,128]{2,1,0:T(8,128)} %refs_5_.3) | copy-start | bytes 6291460
  76.8 3.0 %copy-start.2 = (f32[2,256,16,128]{3,2,1,0:T(8,128)S(1)}, f32[2,256,16,128]{3,2,1,0:T(8,128)}, u32[]{:S(2)}) copy-start(f32[2,256,16,128]{3,2,1,0:T(8,128)} %refs_4_.3) | copy-start | bytes 12582916
  77.8 2.0 %collective-permute-start.19 = (f32[2,8,64,128]{3,2,1,0:T(8,128)S(1)}, f32[2,8,64,128]{3,2,1,0:T(8,128)S(1)}, u32[]{:S(2)}, u32[]{:S(2)}) collective-permute-start(f32[2,8,64,128]{3,2,1,0:T(8,128)S(1)} %get-tuple-element.73), channel_id=1, source_target_pairs={{0,1},{1,0},{2,3},{3,2},{4,5},{5,4},{6,7},{7,6},{8,9},{9,8},{10,11... | collective-permute-start | bytes 1572872 | tf_op jit(solution)/shard_map/ppermute | solution.py:477
  78.0 4.1 %collective-permute-start.16 = (f32[2,8,64,128]{3,2,1,0:T(8,128)S(1)}, f32[2,8,64,128]{3,2,1,0:T(8,128)S(1)}, u32[]{:S(2)}, u32[]{:S(2)}) collective-permute-start(f32[2,8,64,128]{3,2,1,0:T(8,128)S(1)} %get-tuple-element.65), channel_id=1, source_target_pairs={{0,1},{1,0},{2,3},{3,2},{4,5},{5,4},{6,7},{7,6},{8,9},{9,8},{10,11... | collective-permute-start | bytes 1572872 | tf_op jit(solution)/shard_map/ppermute | solution.py:477
  79.3 2.8 %collective-permute-start.17 = (f32[2,8,64,128]{3,2,1,0:T(8,128)S(1)}, f32[2,8,64,128]{3,2,1,0:T(8,128)S(1)}, u32[]{:S(2)}, u32[]{:S(2)}) collective-permute-start(f32[2,8,64,128]{3,2,1,0:T(8,128)S(1)} %get-tuple-element.66), channel_id=1, source_target_pairs={{0,1},{1,0},{2,3},{3,2},{4,5},{5,4},{6,7},{7,6},{8,9},{9,8},{10,11... | collective-permute-start | bytes 1572872 | tf_op jit(solution)/shard_map/ppermute | solution.py:477
  84.5 1.3 %collective-permute-start.20 = (f32[4,128]{1,0:T(4,128)S(1)}, f32[4,128]{1,0:T(4,128)S(1)}, u32[]{:S(2)}, u32[]{:S(2)}) collective-permute-start(f32[4,128]{1,0:T(4,128)S(1)} %add.6), channel_id=1, source_target_pairs={{0,1},{1,0},{2,3},{3,2},{4,5},{5,4},{6,7},{7,6},{8,9},{9,8},{10,11... | collective-permute-start | bytes 6152 | tf_op jit(solution)/shard_map/ppermute | solution.py:492

commit v5 on v4

--- a/solution.py
+++ b/solution.py
@@ -70,23 +70,31 @@
     return jnp.where(first, keep, recv), jnp.where(first, recv, keep)
 
 
-def forward_x(part, s_ref, src, send, keep):
+def forward_x(chunk, s_ref, values, send, keep, *parts):
     me = lax.axis_index("py")
-    _, nx, ny, w = src.shape
-    nk = nx // 2
-    for c in range(2):
-        flat = src.at[c].reshape(nx * ny, w)
-        cols = []
-        for y in range(YB):
-            high, low = split(flat[pl.ds(part * YB + y, nx, stride=ny), :])
-            cols.append(jnp.concatenate([high, low, high], axis=0))
-        right = jnp.concatenate(cols, axis=1)
-        for half, out in ((1 - me, send), (me, keep)):
-            rows = pl.ds(pl.multiple_of(half * nk, nk), nk)
-            high, low = s_ref[0, rows, :], s_ref[1, rows, :]
-            got = dot(jnp.concatenate([high, high, low], axis=1), right)
+    _, ny, kc, w = send.shape
+    nx = s_ref.shape[1]
+    for h in range(ny // YB):
+        for c in range(2):
+            if parts:
+                flat = values.at[c].reshape(nx * ny, w)
+                cols = []
+                for y in range(YB):
+                    cols.append(jnp.concatenate(split(flat[pl.ds(h * YB + y, nx, stride=ny), :]), axis=0))
+                both = jnp.concatenate(cols, axis=1)
+                parts[0][c, h] = both
+            else:
+                both = values[c, h]
+            right = jnp.concatenate([both, both[:nx]], axis=0)
+            left = []
+            for half in (1 - me, me):
+                rows = pl.ds(pl.multiple_of(half * (nx // 2) + chunk * kc, kc), kc)
+                high, low = s_ref[0, rows, :], s_ref[1, rows, :]
+                left.append(jnp.concatenate([high, high, low], axis=1))
+            got = dot(jnp.concatenate(left, axis=0), right)
             for y in range(YB):
-                out[c, y] = got[:, y * w : (y + 1) * w]
+                send[c, h * YB + y] = got[:kc, y * w : (y + 1) * w]
+                keep[c, h * YB + y] = got[kc:, y * w : (y + 1) * w]
 
 
 def own_rows(root, block, kb):
@@ -105,45 +113,43 @@
     return result
 
 
-def forward_z(chunk, first, s_ref, root, keep, recv, *refs):
-    if first:
-        f_out, pq = refs
-    else:
-        before, f_out, pq, send = refs
+def forward_z(chunk, s_ref, root, keep, recv, *refs):
+    *_, f0, f1, pq, send, done = refs
+    done[...] = jnp.zeros_like(done)
     me = lax.axis_index("py")
     ring, place = lax.axis_size("px"), lax.axis_index("px")
-    _, ny, _, w = keep.shape
-    _, _, kc, nz = f_out.shape
+    _, ny, kc, w = keep.shape
+    nz = f0.shape[3]
 
     def block(i, carry):
         k = pl.ds(pl.multiple_of(i * KB, KB), KB)
-        here = pl.ds(pl.multiple_of(chunk * kc + i * KB, KB), KB)
-        shape = 2 * ny * KB, w
-        both = by_half(me, keep[:, :, here, :].reshape(shape), recv[:, :, here, :].reshape(shape))
-        high, low = split(jnp.concatenate(both, axis=1))
-        total = dot(jnp.concatenate([high, low, high], axis=1), stack(s_ref, 0))
-        total = total.reshape(2, ny, KB, nz)
-        f_out[:, :, k, :] = total
         rows = own_rows(root, chunk * (kc // KB) + i, KB)
         lam = root[0, rows, :], root[1, rows, :]
-        row = [(total[0, j], total[1, j]) for j in range(ny)]
-        p = row[0] if first else cadd(cmul(lam, (before[0, k, :], before[1, k, :])), row[0])
-        q = row[ny - 1]
-        for j in range(1, ny):
-            p = cadd(cmul(lam, p), row[j])
-            q = cadd(cmul(lam, q), row[ny - 1 - j])
-        if not first:
-            q = cadd(cmul(power(lam, ny), q), (before[2, k, :], before[3, k, :]))
-            wide = 2 * ny
-            left, right = images(lam, 2 * wide, ring, place)
-            edge = power(lam, wide + 1)
-            p, q = (
-                csub(p, cmul(cmul(left, edge), q)),
-                csub(q, cmul(cmul(right, edge), p)),
-            )
-            even = place % 2 == 0
-            for c in range(2):
-                send[c, k, :] = jnp.where(even, p[c], q[c])
+        p, q = None, None
+        for h, f in enumerate((f0, f1)):
+            here = slice(h * YB, (h + 1) * YB)
+            shape = 2 * YB * KB, w
+            both = by_half(me, keep[:, here, k, :].reshape(shape), recv[:, here, k, :].reshape(shape))
+            high, low = split(jnp.concatenate(both, axis=1))
+            total = dot(jnp.concatenate([high, low, high], axis=1), stack(s_ref, 0))
+            total = total.reshape(2, YB, KB, nz)
+            f[:, :, k, :] = total
+            row = [(total[0, j], total[1, j]) for j in range(YB)]
+            p = row[0] if p is None else cadd(cmul(lam, p), row[0])
+            part = row[YB - 1]
+            for j in range(1, YB):
+                p = cadd(cmul(lam, p), row[j])
+                part = cadd(cmul(lam, part), row[YB - 1 - j])
+            q = part if q is None else cadd(cmul(power(lam, h * YB), part), q)
+        left, right = images(lam, 2 * ny, ring, place)
+        edge = power(lam, ny + 1)
+        p, q = (
+            csub(p, cmul(cmul(left, edge), q)),
+            csub(q, cmul(cmul(right, edge), p)),
+        )
+        even = place % 2 == 0
+        for c in range(2):
+            send[c, k, :] = jnp.where(even, p[c], q[c])
         for c, part in enumerate((*p, *q)):
             pq[c, k, :] = part
         return carry
@@ -179,7 +185,9 @@
     out[0], out[1] = total
 
 
-def fold_pair(chunk, exponent, root, pq, recv, out):
+def fold_pair(chunk, exponent, root, pq, recv, *refs):
+    *_, out, done = refs
+    done[...] = jnp.zeros_like(done)
     kc = out.shape[1]
     rows = own_rows(root, chunk, kc)
     far = power((root[0, rows, :], root[1, rows, :]), exponent)
@@ -382,44 +390,47 @@
     table_x = jnp.asarray(np.stack(halves_of(sine_table(nx))))
     table_z = table_x if nz == nx else jnp.asarray(np.stack(halves_of(sine_table(nz))))
     root = jnp.asarray(root_tables(nx, nz))
-    piece = sds(2, YB, nk, w)
     flops = 2 * 2 * nx * YB * w * nx * 3
     est = cost(flops, 4 * 2**20)
 
-    moved = []
-    for h in range(2):
-        send, keep = pl.pallas_call(
-            functools.partial(forward_x, h),
+    kc = nk // CHUNKS
+    plane, block, piece = sds(2, kc, nz), sds(2, YB, kc, nz), sds(2, ny, kc, w)
+    parts = jax.ShapeDtypeStruct((2, ny // YB, 2 * nx, YB * w), bf16)
+    moved, values = [], source
+    for c in range(CHUNKS):
+        first = c == 0
+        send, keep, *left = pl.pallas_call(
+            functools.partial(forward_x, c),
             in_specs=[VM] * 2,
-            out_specs=[VM] * 2,
-            out_shape=[piece, piece],
+            out_specs=[VM] * (2 + first),
+            out_shape=[piece, piece] + [parts] * first,
+            compiler_params=params(16),
+            cost_estimate=est,
+            name="forward_x",
+        )(table_x, values)
+        values = left[0] if first else values
+        moved.append((keep, lax.ppermute(send, "py", other)))
+    f, pq, sends, after = [], [], [], ()
+    for c in range(CHUNKS):
+        *got, carry, send, mark = pl.pallas_call(
+            functools.partial(forward_z, c),
+            in_specs=[VM] * (4 + len(after)),
+            out_specs=[VM] * 5,
+            out_shape=[block, block, sds(4, kc, nz), plane, sds(8, 128)],
             compiler_params=params(12),
             cost_estimate=est,
-            name="forward_x",
-        )(table_x, source)
-        moved.append((keep, lax.ppermute(send, "py", other)))
-    kc = nk // CHUNKS
-    plane, block = sds(2, kc, nz), sds(2, YB, kc, nz)
-    f, pq, sends = {}, [()] * CHUNKS, []
-    for h in range(2):
-        for c in range(CHUNKS):
-            before = () if h == 0 else (pq[c],)
-            f[h, c], pq[c], *send = pl.pallas_call(
-                functools.partial(forward_z, c, h == 0),
-                in_specs=[VM] * (4 + h),
-                out_specs=[VM] * (2 + h),
-                out_shape=[block, sds(4, kc, nz)] + [plane] * h,
-                compiler_params=params(12),
-                cost_estimate=est,
-                name="forward_z",
-            )(table_z, root, *moved[h], *before)
-            sends += send
+            name="forward_z",
+        )(table_z, root, *moved[c], *after)
+        after = (mark,)
+        f.append(got)
+        pq.append(carry)
+        sends.append(send)
 
     def small(body, n_in, out, name):
         return pl.pallas_call(
             body,
             in_specs=[VM] * n_in,
-            out_specs=VM,
+            out_specs=VM if not isinstance(out, list) else [VM] * len(out),
             out_shape=out,
             compiler_params=params(4),
             cost_estimate=cost(2 * 10**6, 2**19),
@@ -443,11 +454,17 @@
             compiler_params=params(8),
             cost_estimate=cost(flops // 8, 8 * 2**20),
             name="local_solve",
-        )(root, f[0, c], f[1, c])
+        )(root, *f[c])
         for c in range(CHUNKS)
     ]
     near = [lax.ppermute(s, "px", pair) for s in sends]
-    now = [small(functools.partial(fold_pair, c, ny), 3, plane, "fold")(root, pq[c], r) for c, r in enumerate(near)]
+    now, after = [], ()
+    for c, r in enumerate(near):
+        got, mark = small(functools.partial(fold_pair, c, ny), 3 + len(after), [plane, sds(8, 128)], "fold")(
+            root, pq[c], r, *after
+        )
+        now.append(got)
+        after = (mark,)
     for level, (route, blocks) in enumerate([(quad, 2)] + [(hop, 4) for hop in hops] + [(down, 2)]):
         for c, s in enumerate(now):
             recv = lax.ppermute(s, "px", route)

time: 106 us -> 104 us (0.981)
  blocking collectives: 17.4 us -> 16.1 us
    all_to_all x1, blocking collectives: 17.4 us -> 16.1 us  [on_device(): lax.all_to_all(jnp.broadcast_to(sums[None], (ring, 4, w)), 'px', 0, 0, ti...]
    pallas_call x8 -> x6, Pallas kernels: 7.45 us -> 8.26 us  [the longest x2 4.27 us: on_device(): pl.pallas_call(functools.partial(forward_z, c), in_specs=[VM] * (4 + len(...]
  transfers between devices with their start and end apart: 21 -> 21, of which waited for: 9 -> 8; matrix products, arithmetic and copies ran while one was open for 0% -> 0% of each run, Pallas kernels for 13% -> 15%
where the time goes in v5:
time: 104 us
  starting transfers between devices  50.2 us (48%)
  Pallas kernels  22.3 us (21%)
  blocking collectives  16.1 us (15%)
  waiting for transfers between devices  11.3 us (11%)
  local copies, waits for them, and re-layouts  3.25 us (3%)
    ppermute x2, starting transfers between devices, on_device(): two = [lax.ppermute(s, 'px', pair) for s in one]  37.7 us
    all_to_all x1, blocking collectives, on_device(): lax.all_to_all(jnp.broadcast_to(sums[None], (ring, 4, w)), 'px', 0, 0, ti...  16.1 us
    ppermute x8, starting transfers between devices, on_device(): recv = lax.ppermute(s, 'px', route)  6.62 us
    ppermute x8, waiting for transfers between devices, on_device(): recv = lax.ppermute(s, 'px', route)  4.91 us
    pallas_call x2, Pallas kernels, on_device(): pl.pallas_call(functools.partial(inverse_x, h), in_specs=[VM] * (3 + 2 *...  4.62 us
    pallas_call x2, Pallas kernels, on_device(): pl.pallas_call(functools.partial(forward_z, c), in_specs=[VM] * (4 + len(...  4.27 us
    ppermute x2, waiting for transfers between devices, on_device(): near = [lax.ppermute(s, 'px', pair) for s in sends]  3.82 us
    pallas_call x4, Pallas kernels, on_device(): pl.pallas_call(functools.partial(inverse_z, c, h), in_specs=[VM] * 4, out...  3.65 us
  transfers between devices with their start and end apart: 21, of which 8 were waited for; matrix products, arithmetic and copies ran while one was open for 0% of the time, Pallas kernels for 15%

profile of v5, /device:TPU:86, one launch (start us, length us, event | category | flops | bytes accessed | tf_op | source)
XLA Modules:
  0.0 103.7 jit_solution(8335252475888697897)
XLA Ops:
  0.0 2.3 %copy-done.1 = f32[2,256,16,128]{3,2,1,0:T(8,128)S(1)} copy-done((f32[2,256,16,128]{3,2,1,0:T(8,128)S(1)}, f32[2,256,16,128]{3,2,1,0:T(8,128)}, u32[]{:S(2)}) %copy-start.1) | copy-done | bytes 4194328
  2.3 0.9 copy-done.3
  3.2 2.3 %forward_x.2 = (f32[2,16,64,128]{3,2,1,0:T(8,128)S(1)}, f32[2,16,64,128]{3,2,1,0:T(8,128)S(1)}, bf16[2,2,512,1024]{3,2,1,0:T(8,128)(2,1)S(1)}) custom-call(bf16[2,256,256]{2,1,0:T(8,128)(2,1)S(1)} %copy-done.3, f32[2,256,16,128]{3,2,1,0:T(8,128)S(1)} %copy-done.1), custom_call_target="tpu_custom_call" | custom-call | flops 805306368 | bytes 4194304 | tf_op jit(solution)/shard_map/forward_x/pallas_call | solution.py:402
  5.6 0.1 collective-permute-start
  5.7 1.0 forward_x.3
  6.7 0.6 collective-permute-start.8
  7.3 1.0 %collective-permute-done.recv = f32[2,16,64,128]{3,2,1,0:T(8,128)S(1)} collective-permute-done((f32[2,16,64,128]{3,2,1,0:T(8,128)S(1)}, f32[2,16,64,128]{3,2,1,0:T(8,128)S(1)}, u32[]{:S(2)}, u32[]{:S(2)}) %collective-permute-start) | collective-permute-done | bytes 1048608 | tf_op jit(solution)/shard_map/ppermute | solution.py:412
  8.3 1.9 %forward_z.2 = (f32[2,8,64,256]{3,2,1,0:T(8,128)S(1)}, f32[2,8,64,256]{3,2,1,0:T(8,128)S(1)}, f32[4,64,256]{2,1,0:T(8,128)S(1)}, f32[2,64,256]{2,1,0:T(8,128)S(1)}, f32[8,128]{1,0:T(8,128)S(1)}) custom-call(bf16[2,256,256]{2,1,0:T(8,128)(2,1)S(1)} %copy-done.4, f32[4,256,256]{2,1,0:T(8,128)S(1)} %copy-done, f32[2,16,64,128]{3,2,1,0:T(8,128)S(1)} %get-tuple-element.44.keep, ...), custom_call_target="tpu_custom_call" | custom-call | flops 805306368 | bytes 4194304 | tf_op jit(solution)/shard_map/forward_z/pallas_call | solution.py:415
  10.2 2.2 %collective-permute-start.1 = (f32[2,64,256]{2,1,0:T(8,128)S(1)}, f32[2,64,256]{2,1,0:T(8,128)S(1)}, u32[]{:S(2)}, u32[]{:S(2)}) collective-permute-start(f32[2,64,256]{2,1,0:T(8,128)S(1)} %get-tuple-element.47), channel_id=1, source_target_pairs={{0,2},{4,6},{8,10},{12,14},{16,18},{20,22},{24,26},{28,30},{30,28}... | collective-permute-start | bytes 393224 | tf_op jit(solution)/shard_map/ppermute | solution.py:460
  12.4 0.0 collective-permute-done.8.recv
  12.4 2.4 %forward_z.3 = (f32[2,8,64,256]{3,2,1,0:T(8,128)S(1)}, f32[2,8,64,256]{3,2,1,0:T(8,128)S(1)}, f32[4,64,256]{2,1,0:T(8,128)S(1)}, f32[2,64,256]{2,1,0:T(8,128)S(1)}, f32[8,128]{1,0:T(8,128)}) custom-call(bf16[2,256,256]{2,1,0:T(8,128)(2,1)S(1)} %copy-done.4, f32[4,256,256]{2,1,0:T(8,128)S(1)} %copy-done, f32[2,16,64,128]{3,2,1,0:T(8,128)S(1)} %get-tuple-element.57.keep, ...), custom_call_target="tpu_custom_call" | custom-call | flops 805306368 | bytes 4194304 | tf_op jit(solution)/shard_map/forward_z/pallas_call | solution.py:415
  14.9 0.0 collective-permute-start.9
  14.9 1.3 %collective-permute-done.1.recv.near = f32[2,64,256]{2,1,0:T(8,128)S(1)} collective-permute-done((f32[2,64,256]{2,1,0:T(8,128)S(1)}, f32[2,64,256]{2,1,0:T(8,128)S(1)}, u32[]{:S(2)}, u32[]{:S(2)}) %collective-permute-start.1) | collective-permute-done | bytes 131104 | tf_op jit(solution)/shard_map/ppermute | solution.py:460
  16.3 0.1 fold.10
  16.3 1.3 %collective-permute-start.2 = (f32[2,64,256]{2,1,0:T(8,128)S(1)}, f32[2,64,256]{2,1,0:T(8,128)S(1)}, u32[]{:S(2)}, u32[]{:S(2)}) collective-permute-start(f32[2,64,256]{2,1,0:T(8,128)S(1)} %get-tuple-element.48.now), channel_id=1, source_target_pairs={{2,6},{10,14},{18,22},{26,30},{28,24},{20,16},{12,8},{4,0},{3,7},{... | collective-permute-start | bytes 393224 | tf_op jit(solution)/shard_map/ppermute | solution.py:470
  17.6 2.5 %collective-permute-done.9.recv.near = f32[2,64,256]{2,1,0:T(8,128)S(1)} collective-permute-done((f32[2,64,256]{2,1,0:T(8,128)S(1)}, f32[2,64,256]{2,1,0:T(8,128)S(1)}, u32[]{:S(2)}, u32[]{:S(2)}) %collective-permute-start.9) | collective-permute-done | bytes 131104 | tf_op jit(solution)/shard_map/ppermute | solution.py:460
  20.1 0.6 fold.15
  20.7 1.3 %collective-permute-start.10 = (f32[2,64,256]{2,1,0:T(8,128)S(1)}, f32[2,64,256]{2,1,0:T(8,128)S(1)}, u32[]{:S(2)}, u32[]{:S(2)}) collective-permute-start(f32[2,64,256]{2,1,0:T(8,128)S(1)} %get-tuple-element.63.now), channel_id=1, source_target_pairs={{2,6},{10,14},{18,22},{26,30},{28,24},{20,16},{12,8},{4,0},{3,7},{... | collective-permute-start | bytes 393224 | tf_op jit(solution)/shard_map/ppermute | solution.py:470
  22.0 2.5 %collective-permute-done.2.refs_0_ = f32[2,64,256]{2,1,0:T(8,128)S(1)} collective-permute-done((f32[2,64,256]{2,1,0:T(8,128)S(1)}, f32[2,64,256]{2,1,0:T(8,128)S(1)}, u32[]{:S(2)}, u32[]{:S(2)}) %collective-permute-start.2) | collective-permute-done | bytes 131104 | tf_op jit(solution)/shard_map/ppermute | solution.py:470
  24.5 0.1 fold.11.now
  24.6 0.7 collective-permute-start.3
  25.3 0.9 local_solve.2
  26.2 2.4 %collective-permute-done.10.refs_0_ = f32[2,64,256]{2,1,0:T(8,128)S(1)} collective-permute-done((f32[2,64,256]{2,1,0:T(8,128)S(1)}, f32[2,64,256]{2,1,0:T(8,128)S(1)}, u32[]{:S(2)}, u32[]{:S(2)}) %collective-permute-start.10) | collective-permute-done | bytes 131104 | tf_op jit(solution)/shard_map/ppermute | solution.py:470
  28.6 0.1 fold.16.now
  28.7 0.7 collective-permute-start.11
  29.4 0.0 collective-permute-done.3.refs_0_
  29.4 0.1 fold.12.now
  29.5 0.7 collective-permute-start.4
  30.2 0.9 local_solve.3
  31.1 0.1 fold.17.now
  31.2 0.7 collective-permute-start.12
  31.9 0.1 fold.13.now
  32.0 0.7 collective-permute-start.5
  32.7 0.1 fold.18.now
  32.8 0.7 collective-permute-start.13
  33.5 0.0 collective-permute-done.5.refs_0_
  33.5 0.1 fold.14
  33.6 0.7 collective-permute-start.6
  34.3 0.1 fold.19
  34.4 0.7 collective-permute-start.14
  35.1 33.7 %collective-permute-start.7 = (f32[2,64,256]{2,1,0:T(8,128)S(1)}, f32[2,64,256]{2,1,0:T(8,128)S(1)}, u32[]{:S(2)}, u32[]{:S(2)}) collective-permute-start(f32[2,64,256]{2,1,0:T(8,128)S(1)} %collective-permute-done.6.one), channel_id=1, source_target_pairs={{0,2},{4,6},{8,10},{12,14},{16,18},{20,22},{24,26},{28,30},{30,28}... | collective-permute-start | bytes 393224 | tf_op jit(solution)/shard_map/ppermute | solution.py:475
  68.7 4.1 %collective-permute-start.15 = (f32[2,64,256]{2,1,0:T(8,128)S(1)}, f32[2,64,256]{2,1,0:T(8,128)S(1)}, u32[]{:S(2)}, u32[]{:S(2)}) collective-permute-start(f32[2,64,256]{2,1,0:T(8,128)S(1)} %collective-permute-done.14.one), channel_id=1, source_target_pairs={{0,2},{4,6},{8,10},{12,14},{16,18},{20,22},{24,26},{28,30},{30,28}... | collective-permute-start | bytes 393224 | tf_op jit(solution)/shard_map/ppermute | solution.py:475
  72.8 0.4 carries.2.fb
  73.2 0.9 inverse_z.6
  74.1 0.3 collective-permute-start.18
  74.5 0.9 inverse_z.4
  75.4 0.0 copy-start.2
  75.4 0.0 copy-start.5
  75.4 0.3 collective-permute-done.15.two
  75.7 0.4 carries.3.fb
  76.2 0.9 inverse_z.7
  77.1 0.3 collective-permute-start.19
  77.4 0.3 collective-permute-start.16
  77.7 0.9 inverse_z.5
  78.6 0.3 collective-permute-start.17
  78.9 0.2 collective-permute-done.19.refs_3_
  79.1 2.3 %inverse_x.3 = (f32[2,256,8,128]{3,2,1,0:T(8,128)S(1)}, f32[4,128]{1,0:T(4,128)S(1)}) custom-call(bf16[2,256,256]{2,1,0:T(8,128)(2,1)S(1)} %copy-done.4, f32[2,8,64,128]{3,2,1,0:T(8,128)S(1)} %get-tuple-element.75.refs_0_, f32[2,8,64,128]{3,2,1,0:T(8,128)S(1)} %get-tuple-element.77.refs_1_, f32[2,8,64,128]{3,2,1,0:T(8,128)S(1)} %collective-permute-done.18.refs_2_, ...), custom_call_target="tpu_custom_call" | custom-call | flops 805306368 | bytes 4194304 | tf_op jit(solution)/shard_map/inverse_x/pallas_call | solution.py:497
  81.4 0.0 collective-permute-done.16.refs_2_
  81.5 0.0 collective-permute-done.17.refs_3_
  81.5 2.3 %inverse_x.2 = (f32[2,256,8,128]{3,2,1,0:T(8,128)S(1)}, f32[4,128]{1,0:T(4,128)S(1)}) custom-call(bf16[2,256,256]{2,1,0:T(8,128)(2,1)S(1)} %copy-done.4, f32[2,8,64,128]{3,2,1,0:T(8,128)S(1)} %get-tuple-element.55.refs_0_, f32[2,8,64,128]{3,2,1,0:T(8,128)S(1)} %get-tuple-element.70.refs_1_, f32[2,8,64,128]{3,2,1,0:T(8,128)S(1)} %collective-permute-done.16.refs_2_, ...), custom_call_target="tpu_custom_call" | custom-call | flops 805306368 | bytes 4194304 | tf_op jit(solution)/shard_map/inverse_x/pallas_call | solution.py:497
  83.8 0.3 collective-permute-start.20
  84.1 1.0 collective-permute-done.20
  85.1 16.1 %all_to_all.5.total = f32[16,4,128]{2,1,0:T(4,128)S(1)} all-to-all(f32[16,4,128]{2,1,0:T(4,128)S(1)} %broadcast_in_dim.2), channel_id=1, replica_groups=mesh['samples'=4,'px'=16,'py'=2] {'px'}, dimensions={0} | all-to-all | bytes 65536 | tf_op jit(solution)/shard_map/all_to_all | solution.py:510
  101.2 2.3 %finish.1 = f32[2,256,16,128]{3,2,1,0:T(8,128)} custom-call(f32[16,4,128]{2,1,0:T(4,128)S(1)} %all_to_all.5.total, f32[2,256,8,128]{3,2,1,0:T(8,128)S(1)} %get-tuple-element.81.ps0, f32[2,256,8,128]{3,2,1,0:T(8,128)S(1)} %get-tuple-element.82.ps1), custom_call_target="tpu_custom_call" | custom-call | flops 10000000 | bytes 8388608 | tf_op jit(solution)/shard_map/finish/pallas_call | solution.py:511
  (19 shorter events, 0.1 us)
Async XLA Ops:
  0.0 8.3 %copy-start = (f32[4,256,256]{2,1,0:T(8,128)S(1)}, f32[4,256,256]{2,1,0:T(8,128)}, u32[]{:S(2)}) copy-start(f32[4,256,256]{2,1,0:T(8,128)} %constant.5.clone.root) | copy-start | bytes 3145732
  0.0 2.3 %copy-start.1 = (f32[2,256,16,128]{3,2,1,0:T(8,128)S(1)}, f32[2,256,16,128]{3,2,1,0:T(8,128)}, u32[]{:S(2)}) copy-start(f32[2,256,16,128]{3,2,1,0:T(8,128)} %refs_4_.3) | copy-start | bytes 12582916
  2.3 0.9 copy-start.3
  3.2 5.1 %copy-start.4 = (bf16[2,256,256]{2,1,0:T(8,128)(2,1)S(1)}, bf16[2,256,256]{2,1,0:T(8,128)(2,1)}, u32[]{:S(2)}) copy-start(bf16[2,256,256]{2,1,0:T(8,128)(2,1)} %constant.4.clone.s_ref) | copy-start | bytes 786436
  5.6 2.8 %collective-permute-start = (f32[2,16,64,128]{3,2,1,0:T(8,128)S(1)}, f32[2,16,64,128]{3,2,1,0:T(8,128)S(1)}, u32[]{:S(2)}, u32[]{:S(2)}) collective-permute-start(f32[2,16,64,128]{3,2,1,0:T(8,128)S(1)} %get-tuple-element.45), channel_id=1, source_target_pairs={{0,1},{1,0},{2,3},{3,2},{4,5},{5,4},{6,7},{7,6},{8,9},{9,8},{10,11... | collective-permute-start | bytes 3145736 | tf_op jit(solution)/shard_map/ppermute | solution.py:412
  6.7 5.7 %collective-permute-start.8 = (f32[2,16,64,128]{3,2,1,0:T(8,128)S(1)}, f32[2,16,64,128]{3,2,1,0:T(8,128)S(1)}, u32[]{:S(2)}, u32[]{:S(2)}) collective-permute-start(f32[2,16,64,128]{3,2,1,0:T(8,128)S(1)} %get-tuple-element.58), channel_id=1, source_target_pairs={{0,1},{1,0},{2,3},{3,2},{4,5},{5,4},{6,7},{7,6},{8,9},{9,8},{10,11... | collective-permute-start | bytes 3145736 | tf_op jit(solution)/shard_map/ppermute | solution.py:412
  10.2 6.0 %collective-permute-start.1 = (f32[2,64,256]{2,1,0:T(8,128)S(1)}, f32[2,64,256]{2,1,0:T(8,128)S(1)}, u32[]{:S(2)}, u32[]{:S(2)}) collective-permute-start(f32[2,64,256]{2,1,0:T(8,128)S(1)} %get-tuple-element.47), channel_id=1, source_target_pairs={{0,2},{4,6},{8,10},{12,14},{16,18},{20,22},{24,26},{28,30},{30,28}... | collective-permute-start | bytes 393224 | tf_op jit(solution)/shard_map/ppermute | solution.py:460
  14.9 5.3 %collective-permute-start.9 = (f32[2,64,256]{2,1,0:T(8,128)S(1)}, f32[2,64,256]{2,1,0:T(8,128)S(1)}, u32[]{:S(2)}, u32[]{:S(2)}) collective-permute-start(f32[2,64,256]{2,1,0:T(8,128)S(1)} %get-tuple-element.61), channel_id=1, source_target_pairs={{0,2},{4,6},{8,10},{12,14},{16,18},{20,22},{24,26},{28,30},{30,28}... | collective-permute-start | bytes 393224 | tf_op jit(solution)/shard_map/ppermute | solution.py:460
  16.3 8.2 %collective-permute-start.2 = (f32[2,64,256]{2,1,0:T(8,128)S(1)}, f32[2,64,256]{2,1,0:T(8,128)S(1)}, u32[]{:S(2)}, u32[]{:S(2)}) collective-permute-start(f32[2,64,256]{2,1,0:T(8,128)S(1)} %get-tuple-element.48.now), channel_id=1, source_target_pairs={{2,6},{10,14},{18,22},{26,30},{28,24},{20,16},{12,8},{4,0},{3,7},{... | collective-permute-start | bytes 393224 | tf_op jit(solution)/shard_map/ppermute | solution.py:470
  20.7 7.9 %collective-permute-start.10 = (f32[2,64,256]{2,1,0:T(8,128)S(1)}, f32[2,64,256]{2,1,0:T(8,128)S(1)}, u32[]{:S(2)}, u32[]{:S(2)}) collective-permute-start(f32[2,64,256]{2,1,0:T(8,128)S(1)} %get-tuple-element.63.now), channel_id=1, source_target_pairs={{2,6},{10,14},{18,22},{26,30},{28,24},{20,16},{12,8},{4,0},{3,7},{... | collective-permute-start | bytes 393224 | tf_op jit(solution)/shard_map/ppermute | solution.py:470
  24.6 4.8 %collective-permute-start.3 = (f32[2,64,256]{2,1,0:T(8,128)S(1)}, f32[2,64,256]{2,1,0:T(8,128)S(1)}, u32[]{:S(2)}, u32[]{:S(2)}) collective-permute-start(f32[2,64,256]{2,1,0:T(8,128)S(1)} %fold.11.now), channel_id=1, source_target_pairs={{6,14},{24,16},{7,15},{25,17},{38,46},{56,48},{39,47},{57,49},{70,... | collective-permute-start | bytes 393224 | tf_op jit(solution)/shard_map/ppermute | solution.py:470
  28.7 2.4 %collective-permute-start.11 = (f32[2,64,256]{2,1,0:T(8,128)S(1)}, f32[2,64,256]{2,1,0:T(8,128)S(1)}, u32[]{:S(2)}, u32[]{:S(2)}) collective-permute-start(f32[2,64,256]{2,1,0:T(8,128)S(1)} %fold.16.now), channel_id=1, source_target_pairs={{6,14},{24,16},{7,15},{25,17},{38,46},{56,48},{39,47},{57,49},{70,... | collective-permute-start | bytes 393224 | tf_op jit(solution)/shard_map/ppermute | solution.py:470
  29.5 2.4 %collective-permute-start.4 = (f32[2,64,256]{2,1,0:T(8,128)S(1)}, f32[2,64,256]{2,1,0:T(8,128)S(1)}, u32[]{:S(2)}, u32[]{:S(2)}) collective-permute-start(f32[2,64,256]{2,1,0:T(8,128)S(1)} %fold.12.now), channel_id=1, source_target_pairs={{14,22},{16,8},{15,23},{17,9},{46,54},{48,40},{47,55},{49,41},{78,... | collective-permute-start | bytes 393224 | tf_op jit(solution)/shard_map/ppermute | solution.py:470
  31.2 1.5 %collective-permute-start.12 = (f32[2,64,256]{2,1,0:T(8,128)S(1)}, f32[2,64,256]{2,1,0:T(8,128)S(1)}, u32[]{:S(2)}, u32[]{:S(2)}) collective-permute-start(f32[2,64,256]{2,1,0:T(8,128)S(1)} %fold.17.now), channel_id=1, source_target_pairs={{14,22},{16,8},{15,23},{17,9},{46,54},{48,40},{47,55},{49,41},{78,... | collective-permute-start | bytes 393224 | tf_op jit(solution)/shard_map/ppermute | solution.py:470
  32.0 1.5 %collective-permute-start.5 = (f32[2,64,256]{2,1,0:T(8,128)S(1)}, f32[2,64,256]{2,1,0:T(8,128)S(1)}, u32[]{:S(2)}, u32[]{:S(2)}) collective-permute-start(f32[2,64,256]{2,1,0:T(8,128)S(1)} %fold.13.now), channel_id=1, source_target_pairs={{6,10},{14,18},{22,26},{24,20},{16,12},{8,4},{7,11},{15,19},{23,27... | collective-permute-start | bytes 393224 | tf_op jit(solution)/shard_map/ppermute | solution.py:470
  32.8 1.5 %collective-permute-start.13 = (f32[2,64,256]{2,1,0:T(8,128)S(1)}, f32[2,64,256]{2,1,0:T(8,128)S(1)}, u32[]{:S(2)}, u32[]{:S(2)}) collective-permute-start(f32[2,64,256]{2,1,0:T(8,128)S(1)} %fold.18.now), channel_id=1, source_target_pairs={{6,10},{14,18},{22,26},{24,20},{16,12},{8,4},{7,11},{15,19},{23,27... | collective-permute-start | bytes 393224 | tf_op jit(solution)/shard_map/ppermute | solution.py:470
  33.6 1.5 %collective-permute-start.6 = (f32[2,64,256]{2,1,0:T(8,128)S(1)}, f32[2,64,256]{2,1,0:T(8,128)S(1)}, u32[]{:S(2)}, u32[]{:S(2)}) collective-permute-start(f32[2,64,256]{2,1,0:T(8,128)S(1)} %fold.14), channel_id=1, source_target_pairs={{2,4},{6,8},{10,12},{14,16},{18,20},{22,24},{26,28},{28,26},{24,22... | collective-permute-start | bytes 393224 | tf_op jit(solution)/shard_map/ppermute | solution.py:474
  34.4 34.4 %collective-permute-start.14 = (f32[2,64,256]{2,1,0:T(8,128)S(1)}, f32[2,64,256]{2,1,0:T(8,128)S(1)}, u32[]{:S(2)}, u32[]{:S(2)}) collective-permute-start(f32[2,64,256]{2,1,0:T(8,128)S(1)} %fold.19), channel_id=1, source_target_pairs={{2,4},{6,8},{10,12},{14,16},{18,20},{22,24},{26,28},{28,26},{24,22... | collective-permute-start | bytes 393224 | tf_op jit(solution)/shard_map/ppermute | solution.py:474
  35.1 37.7 %collective-permute-start.7 = (f32[2,64,256]{2,1,0:T(8,128)S(1)}, f32[2,64,256]{2,1,0:T(8,128)S(1)}, u32[]{:S(2)}, u32[]{:S(2)}) collective-permute-start(f32[2,64,256]{2,1,0:T(8,128)S(1)} %collective-permute-done.6.one), channel_id=1, source_target_pairs={{0,2},{4,6},{8,10},{12,14},{16,18},{20,22},{24,26},{28,30},{30,28}... | collective-permute-start | bytes 393224 | tf_op jit(solution)/shard_map/ppermute | solution.py:475
  68.7 7.0 %collective-permute-start.15 = (f32[2,64,256]{2,1,0:T(8,128)S(1)}, f32[2,64,256]{2,1,0:T(8,128)S(1)}, u32[]{:S(2)}, u32[]{:S(2)}) collective-permute-start(f32[2,64,256]{2,1,0:T(8,128)S(1)} %collective-permute-done.14.one), channel_id=1, source_target_pairs={{0,2},{4,6},{8,10},{12,14},{16,18},{20,22},{24,26},{28,30},{30,28}... | collective-permute-start | bytes 393224 | tf_op jit(solution)/shard_map/ppermute | solution.py:475
  74.1 4.8 %collective-permute-start.18 = (f32[2,8,64,128]{3,2,1,0:T(8,128)S(1)}, f32[2,8,64,128]{3,2,1,0:T(8,128)S(1)}, u32[]{:S(2)}, u32[]{:S(2)}) collective-permute-start(f32[2,8,64,128]{3,2,1,0:T(8,128)S(1)} %get-tuple-element.78), channel_id=1, source_target_pairs={{0,1},{1,0},{2,3},{3,2},{4,5},{5,4},{6,7},{7,6},{8,9},{9,8},{10,11... | collective-permute-start | bytes 1572872 | tf_op jit(solution)/shard_map/ppermute | solution.py:494
  75.4 3.7 %copy-start.2 = (f32[2,256,16,128]{3,2,1,0:T(8,128)S(1)}, f32[2,256,16,128]{3,2,1,0:T(8,128)}, u32[]{:S(2)}) copy-start(f32[2,256,16,128]{3,2,1,0:T(8,128)} %refs_4_.3) | copy-start | bytes 12582916
  75.4 3.7 %copy-start.5 = (f32[256,16,128]{2,1,0:T(8,128)S(1)}, f32[256,16,128]{2,1,0:T(8,128)}, u32[]{:S(2)}) copy-start(f32[256,16,128]{2,1,0:T(8,128)} %refs_5_.3) | copy-start | bytes 6291460
  77.1 2.0 %collective-permute-start.19 = (f32[2,8,64,128]{3,2,1,0:T(8,128)S(1)}, f32[2,8,64,128]{3,2,1,0:T(8,128)S(1)}, u32[]{:S(2)}, u32[]{:S(2)}) collective-permute-start(f32[2,8,64,128]{3,2,1,0:T(8,128)S(1)} %get-tuple-element.79), channel_id=1, source_target_pairs={{0,1},{1,0},{2,3},{3,2},{4,5},{5,4},{6,7},{7,6},{8,9},{9,8},{10,11... | collective-permute-start | bytes 1572872 | tf_op jit(solution)/shard_map/ppermute | solution.py:494
  77.4 4.1 %collective-permute-start.16 = (f32[2,8,64,128]{3,2,1,0:T(8,128)S(1)}, f32[2,8,64,128]{3,2,1,0:T(8,128)S(1)}, u32[]{:S(2)}, u32[]{:S(2)}) collective-permute-start(f32[2,8,64,128]{3,2,1,0:T(8,128)S(1)} %get-tuple-element.71), channel_id=1, source_target_pairs={{0,1},{1,0},{2,3},{3,2},{4,5},{5,4},{6,7},{7,6},{8,9},{9,8},{10,11... | collective-permute-start | bytes 1572872 | tf_op jit(solution)/shard_map/ppermute | solution.py:494
  78.6 2.8 %collective-permute-start.17 = (f32[2,8,64,128]{3,2,1,0:T(8,128)S(1)}, f32[2,8,64,128]{3,2,1,0:T(8,128)S(1)}, u32[]{:S(2)}, u32[]{:S(2)}) collective-permute-start(f32[2,8,64,128]{3,2,1,0:T(8,128)S(1)} %get-tuple-element.72), channel_id=1, source_target_pairs={{0,1},{1,0},{2,3},{3,2},{4,5},{5,4},{6,7},{7,6},{8,9},{9,8},{10,11... | collective-permute-start | bytes 1572872 | tf_op jit(solution)/shard_map/ppermute | solution.py:494
  83.8 1.3 %collective-permute-start.20 = (f32[4,128]{1,0:T(4,128)S(1)}, f32[4,128]{1,0:T(4,128)S(1)}, u32[]{:S(2)}, u32[]{:S(2)}) collective-permute-start(f32[4,128]{1,0:T(4,128)S(1)} %add.6), channel_id=1, source_target_pairs={{0,1},{1,0},{2,3},{3,2},{4,5},{5,4},{6,7},{7,6},{8,9},{9,8},{10,11... | collective-permute-start | bytes 6152 | tf_op jit(solution)/shard_map/ppermute | solution.py:509

commit v6 on v5

--- a/solution.py
+++ b/solution.py
@@ -70,22 +70,37 @@
     return jnp.where(first, keep, recv), jnp.where(first, recv, keep)
 
 
-def forward_x(chunk, s_ref, values, send, keep, *parts):
+def forward_x_first(s_hbm, src_hbm, send, keep, parts, s_ref, values, sems):
+    copies = [pltpu.make_async_copy(s_hbm, s_ref, sems.at[0])]
+    for h in range(2):
+        for c in range(2):
+            rows = pl.ds(h * YB, YB)
+            copies.append(pltpu.make_async_copy(src_hbm.at[c, :, rows, :], values.at[h, c], sems.at[1 + 2 * h + c]))
+    for copy in copies:
+        copy.start()
+    forward_x(0, s_ref, values, send, keep, parts, copies=copies)
+
+
+def forward_x(chunk, s_ref, values, send, keep, *parts, copies=()):
     me = lax.axis_index("py")
     _, ny, kc, w = send.shape
     nx = s_ref.shape[1]
     for h in range(ny // YB):
         for c in range(2):
             if parts:
-                flat = values.at[c].reshape(nx * ny, w)
+                if copies:
+                    copies[1 + 2 * h + c].wait()
+                flat = values.at[h, c].reshape(nx * YB, w)
                 cols = []
                 for y in range(YB):
-                    cols.append(jnp.concatenate(split(flat[pl.ds(h * YB + y, nx, stride=ny), :]), axis=0))
+                    cols.append(jnp.concatenate(split(flat[pl.ds(y, nx, stride=YB), :]), axis=0))
                 both = jnp.concatenate(cols, axis=1)
                 parts[0][c, h] = both
             else:
                 both = values[c, h]
             right = jnp.concatenate([both, both[:nx]], axis=0)
+            if copies and not h and not c:
+                copies[0].wait()
             left = []
             for half in (1 - me, me):
                 rows = pl.ds(pl.multiple_of(half * (nx // 2) + chunk * kc, kc), kc)
@@ -400,11 +415,17 @@
     for c in range(CHUNKS):
         first = c == 0
         send, keep, *left = pl.pallas_call(
-            functools.partial(forward_x, c),
-            in_specs=[VM] * 2,
+            forward_x_first if first else functools.partial(forward_x, c),
+            in_specs=[ANY if first else VM] * 2,
             out_specs=[VM] * (2 + first),
             out_shape=[piece, piece] + [parts] * first,
-            compiler_params=params(16),
+            scratch_shapes=[
+                pltpu.VMEM(table_x.shape, bf16),
+                pltpu.VMEM((2, 2, nx, YB, w), f32),
+                pltpu.SemaphoreType.DMA((5,)),
+            ]
+            * first,
+            compiler_params=params(45 if first else 16),
             cost_estimate=est,
             name="forward_x",
         )(table_x, values)

time: 104 us -> 103 us (level)
  local copies, waits for them, and re-layouts: 3.25 us -> 1.06 us
  Pallas kernels: 22.3 us -> 23.6 us
    unnamed x12 -> x8, local copies, waits for them, and re-layouts: 3.25 us -> 1.05 us
    pallas_call x2, Pallas kernels: 3.31 us -> 4.53 us  [on_device(): pl.pallas_call(forward_x_first if first else functools.partial(forward_x,...]
where the time goes in v6:
time: 103 us
  starting transfers between devices  50.3 us (49%)
  Pallas kernels  23.6 us (23%)
  blocking collectives  16.2 us (16%)
  waiting for transfers between devices  11.2 us (11%)
  local copies, waits for them, and re-layouts  1.06 us (1%)
    ppermute x2, starting transfers between devices, on_device(): two = [lax.ppermute(s, 'px', pair) for s in one]  37.7 us
    all_to_all x1, blocking collectives, on_device(): lax.all_to_all(jnp.broadcast_to(sums[None], (ring, 4, w)), 'px', 0, 0, ti...  16.2 us
    ppermute x8, starting transfers between devices, on_device(): recv = lax.ppermute(s, 'px', route)  6.62 us
    ppermute x8, waiting for transfers between devices, on_device(): recv = lax.ppermute(s, 'px', route)  4.9 us
    pallas_call x2, Pallas kernels, on_device(): pl.pallas_call(functools.partial(inverse_x, h), in_specs=[VM] * (3 + 2 *...  4.67 us
    pallas_call x2, Pallas kernels, on_device(): pl.pallas_call(forward_x_first if first else functools.partial(forward_x,...  4.53 us
    pallas_call x2, Pallas kernels, on_device(): pl.pallas_call(functools.partial(forward_z, c), in_specs=[VM] * (4 + len(...  4.26 us
    ppermute x2, waiting for transfers between devices, on_device(): near = [lax.ppermute(s, 'px', pair) for s in sends]  3.82 us
  transfers between devices with their start and end apart: 21, of which 8 were waited for; matrix products, arithmetic and copies ran while one was open for 0% of the time, Pallas kernels for 15%

profile of v6, /device:TPU:86, one launch (start us, length us, event | category | flops | bytes accessed | tf_op | source)
XLA Modules:
  0.0 102.8 jit_solution(16809198040859300036)
XLA Ops:
  0.0 1.0 %copy-done.2 = bf16[2,256,256]{2,1,0:T(8,128)(2,1)S(1)} copy-done((bf16[2,256,256]{2,1,0:T(8,128)(2,1)S(1)}, bf16[2,256,256]{2,1,0:T(8,128)(2,1)}, u32[]{:S(2)}) %copy-start.2) | copy-done | bytes 262168
  1.0 3.5 %forward_x.2 = (f32[2,16,64,128]{3,2,1,0:T(8,128)S(1)}, f32[2,16,64,128]{3,2,1,0:T(8,128)S(1)}, bf16[2,2,512,1024]{3,2,1,0:T(8,128)(2,1)S(1)}) custom-call(bf16[2,256,256]{2,1,0:T(8,128)(2,1)S(1)} %copy-done.2, f32[2,256,16,128]{3,2,1,0:T(8,128)} %refs_4_.3), custom_call_target="tpu_custom_call" | custom-call | flops 805306368 | bytes 4194304 | tf_op jit(solution)/shard_map/forward_x/pallas_call | solution.py:417
  4.6 0.1 collective-permute-start
  4.7 1.0 forward_x.3
  5.7 0.6 collective-permute-start.8
  6.3 1.0 %collective-permute-done.recv = f32[2,16,64,128]{3,2,1,0:T(8,128)S(1)} collective-permute-done((f32[2,16,64,128]{3,2,1,0:T(8,128)S(1)}, f32[2,16,64,128]{3,2,1,0:T(8,128)S(1)}, u32[]{:S(2)}, u32[]{:S(2)}) %collective-permute-start) | collective-permute-done | bytes 1048608 | tf_op jit(solution)/shard_map/ppermute | solution.py:433
  7.4 1.9 %forward_z.2 = (f32[2,8,64,256]{3,2,1,0:T(8,128)S(1)}, f32[2,8,64,256]{3,2,1,0:T(8,128)S(1)}, f32[4,64,256]{2,1,0:T(8,128)S(1)}, f32[2,64,256]{2,1,0:T(8,128)S(1)}, f32[8,128]{1,0:T(8,128)S(1)}) custom-call(bf16[2,256,256]{2,1,0:T(8,128)(2,1)S(1)} %copy-done.2, f32[4,256,256]{2,1,0:T(8,128)S(1)} %copy-done, f32[2,16,64,128]{3,2,1,0:T(8,128)S(1)} %get-tuple-element.44.keep, ...), custom_call_target="tpu_custom_call" | custom-call | flops 805306368 | bytes 4194304 | tf_op jit(solution)/shard_map/forward_z/pallas_call | solution.py:436
  9.2 2.2 %collective-permute-start.1 = (f32[2,64,256]{2,1,0:T(8,128)S(1)}, f32[2,64,256]{2,1,0:T(8,128)S(1)}, u32[]{:S(2)}, u32[]{:S(2)}) collective-permute-start(f32[2,64,256]{2,1,0:T(8,128)S(1)} %get-tuple-element.47), channel_id=1, source_target_pairs={{0,2},{4,6},{8,10},{12,14},{16,18},{20,22},{24,26},{28,30},{30,28}... | collective-permute-start | bytes 393224 | tf_op jit(solution)/shard_map/ppermute | solution.py:481
  11.5 2.4 %forward_z.3 = (f32[2,8,64,256]{3,2,1,0:T(8,128)S(1)}, f32[2,8,64,256]{3,2,1,0:T(8,128)S(1)}, f32[4,64,256]{2,1,0:T(8,128)S(1)}, f32[2,64,256]{2,1,0:T(8,128)S(1)}, f32[8,128]{1,0:T(8,128)}) custom-call(bf16[2,256,256]{2,1,0:T(8,128)(2,1)S(1)} %copy-done.2, f32[4,256,256]{2,1,0:T(8,128)S(1)} %copy-done, f32[2,16,64,128]{3,2,1,0:T(8,128)S(1)} %get-tuple-element.57.keep, ...), custom_call_target="tpu_custom_call" | custom-call | flops 805306368 | bytes 4194304 | tf_op jit(solution)/shard_map/forward_z/pallas_call | solution.py:436
  13.9 0.1 collective-permute-start.9
  13.9 1.3 %collective-permute-done.1.recv.near = f32[2,64,256]{2,1,0:T(8,128)S(1)} collective-permute-done((f32[2,64,256]{2,1,0:T(8,128)S(1)}, f32[2,64,256]{2,1,0:T(8,128)S(1)}, u32[]{:S(2)}, u32[]{:S(2)}) %collective-permute-start.1) | collective-permute-done | bytes 131104 | tf_op jit(solution)/shard_map/ppermute | solution.py:481
  15.3 0.1 fold.10
  15.4 1.3 %collective-permute-start.2 = (f32[2,64,256]{2,1,0:T(8,128)S(1)}, f32[2,64,256]{2,1,0:T(8,128)S(1)}, u32[]{:S(2)}, u32[]{:S(2)}) collective-permute-start(f32[2,64,256]{2,1,0:T(8,128)S(1)} %get-tuple-element.48.now), channel_id=1, source_target_pairs={{2,6},{10,14},{18,22},{26,30},{28,24},{20,16},{12,8},{4,0},{3,7},{... | collective-permute-start | bytes 393224 | tf_op jit(solution)/shard_map/ppermute | solution.py:491
  16.7 2.5 %collective-permute-done.9.recv.near = f32[2,64,256]{2,1,0:T(8,128)S(1)} collective-permute-done((f32[2,64,256]{2,1,0:T(8,128)S(1)}, f32[2,64,256]{2,1,0:T(8,128)S(1)}, u32[]{:S(2)}, u32[]{:S(2)}) %collective-permute-start.9) | collective-permute-done | bytes 131104 | tf_op jit(solution)/shard_map/ppermute | solution.py:481
  19.1 0.6 fold.15
  19.8 1.3 %collective-permute-start.10 = (f32[2,64,256]{2,1,0:T(8,128)S(1)}, f32[2,64,256]{2,1,0:T(8,128)S(1)}, u32[]{:S(2)}, u32[]{:S(2)}) collective-permute-start(f32[2,64,256]{2,1,0:T(8,128)S(1)} %get-tuple-element.63.now), channel_id=1, source_target_pairs={{2,6},{10,14},{18,22},{26,30},{28,24},{20,16},{12,8},{4,0},{3,7},{... | collective-permute-start | bytes 393224 | tf_op jit(solution)/shard_map/ppermute | solution.py:491
  21.1 2.5 %collective-permute-done.2.refs_0_ = f32[2,64,256]{2,1,0:T(8,128)S(1)} collective-permute-done((f32[2,64,256]{2,1,0:T(8,128)S(1)}, f32[2,64,256]{2,1,0:T(8,128)S(1)}, u32[]{:S(2)}, u32[]{:S(2)}) %collective-permute-start.2) | collective-permute-done | bytes 131104 | tf_op jit(solution)/shard_map/ppermute | solution.py:491
  23.5 0.1 fold.11.now
  23.6 0.7 collective-permute-start.3
  24.3 0.9 local_solve.2
  25.2 2.4 %collective-permute-done.10.refs_0_ = f32[2,64,256]{2,1,0:T(8,128)S(1)} collective-permute-done((f32[2,64,256]{2,1,0:T(8,128)S(1)}, f32[2,64,256]{2,1,0:T(8,128)S(1)}, u32[]{:S(2)}, u32[]{:S(2)}) %collective-permute-start.10) | collective-permute-done | bytes 131104 | tf_op jit(solution)/shard_map/ppermute | solution.py:491
  27.7 0.1 fold.16.now
  27.7 0.7 collective-permute-start.11
  28.4 0.0 collective-permute-done.3.refs_0_
  28.4 0.1 fold.12.now
  28.5 0.7 collective-permute-start.4
  29.2 0.9 local_solve.3
  30.2 0.0 collective-permute-done.11.refs_0_
  30.2 0.1 fold.17.now
  30.3 0.7 collective-permute-start.12
  31.0 0.1 fold.13.now
  31.1 0.7 collective-permute-start.5
  31.7 0.1 fold.18.now
  31.8 0.7 collective-permute-start.13
  32.5 0.0 collective-permute-done.5.refs_0_
  32.5 0.1 fold.14
  32.6 0.7 collective-permute-start.6
  33.3 0.1 fold.19
  33.4 0.7 collective-permute-start.14
  34.1 33.7 %collective-permute-start.7 = (f32[2,64,256]{2,1,0:T(8,128)S(1)}, f32[2,64,256]{2,1,0:T(8,128)S(1)}, u32[]{:S(2)}, u32[]{:S(2)}) collective-permute-start(f32[2,64,256]{2,1,0:T(8,128)S(1)} %collective-permute-done.6.one), channel_id=1, source_target_pairs={{0,2},{4,6},{8,10},{12,14},{16,18},{20,22},{24,26},{28,30},{30,28}... | collective-permute-start | bytes 393224 | tf_op jit(solution)/shard_map/ppermute | solution.py:496
  67.8 0.0 collective-permute-done.14.one
  67.8 4.1 %collective-permute-start.15 = (f32[2,64,256]{2,1,0:T(8,128)S(1)}, f32[2,64,256]{2,1,0:T(8,128)S(1)}, u32[]{:S(2)}, u32[]{:S(2)}) collective-permute-start(f32[2,64,256]{2,1,0:T(8,128)S(1)} %collective-permute-done.14.one), channel_id=1, source_target_pairs={{0,2},{4,6},{8,10},{12,14},{16,18},{20,22},{24,26},{28,30},{30,28}... | collective-permute-start | bytes 393224 | tf_op jit(solution)/shard_map/ppermute | solution.py:496
  71.8 0.0 collective-permute-done.7.two
  71.8 0.4 carries.2.fb
  72.3 0.9 inverse_z.6
  73.2 0.3 collective-permute-start.18
  73.5 0.9 inverse_z.4
  74.5 0.0 copy-start.1
  74.5 0.0 copy-start.3
  74.5 0.3 collective-permute-done.15.two
  74.8 0.4 carries.3.fb
  75.2 0.9 inverse_z.7
  76.1 0.3 collective-permute-start.19
  76.4 0.3 collective-permute-start.16
  76.7 0.9 inverse_z.5
  77.7 0.3 collective-permute-start.17
  78.0 0.1 collective-permute-done.19.refs_3_
  78.1 2.3 %inverse_x.3 = (f32[2,256,8,128]{3,2,1,0:T(8,128)S(1)}, f32[4,128]{1,0:T(4,128)S(1)}) custom-call(bf16[2,256,256]{2,1,0:T(8,128)(2,1)S(1)} %copy-done.2, f32[2,8,64,128]{3,2,1,0:T(8,128)S(1)} %get-tuple-element.75.refs_0_, f32[2,8,64,128]{3,2,1,0:T(8,128)S(1)} %get-tuple-element.77.refs_1_, f32[2,8,64,128]{3,2,1,0:T(8,128)S(1)} %collective-permute-done.18.refs_2_, ...), custom_call_target="tpu_custom_call" | custom-call | flops 805306368 | bytes 4194304 | tf_op jit(solution)/shard_map/inverse_x/pallas_call | solution.py:518
  80.5 0.0 collective-permute-done.16.refs_2_
  80.5 2.3 %inverse_x.2 = (f32[2,256,8,128]{3,2,1,0:T(8,128)S(1)}, f32[4,128]{1,0:T(4,128)S(1)}) custom-call(bf16[2,256,256]{2,1,0:T(8,128)(2,1)S(1)} %copy-done.2, f32[2,8,64,128]{3,2,1,0:T(8,128)S(1)} %get-tuple-element.55.refs_0_, f32[2,8,64,128]{3,2,1,0:T(8,128)S(1)} %get-tuple-element.70.refs_1_, f32[2,8,64,128]{3,2,1,0:T(8,128)S(1)} %collective-permute-done.16.refs_2_, ...), custom_call_target="tpu_custom_call" | custom-call | flops 805306368 | bytes 4194304 | tf_op jit(solution)/shard_map/inverse_x/pallas_call | solution.py:518
  82.9 0.3 collective-permute-start.20
  83.2 0.9 collective-permute-done.20
  84.2 16.2 %all_to_all.5.total = f32[16,4,128]{2,1,0:T(4,128)S(1)} all-to-all(f32[16,4,128]{2,1,0:T(4,128)S(1)} %broadcast_in_dim.2), channel_id=1, replica_groups=mesh['samples'=4,'px'=16,'py'=2] {'px'}, dimensions={0} | all-to-all | bytes 65536 | tf_op jit(solution)/shard_map/all_to_all | solution.py:531
  100.3 2.3 %finish.1 = f32[2,256,16,128]{3,2,1,0:T(8,128)} custom-call(f32[16,4,128]{2,1,0:T(4,128)S(1)} %all_to_all.5.total, f32[2,256,8,128]{3,2,1,0:T(8,128)S(1)} %get-tuple-element.81.ps0, f32[2,256,8,128]{3,2,1,0:T(8,128)S(1)} %get-tuple-element.82.ps1), custom_call_target="tpu_custom_call" | custom-call | flops 10000000 | bytes 8388608 | tf_op jit(solution)/shard_map/finish/pallas_call | solution.py:532
  (15 shorter events, 0.0 us)
Async XLA Ops:
  0.0 7.4 %copy-start = (f32[4,256,256]{2,1,0:T(8,128)S(1)}, f32[4,256,256]{2,1,0:T(8,128)}, u32[]{:S(2)}) copy-start(f32[4,256,256]{2,1,0:T(8,128)} %constant.5.clone.root) | copy-start | bytes 3145732
  0.0 1.0 %copy-start.2 = (bf16[2,256,256]{2,1,0:T(8,128)(2,1)S(1)}, bf16[2,256,256]{2,1,0:T(8,128)(2,1)}, u32[]{:S(2)}) copy-start(bf16[2,256,256]{2,1,0:T(8,128)(2,1)} %constant.4.clone.s_hbm.s_ref) | copy-start | bytes 786436
  4.6 2.8 %collective-permute-start = (f32[2,16,64,128]{3,2,1,0:T(8,128)S(1)}, f32[2,16,64,128]{3,2,1,0:T(8,128)S(1)}, u32[]{:S(2)}, u32[]{:S(2)}) collective-permute-start(f32[2,16,64,128]{3,2,1,0:T(8,128)S(1)} %get-tuple-element.45), channel_id=1, source_target_pairs={{0,1},{1,0},{2,3},{3,2},{4,5},{5,4},{6,7},{7,6},{8,9},{9,8},{10,11... | collective-permute-start | bytes 3145736 | tf_op jit(solution)/shard_map/ppermute | solution.py:433
  5.7 5.7 %collective-permute-start.8 = (f32[2,16,64,128]{3,2,1,0:T(8,128)S(1)}, f32[2,16,64,128]{3,2,1,0:T(8,128)S(1)}, u32[]{:S(2)}, u32[]{:S(2)}) collective-permute-start(f32[2,16,64,128]{3,2,1,0:T(8,128)S(1)} %get-tuple-element.58), channel_id=1, source_target_pairs={{0,1},{1,0},{2,3},{3,2},{4,5},{5,4},{6,7},{7,6},{8,9},{9,8},{10,11... | collective-permute-start | bytes 3145736 | tf_op jit(solution)/shard_map/ppermute | solution.py:433
  9.2 6.0 %collective-permute-start.1 = (f32[2,64,256]{2,1,0:T(8,128)S(1)}, f32[2,64,256]{2,1,0:T(8,128)S(1)}, u32[]{:S(2)}, u32[]{:S(2)}) collective-permute-start(f32[2,64,256]{2,1,0:T(8,128)S(1)} %get-tuple-element.47), channel_id=1, source_target_pairs={{0,2},{4,6},{8,10},{12,14},{16,18},{20,22},{24,26},{28,30},{30,28}... | collective-permute-start | bytes 393224 | tf_op jit(solution)/shard_map/ppermute | solution.py:481
  13.9 5.3 %collective-permute-start.9 = (f32[2,64,256]{2,1,0:T(8,128)S(1)}, f32[2,64,256]{2,1,0:T(8,128)S(1)}, u32[]{:S(2)}, u32[]{:S(2)}) collective-permute-start(f32[2,64,256]{2,1,0:T(8,128)S(1)} %get-tuple-element.61), channel_id=1, source_target_pairs={{0,2},{4,6},{8,10},{12,14},{16,18},{20,22},{24,26},{28,30},{30,28}... | collective-permute-start | bytes 393224 | tf_op jit(solution)/shard_map/ppermute | solution.py:481
  15.4 8.2 %collective-permute-start.2 = (f32[2,64,256]{2,1,0:T(8,128)S(1)}, f32[2,64,256]{2,1,0:T(8,128)S(1)}, u32[]{:S(2)}, u32[]{:S(2)}) collective-permute-start(f32[2,64,256]{2,1,0:T(8,128)S(1)} %get-tuple-element.48.now), channel_id=1, source_target_pairs={{2,6},{10,14},{18,22},{26,30},{28,24},{20,16},{12,8},{4,0},{3,7},{... | collective-permute-start | bytes 393224 | tf_op jit(solution)/shard_map/ppermute | solution.py:491
  19.8 7.9 %collective-permute-start.10 = (f32[2,64,256]{2,1,0:T(8,128)S(1)}, f32[2,64,256]{2,1,0:T(8,128)S(1)}, u32[]{:S(2)}, u32[]{:S(2)}) collective-permute-start(f32[2,64,256]{2,1,0:T(8,128)S(1)} %get-tuple-element.63.now), channel_id=1, source_target_pairs={{2,6},{10,14},{18,22},{26,30},{28,24},{20,16},{12,8},{4,0},{3,7},{... | collective-permute-start | bytes 393224 | tf_op jit(solution)/shard_map/ppermute | solution.py:491
  23.6 4.8 %collective-permute-start.3 = (f32[2,64,256]{2,1,0:T(8,128)S(1)}, f32[2,64,256]{2,1,0:T(8,128)S(1)}, u32[]{:S(2)}, u32[]{:S(2)}) collective-permute-start(f32[2,64,256]{2,1,0:T(8,128)S(1)} %fold.11.now), channel_id=1, source_target_pairs={{6,14},{24,16},{7,15},{25,17},{38,46},{56,48},{39,47},{57,49},{70,... | collective-permute-start | bytes 393224 | tf_op jit(solution)/shard_map/ppermute | solution.py:491
  27.7 2.4 %collective-permute-start.11 = (f32[2,64,256]{2,1,0:T(8,128)S(1)}, f32[2,64,256]{2,1,0:T(8,128)S(1)}, u32[]{:S(2)}, u32[]{:S(2)}) collective-permute-start(f32[2,64,256]{2,1,0:T(8,128)S(1)} %fold.16.now), channel_id=1, source_target_pairs={{6,14},{24,16},{7,15},{25,17},{38,46},{56,48},{39,47},{57,49},{70,... | collective-permute-start | bytes 393224 | tf_op jit(solution)/shard_map/ppermute | solution.py:491
  28.5 2.4 %collective-permute-start.4 = (f32[2,64,256]{2,1,0:T(8,128)S(1)}, f32[2,64,256]{2,1,0:T(8,128)S(1)}, u32[]{:S(2)}, u32[]{:S(2)}) collective-permute-start(f32[2,64,256]{2,1,0:T(8,128)S(1)} %fold.12.now), channel_id=1, source_target_pairs={{14,22},{16,8},{15,23},{17,9},{46,54},{48,40},{47,55},{49,41},{78,... | collective-permute-start | bytes 393224 | tf_op jit(solution)/shard_map/ppermute | solution.py:491
  30.3 1.5 %collective-permute-start.12 = (f32[2,64,256]{2,1,0:T(8,128)S(1)}, f32[2,64,256]{2,1,0:T(8,128)S(1)}, u32[]{:S(2)}, u32[]{:S(2)}) collective-permute-start(f32[2,64,256]{2,1,0:T(8,128)S(1)} %fold.17.now), channel_id=1, source_target_pairs={{14,22},{16,8},{15,23},{17,9},{46,54},{48,40},{47,55},{49,41},{78,... | collective-permute-start | bytes 393224 | tf_op jit(solution)/shard_map/ppermute | solution.py:491
  31.1 1.5 %collective-permute-start.5 = (f32[2,64,256]{2,1,0:T(8,128)S(1)}, f32[2,64,256]{2,1,0:T(8,128)S(1)}, u32[]{:S(2)}, u32[]{:S(2)}) collective-permute-start(f32[2,64,256]{2,1,0:T(8,128)S(1)} %fold.13.now), channel_id=1, source_target_pairs={{6,10},{14,18},{22,26},{24,20},{16,12},{8,4},{7,11},{15,19},{23,27... | collective-permute-start | bytes 393224 | tf_op jit(solution)/shard_map/ppermute | solution.py:491
  31.8 1.5 %collective-permute-start.13 = (f32[2,64,256]{2,1,0:T(8,128)S(1)}, f32[2,64,256]{2,1,0:T(8,128)S(1)}, u32[]{:S(2)}, u32[]{:S(2)}) collective-permute-start(f32[2,64,256]{2,1,0:T(8,128)S(1)} %fold.18.now), channel_id=1, source_target_pairs={{6,10},{14,18},{22,26},{24,20},{16,12},{8,4},{7,11},{15,19},{23,27... | collective-permute-start | bytes 393224 | tf_op jit(solution)/shard_map/ppermute | solution.py:491
  32.6 1.5 %collective-permute-start.6 = (f32[2,64,256]{2,1,0:T(8,128)S(1)}, f32[2,64,256]{2,1,0:T(8,128)S(1)}, u32[]{:S(2)}, u32[]{:S(2)}) collective-permute-start(f32[2,64,256]{2,1,0:T(8,128)S(1)} %fold.14), channel_id=1, source_target_pairs={{2,4},{6,8},{10,12},{14,16},{18,20},{22,24},{26,28},{28,26},{24,22... | collective-permute-start | bytes 393224 | tf_op jit(solution)/shard_map/ppermute | solution.py:495
  33.4 34.4 %collective-permute-start.14 = (f32[2,64,256]{2,1,0:T(8,128)S(1)}, f32[2,64,256]{2,1,0:T(8,128)S(1)}, u32[]{:S(2)}, u32[]{:S(2)}) collective-permute-start(f32[2,64,256]{2,1,0:T(8,128)S(1)} %fold.19), channel_id=1, source_target_pairs={{2,4},{6,8},{10,12},{14,16},{18,20},{22,24},{26,28},{28,26},{24,22... | collective-permute-start | bytes 393224 | tf_op jit(solution)/shard_map/ppermute | solution.py:495
  34.1 37.7 %collective-permute-start.7 = (f32[2,64,256]{2,1,0:T(8,128)S(1)}, f32[2,64,256]{2,1,0:T(8,128)S(1)}, u32[]{:S(2)}, u32[]{:S(2)}) collective-permute-start(f32[2,64,256]{2,1,0:T(8,128)S(1)} %collective-permute-done.6.one), channel_id=1, source_target_pairs={{0,2},{4,6},{8,10},{12,14},{16,18},{20,22},{24,26},{28,30},{30,28}... | collective-permute-start | bytes 393224 | tf_op jit(solution)/shard_map/ppermute | solution.py:496
  67.8 7.0 %collective-permute-start.15 = (f32[2,64,256]{2,1,0:T(8,128)S(1)}, f32[2,64,256]{2,1,0:T(8,128)S(1)}, u32[]{:S(2)}, u32[]{:S(2)}) collective-permute-start(f32[2,64,256]{2,1,0:T(8,128)S(1)} %collective-permute-done.14.one), channel_id=1, source_target_pairs={{0,2},{4,6},{8,10},{12,14},{16,18},{20,22},{24,26},{28,30},{30,28}... | collective-permute-start | bytes 393224 | tf_op jit(solution)/shard_map/ppermute | solution.py:496
  73.2 4.8 %collective-permute-start.18 = (f32[2,8,64,128]{3,2,1,0:T(8,128)S(1)}, f32[2,8,64,128]{3,2,1,0:T(8,128)S(1)}, u32[]{:S(2)}, u32[]{:S(2)}) collective-permute-start(f32[2,8,64,128]{3,2,1,0:T(8,128)S(1)} %get-tuple-element.78), channel_id=1, source_target_pairs={{0,1},{1,0},{2,3},{3,2},{4,5},{5,4},{6,7},{7,6},{8,9},{9,8},{10,11... | collective-permute-start | bytes 1572872 | tf_op jit(solution)/shard_map/ppermute | solution.py:515
  74.5 3.7 %copy-start.1 = (f32[2,256,16,128]{3,2,1,0:T(8,128)S(1)}, f32[2,256,16,128]{3,2,1,0:T(8,128)}, u32[]{:S(2)}) copy-start(f32[2,256,16,128]{3,2,1,0:T(8,128)} %refs_4_.3) | copy-start | bytes 12582916
  74.5 3.7 %copy-start.3 = (f32[256,16,128]{2,1,0:T(8,128)S(1)}, f32[256,16,128]{2,1,0:T(8,128)}, u32[]{:S(2)}) copy-start(f32[256,16,128]{2,1,0:T(8,128)} %refs_5_.3) | copy-start | bytes 6291460
  76.1 2.0 %collective-permute-start.19 = (f32[2,8,64,128]{3,2,1,0:T(8,128)S(1)}, f32[2,8,64,128]{3,2,1,0:T(8,128)S(1)}, u32[]{:S(2)}, u32[]{:S(2)}) collective-permute-start(f32[2,8,64,128]{3,2,1,0:T(8,128)S(1)} %get-tuple-element.79), channel_id=1, source_target_pairs={{0,1},{1,0},{2,3},{3,2},{4,5},{5,4},{6,7},{7,6},{8,9},{9,8},{10,11... | collective-permute-start | bytes 1572872 | tf_op jit(solution)/shard_map/ppermute | solution.py:515
  76.4 4.0 %collective-permute-start.16 = (f32[2,8,64,128]{3,2,1,0:T(8,128)S(1)}, f32[2,8,64,128]{3,2,1,0:T(8,128)S(1)}, u32[]{:S(2)}, u32[]{:S(2)}) collective-permute-start(f32[2,8,64,128]{3,2,1,0:T(8,128)S(1)} %get-tuple-element.71), channel_id=1, source_target_pairs={{0,1},{1,0},{2,3},{3,2},{4,5},{5,4},{6,7},{7,6},{8,9},{9,8},{10,11... | collective-permute-start | bytes 1572872 | tf_op jit(solution)/shard_map/ppermute | solution.py:515
  77.7 2.8 %collective-permute-start.17 = (f32[2,8,64,128]{3,2,1,0:T(8,128)S(1)}, f32[2,8,64,128]{3,2,1,0:T(8,128)S(1)}, u32[]{:S(2)}, u32[]{:S(2)}) collective-permute-start(f32[2,8,64,128]{3,2,1,0:T(8,128)S(1)} %get-tuple-element.72), channel_id=1, source_target_pairs={{0,1},{1,0},{2,3},{3,2},{4,5},{5,4},{6,7},{7,6},{8,9},{9,8},{10,11... | collective-permute-start | bytes 1572872 | tf_op jit(solution)/shard_map/ppermute | solution.py:515
  82.9 1.3 %collective-permute-start.20 = (f32[4,128]{1,0:T(4,128)S(1)}, f32[4,128]{1,0:T(4,128)S(1)}, u32[]{:S(2)}, u32[]{:S(2)}) collective-permute-start(f32[4,128]{1,0:T(4,128)S(1)} %add.6), channel_id=1, source_target_pairs={{0,1},{1,0},{2,3},{3,2},{4,5},{5,4},{6,7},{7,6},{8,9},{9,8},{10,11... | collective-permute-start | bytes 6152 | tf_op jit(solution)/shard_map/ppermute | solution.py:530

commit v7 on v6

--- a/solution.py
+++ b/solution.py
@@ -13,7 +13,7 @@
 f32 = jnp.float32
 bf16 = jnp.bfloat16
 YB = 8
-KB = 32
+KB = 64
 XC = 32
 CHUNKS = 2
 

time: 103 us -> 102 us (level)
  no operation moved by 1% of the time
where the time goes in v7:
time: 102 us
  starting transfers between devices  49.5 us (49%)
  Pallas kernels  23.7 us (23%)
  blocking collectives  16 us (16%)
  waiting for transfers between devices  11.5 us (11%)
  local copies, waits for them, and re-layouts  1.06 us (1%)
    ppermute x2, starting transfers between devices, on_device(): two = [lax.ppermute(s, 'px', pair) for s in one]  37.1 us
    all_to_all x1, blocking collectives, on_device(): lax.all_to_all(jnp.broadcast_to(sums[None], (ring, 4, w)), 'px', 0, 0, ti...  16 us
    ppermute x8, starting transfers between devices, on_device(): recv = lax.ppermute(s, 'px', route)  6.62 us
    pallas_call x2, Pallas kernels, on_device(): pl.pallas_call(functools.partial(inverse_x, h), in_specs=[VM] * (3 + 2 *...  4.68 us
    pallas_call x2, Pallas kernels, on_device(): pl.pallas_call(forward_x_first if first else functools.partial(forward_x,...  4.53 us
    ppermute x8, waiting for transfers between devices, on_device(): recv = lax.ppermute(s, 'px', route)  4.46 us
    pallas_call x2, Pallas kernels, on_device(): pl.pallas_call(functools.partial(forward_z, c), in_specs=[VM] * (4 + len(...  3.97 us
    ppermute x2, waiting for transfers between devices, on_device(): near = [lax.ppermute(s, 'px', pair) for s in sends]  3.84 us
  transfers between devices with their start and end apart: 21, of which 8 were waited for; matrix products, arithmetic and copies ran while one was open for 0% of the time, Pallas kernels for 15%

profile of v7, /device:TPU:86, one launch (start us, length us, event | category | flops | bytes accessed | tf_op | source)
XLA Modules:
  0.0 102.2 jit_solution(16905397410186005462)
XLA Ops:
  0.0 1.0 %copy-done.2 = bf16[2,256,256]{2,1,0:T(8,128)(2,1)S(1)} copy-done((bf16[2,256,256]{2,1,0:T(8,128)(2,1)S(1)}, bf16[2,256,256]{2,1,0:T(8,128)(2,1)}, u32[]{:S(2)}) %copy-start.2) | copy-done | bytes 262168
  1.0 3.5 %forward_x.2 = (f32[2,16,64,128]{3,2,1,0:T(8,128)S(1)}, f32[2,16,64,128]{3,2,1,0:T(8,128)S(1)}, bf16[2,2,512,1024]{3,2,1,0:T(8,128)(2,1)S(1)}) custom-call(bf16[2,256,256]{2,1,0:T(8,128)(2,1)S(1)} %copy-done.2, f32[2,256,16,128]{3,2,1,0:T(8,128)} %refs_4_.3), custom_call_target="tpu_custom_call" | custom-call | flops 805306368 | bytes 4194304 | tf_op jit(solution)/shard_map/forward_x/pallas_call | solution.py:417
  4.6 0.1 collective-permute-start
  4.7 1.0 forward_x.3
  5.7 0.6 collective-permute-start.8
  6.3 1.0 %collective-permute-done.recv = f32[2,16,64,128]{3,2,1,0:T(8,128)S(1)} collective-permute-done((f32[2,16,64,128]{3,2,1,0:T(8,128)S(1)}, f32[2,16,64,128]{3,2,1,0:T(8,128)S(1)}, u32[]{:S(2)}, u32[]{:S(2)}) %collective-permute-start) | collective-permute-done | bytes 1048608 | tf_op jit(solution)/shard_map/ppermute | solution.py:433
  7.4 1.7 %forward_z.2 = (f32[2,8,64,256]{3,2,1,0:T(8,128)S(1)}, f32[2,8,64,256]{3,2,1,0:T(8,128)S(1)}, f32[4,64,256]{2,1,0:T(8,128)S(1)}, f32[2,64,256]{2,1,0:T(8,128)S(1)}, f32[8,128]{1,0:T(8,128)S(1)}) custom-call(bf16[2,256,256]{2,1,0:T(8,128)(2,1)S(1)} %copy-done.2, f32[4,256,256]{2,1,0:T(8,128)S(1)} %copy-done, f32[2,16,64,128]{3,2,1,0:T(8,128)S(1)} %get-tuple-element.44.keep, ...), custom_call_target="tpu_custom_call" | custom-call | flops 805306368 | bytes 4194304 | tf_op jit(solution)/shard_map/forward_z/pallas_call | solution.py:436
  9.1 2.2 %collective-permute-start.1 = (f32[2,64,256]{2,1,0:T(8,128)S(1)}, f32[2,64,256]{2,1,0:T(8,128)S(1)}, u32[]{:S(2)}, u32[]{:S(2)}) collective-permute-start(f32[2,64,256]{2,1,0:T(8,128)S(1)} %get-tuple-element.47), channel_id=1, source_target_pairs={{0,2},{4,6},{8,10},{12,14},{16,18},{20,22},{24,26},{28,30},{30,28}... | collective-permute-start | bytes 393224 | tf_op jit(solution)/shard_map/ppermute | solution.py:481
  11.3 2.3 %forward_z.3 = (f32[2,8,64,256]{3,2,1,0:T(8,128)S(1)}, f32[2,8,64,256]{3,2,1,0:T(8,128)S(1)}, f32[4,64,256]{2,1,0:T(8,128)S(1)}, f32[2,64,256]{2,1,0:T(8,128)S(1)}, f32[8,128]{1,0:T(8,128)}) custom-call(bf16[2,256,256]{2,1,0:T(8,128)(2,1)S(1)} %copy-done.2, f32[4,256,256]{2,1,0:T(8,128)S(1)} %copy-done, f32[2,16,64,128]{3,2,1,0:T(8,128)S(1)} %get-tuple-element.57.keep, ...), custom_call_target="tpu_custom_call" | custom-call | flops 805306368 | bytes 4194304 | tf_op jit(solution)/shard_map/forward_z/pallas_call | solution.py:436
  13.6 0.0 collective-permute-start.9
  13.6 1.5 %collective-permute-done.1.recv.near = f32[2,64,256]{2,1,0:T(8,128)S(1)} collective-permute-done((f32[2,64,256]{2,1,0:T(8,128)S(1)}, f32[2,64,256]{2,1,0:T(8,128)S(1)}, u32[]{:S(2)}, u32[]{:S(2)}) %collective-permute-start.1) | collective-permute-done | bytes 131104 | tf_op jit(solution)/shard_map/ppermute | solution.py:481
  15.1 0.1 fold.10
  15.2 1.3 %collective-permute-start.2 = (f32[2,64,256]{2,1,0:T(8,128)S(1)}, f32[2,64,256]{2,1,0:T(8,128)S(1)}, u32[]{:S(2)}, u32[]{:S(2)}) collective-permute-start(f32[2,64,256]{2,1,0:T(8,128)S(1)} %get-tuple-element.48.now), channel_id=1, source_target_pairs={{2,6},{10,14},{18,22},{26,30},{28,24},{20,16},{12,8},{4,0},{3,7},{... | collective-permute-start | bytes 393224 | tf_op jit(solution)/shard_map/ppermute | solution.py:491
  16.5 2.3 %collective-permute-done.9.recv.near = f32[2,64,256]{2,1,0:T(8,128)S(1)} collective-permute-done((f32[2,64,256]{2,1,0:T(8,128)S(1)}, f32[2,64,256]{2,1,0:T(8,128)S(1)}, u32[]{:S(2)}, u32[]{:S(2)}) %collective-permute-start.9) | collective-permute-done | bytes 131104 | tf_op jit(solution)/shard_map/ppermute | solution.py:481
  18.8 0.6 fold.15
  19.5 1.3 %collective-permute-start.10 = (f32[2,64,256]{2,1,0:T(8,128)S(1)}, f32[2,64,256]{2,1,0:T(8,128)S(1)}, u32[]{:S(2)}, u32[]{:S(2)}) collective-permute-start(f32[2,64,256]{2,1,0:T(8,128)S(1)} %get-tuple-element.63.now), channel_id=1, source_target_pairs={{2,6},{10,14},{18,22},{26,30},{28,24},{20,16},{12,8},{4,0},{3,7},{... | collective-permute-start | bytes 393224 | tf_op jit(solution)/shard_map/ppermute | solution.py:491
  20.8 2.6 %collective-permute-done.2.refs_0_ = f32[2,64,256]{2,1,0:T(8,128)S(1)} collective-permute-done((f32[2,64,256]{2,1,0:T(8,128)S(1)}, f32[2,64,256]{2,1,0:T(8,128)S(1)}, u32[]{:S(2)}, u32[]{:S(2)}) %collective-permute-start.2) | collective-permute-done | bytes 131104 | tf_op jit(solution)/shard_map/ppermute | solution.py:491
  23.4 0.1 fold.11.now
  23.5 0.7 collective-permute-start.3
  24.1 1.4 %local_solve.2 = (f32[2,8,64,256]{3,2,1,0:T(8,128)S(1)}, f32[2,8,64,256]{3,2,1,0:T(8,128)S(1)}) custom-call(f32[4,256,256]{2,1,0:T(8,128)S(1)} %copy-done, f32[2,8,64,256]{3,2,1,0:T(8,128)S(1)} %get-tuple-element.49.f0, f32[2,8,64,256]{3,2,1,0:T(8,128)S(1)} %get-tuple-element.50.f1), custom_call_target="tpu_custom_call" | custom-call | flops 100663296 | bytes 8388608 | tf_op jit(solution)/shard_map/local_solve/pallas_call | solution.py:470
  25.5 1.8 %collective-permute-done.10.refs_0_ = f32[2,64,256]{2,1,0:T(8,128)S(1)} collective-permute-done((f32[2,64,256]{2,1,0:T(8,128)S(1)}, f32[2,64,256]{2,1,0:T(8,128)S(1)}, u32[]{:S(2)}, u32[]{:S(2)}) %collective-permute-start.10) | collective-permute-done | bytes 131104 | tf_op jit(solution)/shard_map/ppermute | solution.py:491
  27.3 0.1 fold.16.now
  27.4 0.7 collective-permute-start.11
  28.1 0.0 collective-permute-done.3.refs_0_
  28.1 0.1 fold.12.now
  28.2 0.7 collective-permute-start.4
  28.9 1.4 %local_solve.3 = (f32[2,8,64,256]{3,2,1,0:T(8,128)S(1)}, f32[2,8,64,256]{3,2,1,0:T(8,128)S(1)}) custom-call(f32[4,256,256]{2,1,0:T(8,128)S(1)} %copy-done, f32[2,8,64,256]{3,2,1,0:T(8,128)S(1)} %get-tuple-element.64.f0, f32[2,8,64,256]{3,2,1,0:T(8,128)S(1)} %get-tuple-element.65.f1), custom_call_target="tpu_custom_call" | custom-call | flops 100663296 | bytes 8388608 | tf_op jit(solution)/shard_map/local_solve/pallas_call | solution.py:470
  30.3 0.1 fold.17.now
  30.4 0.7 collective-permute-start.12
  31.1 0.0 collective-permute-done.4.refs_0_
  31.1 0.1 fold.13.now
  31.2 0.7 collective-permute-start.5
  31.9 0.0 collective-permute-done.12.refs_0_
  31.9 0.1 fold.18.now
  32.0 0.7 collective-permute-start.13
  32.7 0.0 collective-permute-done.5.refs_0_
  32.7 0.1 fold.14
  32.8 0.8 collective-permute-start.6
  33.6 0.0 collective-permute-done.13.refs_0_
  33.7 0.1 fold.19
  33.7 0.7 collective-permute-start.14
  34.4 0.0 collective-permute-done.6.one
  34.4 33.0 %collective-permute-start.7 = (f32[2,64,256]{2,1,0:T(8,128)S(1)}, f32[2,64,256]{2,1,0:T(8,128)S(1)}, u32[]{:S(2)}, u32[]{:S(2)}) collective-permute-start(f32[2,64,256]{2,1,0:T(8,128)S(1)} %collective-permute-done.6.one), channel_id=1, source_target_pairs={{0,2},{4,6},{8,10},{12,14},{16,18},{20,22},{24,26},{28,30},{30,28}... | collective-permute-start | bytes 393224 | tf_op jit(solution)/shard_map/ppermute | solution.py:496
  67.5 4.1 %collective-permute-start.15 = (f32[2,64,256]{2,1,0:T(8,128)S(1)}, f32[2,64,256]{2,1,0:T(8,128)S(1)}, u32[]{:S(2)}, u32[]{:S(2)}) collective-permute-start(f32[2,64,256]{2,1,0:T(8,128)S(1)} %collective-permute-done.14.one), channel_id=1, source_target_pairs={{0,2},{4,6},{8,10},{12,14},{16,18},{20,22},{24,26},{28,30},{30,28}... | collective-permute-start | bytes 393224 | tf_op jit(solution)/shard_map/ppermute | solution.py:496
  71.5 0.4 carries.2.fb
  71.9 0.8 inverse_z.6
  72.8 0.1 collective-permute-start.18
  72.9 0.8 inverse_z.4
  73.7 0.0 copy-start.1
  73.7 0.0 copy-start.3
  73.7 0.7 collective-permute-done.15.two
  74.5 0.4 carries.3.fb
  74.9 0.8 inverse_z.7
  75.7 0.1 collective-permute-start.19
  75.8 0.5 collective-permute-start.16
  76.3 0.8 inverse_z.5
  77.1 0.3 collective-permute-start.17
  77.4 0.3 collective-permute-done.19.refs_3_
  77.7 2.3 %inverse_x.3 = (f32[2,256,8,128]{3,2,1,0:T(8,128)S(1)}, f32[4,128]{1,0:T(4,128)S(1)}) custom-call(bf16[2,256,256]{2,1,0:T(8,128)(2,1)S(1)} %copy-done.2, f32[2,8,64,128]{3,2,1,0:T(8,128)S(1)} %get-tuple-element.75.refs_0_, f32[2,8,64,128]{3,2,1,0:T(8,128)S(1)} %get-tuple-element.77.refs_1_, f32[2,8,64,128]{3,2,1,0:T(8,128)S(1)} %collective-permute-done.18.refs_2_, ...), custom_call_target="tpu_custom_call" | custom-call | flops 805306368 | bytes 4194304 | tf_op jit(solution)/shard_map/inverse_x/pallas_call | solution.py:518
  80.1 2.3 %inverse_x.2 = (f32[2,256,8,128]{3,2,1,0:T(8,128)S(1)}, f32[4,128]{1,0:T(4,128)S(1)}) custom-call(bf16[2,256,256]{2,1,0:T(8,128)(2,1)S(1)} %copy-done.2, f32[2,8,64,128]{3,2,1,0:T(8,128)S(1)} %get-tuple-element.55.refs_0_, f32[2,8,64,128]{3,2,1,0:T(8,128)S(1)} %get-tuple-element.70.refs_1_, f32[2,8,64,128]{3,2,1,0:T(8,128)S(1)} %collective-permute-done.16.refs_2_, ...), custom_call_target="tpu_custom_call" | custom-call | flops 805306368 | bytes 4194304 | tf_op jit(solution)/shard_map/inverse_x/pallas_call | solution.py:518
  82.4 0.2 collective-permute-start.20
  82.7 1.0 %collective-permute-done.20 = f32[4,128]{1,0:T(4,128)S(1)} collective-permute-done((f32[4,128]{1,0:T(4,128)S(1)}, f32[4,128]{1,0:T(4,128)S(1)}, u32[]{:S(2)}, u32[]{:S(2)}) %collective-permute-start.20) | collective-permute-done | bytes 2080 | tf_op jit(solution)/shard_map/ppermute | solution.py:530
  83.7 16.0 %all_to_all.5.total = f32[16,4,128]{2,1,0:T(4,128)S(1)} all-to-all(f32[16,4,128]{2,1,0:T(4,128)S(1)} %broadcast_in_dim.2), channel_id=1, replica_groups=mesh['samples'=4,'px'=16,'py'=2] {'px'}, dimensions={0} | all-to-all | bytes 65536 | tf_op jit(solution)/shard_map/all_to_all | solution.py:531
  99.7 2.3 %finish.1 = f32[2,256,16,128]{3,2,1,0:T(8,128)} custom-call(f32[16,4,128]{2,1,0:T(4,128)S(1)} %all_to_all.5.total, f32[2,256,8,128]{3,2,1,0:T(8,128)S(1)} %get-tuple-element.81.ps0, f32[2,256,8,128]{3,2,1,0:T(8,128)S(1)} %get-tuple-element.82.ps1), custom_call_target="tpu_custom_call" | custom-call | flops 10000000 | bytes 8388608 | tf_op jit(solution)/shard_map/finish/pallas_call | solution.py:532
  (15 shorter events, 0.0 us)
Async XLA Ops:
  0.0 7.4 %copy-start = (f32[4,256,256]{2,1,0:T(8,128)S(1)}, f32[4,256,256]{2,1,0:T(8,128)}, u32[]{:S(2)}) copy-start(f32[4,256,256]{2,1,0:T(8,128)} %constant.5.clone.root) | copy-start | bytes 3145732
  0.0 1.0 %copy-start.2 = (bf16[2,256,256]{2,1,0:T(8,128)(2,1)S(1)}, bf16[2,256,256]{2,1,0:T(8,128)(2,1)}, u32[]{:S(2)}) copy-start(bf16[2,256,256]{2,1,0:T(8,128)(2,1)} %constant.4.clone.s_hbm.s_ref) | copy-start | bytes 786436
  4.6 2.8 %collective-permute-start = (f32[2,16,64,128]{3,2,1,0:T(8,128)S(1)}, f32[2,16,64,128]{3,2,1,0:T(8,128)S(1)}, u32[]{:S(2)}, u32[]{:S(2)}) collective-permute-start(f32[2,16,64,128]{3,2,1,0:T(8,128)S(1)} %get-tuple-element.45), channel_id=1, source_target_pairs={{0,1},{1,0},{2,3},{3,2},{4,5},{5,4},{6,7},{7,6},{8,9},{9,8},{10,11... | collective-permute-start | bytes 3145736 | tf_op jit(solution)/shard_map/ppermute | solution.py:433
  5.7 5.6 %collective-permute-start.8 = (f32[2,16,64,128]{3,2,1,0:T(8,128)S(1)}, f32[2,16,64,128]{3,2,1,0:T(8,128)S(1)}, u32[]{:S(2)}, u32[]{:S(2)}) collective-permute-start(f32[2,16,64,128]{3,2,1,0:T(8,128)S(1)} %get-tuple-element.58), channel_id=1, source_target_pairs={{0,1},{1,0},{2,3},{3,2},{4,5},{5,4},{6,7},{7,6},{8,9},{9,8},{10,11... | collective-permute-start | bytes 3145736 | tf_op jit(solution)/shard_map/ppermute | solution.py:433
  9.1 6.0 %collective-permute-start.1 = (f32[2,64,256]{2,1,0:T(8,128)S(1)}, f32[2,64,256]{2,1,0:T(8,128)S(1)}, u32[]{:S(2)}, u32[]{:S(2)}) collective-permute-start(f32[2,64,256]{2,1,0:T(8,128)S(1)} %get-tuple-element.47), channel_id=1, source_target_pairs={{0,2},{4,6},{8,10},{12,14},{16,18},{20,22},{24,26},{28,30},{30,28}... | collective-permute-start | bytes 393224 | tf_op jit(solution)/shard_map/ppermute | solution.py:481
  13.6 5.3 %collective-permute-start.9 = (f32[2,64,256]{2,1,0:T(8,128)S(1)}, f32[2,64,256]{2,1,0:T(8,128)S(1)}, u32[]{:S(2)}, u32[]{:S(2)}) collective-permute-start(f32[2,64,256]{2,1,0:T(8,128)S(1)} %get-tuple-element.61), channel_id=1, source_target_pairs={{0,2},{4,6},{8,10},{12,14},{16,18},{20,22},{24,26},{28,30},{30,28}... | collective-permute-start | bytes 393224 | tf_op jit(solution)/shard_map/ppermute | solution.py:481
  15.2 8.2 %collective-permute-start.2 = (f32[2,64,256]{2,1,0:T(8,128)S(1)}, f32[2,64,256]{2,1,0:T(8,128)S(1)}, u32[]{:S(2)}, u32[]{:S(2)}) collective-permute-start(f32[2,64,256]{2,1,0:T(8,128)S(1)} %get-tuple-element.48.now), channel_id=1, source_target_pairs={{2,6},{10,14},{18,22},{26,30},{28,24},{20,16},{12,8},{4,0},{3,7},{... | collective-permute-start | bytes 393224 | tf_op jit(solution)/shard_map/ppermute | solution.py:491
  19.5 7.9 %collective-permute-start.10 = (f32[2,64,256]{2,1,0:T(8,128)S(1)}, f32[2,64,256]{2,1,0:T(8,128)S(1)}, u32[]{:S(2)}, u32[]{:S(2)}) collective-permute-start(f32[2,64,256]{2,1,0:T(8,128)S(1)} %get-tuple-element.63.now), channel_id=1, source_target_pairs={{2,6},{10,14},{18,22},{26,30},{28,24},{20,16},{12,8},{4,0},{3,7},{... | collective-permute-start | bytes 393224 | tf_op jit(solution)/shard_map/ppermute | solution.py:491
  23.5 4.7 %collective-permute-start.3 = (f32[2,64,256]{2,1,0:T(8,128)S(1)}, f32[2,64,256]{2,1,0:T(8,128)S(1)}, u32[]{:S(2)}, u32[]{:S(2)}) collective-permute-start(f32[2,64,256]{2,1,0:T(8,128)S(1)} %fold.11.now), channel_id=1, source_target_pairs={{6,14},{24,16},{7,15},{25,17},{38,46},{56,48},{39,47},{57,49},{70,... | collective-permute-start | bytes 393224 | tf_op jit(solution)/shard_map/ppermute | solution.py:491
  27.4 2.9 %collective-permute-start.11 = (f32[2,64,256]{2,1,0:T(8,128)S(1)}, f32[2,64,256]{2,1,0:T(8,128)S(1)}, u32[]{:S(2)}, u32[]{:S(2)}) collective-permute-start(f32[2,64,256]{2,1,0:T(8,128)S(1)} %fold.16.now), channel_id=1, source_target_pairs={{6,14},{24,16},{7,15},{25,17},{38,46},{56,48},{39,47},{57,49},{70,... | collective-permute-start | bytes 393224 | tf_op jit(solution)/shard_map/ppermute | solution.py:491
  28.2 2.9 %collective-permute-start.4 = (f32[2,64,256]{2,1,0:T(8,128)S(1)}, f32[2,64,256]{2,1,0:T(8,128)S(1)}, u32[]{:S(2)}, u32[]{:S(2)}) collective-permute-start(f32[2,64,256]{2,1,0:T(8,128)S(1)} %fold.12.now), channel_id=1, source_target_pairs={{14,22},{16,8},{15,23},{17,9},{46,54},{48,40},{47,55},{49,41},{78,... | collective-permute-start | bytes 393224 | tf_op jit(solution)/shard_map/ppermute | solution.py:491
  30.4 1.5 %collective-permute-start.12 = (f32[2,64,256]{2,1,0:T(8,128)S(1)}, f32[2,64,256]{2,1,0:T(8,128)S(1)}, u32[]{:S(2)}, u32[]{:S(2)}) collective-permute-start(f32[2,64,256]{2,1,0:T(8,128)S(1)} %fold.17.now), channel_id=1, source_target_pairs={{14,22},{16,8},{15,23},{17,9},{46,54},{48,40},{47,55},{49,41},{78,... | collective-permute-start | bytes 393224 | tf_op jit(solution)/shard_map/ppermute | solution.py:491
  31.2 1.5 %collective-permute-start.5 = (f32[2,64,256]{2,1,0:T(8,128)S(1)}, f32[2,64,256]{2,1,0:T(8,128)S(1)}, u32[]{:S(2)}, u32[]{:S(2)}) collective-permute-start(f32[2,64,256]{2,1,0:T(8,128)S(1)} %fold.13.now), channel_id=1, source_target_pairs={{6,10},{14,18},{22,26},{24,20},{16,12},{8,4},{7,11},{15,19},{23,27... | collective-permute-start | bytes 393224 | tf_op jit(solution)/shard_map/ppermute | solution.py:491
  32.0 1.6 %collective-permute-start.13 = (f32[2,64,256]{2,1,0:T(8,128)S(1)}, f32[2,64,256]{2,1,0:T(8,128)S(1)}, u32[]{:S(2)}, u32[]{:S(2)}) collective-permute-start(f32[2,64,256]{2,1,0:T(8,128)S(1)} %fold.18.now), channel_id=1, source_target_pairs={{6,10},{14,18},{22,26},{24,20},{16,12},{8,4},{7,11},{15,19},{23,27... | collective-permute-start | bytes 393224 | tf_op jit(solution)/shard_map/ppermute | solution.py:491
  32.8 1.6 %collective-permute-start.6 = (f32[2,64,256]{2,1,0:T(8,128)S(1)}, f32[2,64,256]{2,1,0:T(8,128)S(1)}, u32[]{:S(2)}, u32[]{:S(2)}) collective-permute-start(f32[2,64,256]{2,1,0:T(8,128)S(1)} %fold.14), channel_id=1, source_target_pairs={{2,4},{6,8},{10,12},{14,16},{18,20},{22,24},{26,28},{28,26},{24,22... | collective-permute-start | bytes 393224 | tf_op jit(solution)/shard_map/ppermute | solution.py:495
  33.7 33.7 %collective-permute-start.14 = (f32[2,64,256]{2,1,0:T(8,128)S(1)}, f32[2,64,256]{2,1,0:T(8,128)S(1)}, u32[]{:S(2)}, u32[]{:S(2)}) collective-permute-start(f32[2,64,256]{2,1,0:T(8,128)S(1)} %fold.19), channel_id=1, source_target_pairs={{2,4},{6,8},{10,12},{14,16},{18,20},{22,24},{26,28},{28,26},{24,22... | collective-permute-start | bytes 393224 | tf_op jit(solution)/shard_map/ppermute | solution.py:495
  34.4 37.1 %collective-permute-start.7 = (f32[2,64,256]{2,1,0:T(8,128)S(1)}, f32[2,64,256]{2,1,0:T(8,128)S(1)}, u32[]{:S(2)}, u32[]{:S(2)}) collective-permute-start(f32[2,64,256]{2,1,0:T(8,128)S(1)} %collective-permute-done.6.one), channel_id=1, source_target_pairs={{0,2},{4,6},{8,10},{12,14},{16,18},{20,22},{24,26},{28,30},{30,28}... | collective-permute-start | bytes 393224 | tf_op jit(solution)/shard_map/ppermute | solution.py:496
  67.5 7.0 %collective-permute-start.15 = (f32[2,64,256]{2,1,0:T(8,128)S(1)}, f32[2,64,256]{2,1,0:T(8,128)S(1)}, u32[]{:S(2)}, u32[]{:S(2)}) collective-permute-start(f32[2,64,256]{2,1,0:T(8,128)S(1)} %collective-permute-done.14.one), channel_id=1, source_target_pairs={{0,2},{4,6},{8,10},{12,14},{16,18},{20,22},{24,26},{28,30},{30,28}... | collective-permute-start | bytes 393224 | tf_op jit(solution)/shard_map/ppermute | solution.py:496
  72.8 4.6 %collective-permute-start.18 = (f32[2,8,64,128]{3,2,1,0:T(8,128)S(1)}, f32[2,8,64,128]{3,2,1,0:T(8,128)S(1)}, u32[]{:S(2)}, u32[]{:S(2)}) collective-permute-start(f32[2,8,64,128]{3,2,1,0:T(8,128)S(1)} %get-tuple-element.78), channel_id=1, source_target_pairs={{0,1},{1,0},{2,3},{3,2},{4,5},{5,4},{6,7},{7,6},{8,9},{9,8},{10,11... | collective-permute-start | bytes 1572872 | tf_op jit(solution)/shard_map/ppermute | solution.py:515
  73.7 4.0 %copy-start.1 = (f32[2,256,16,128]{3,2,1,0:T(8,128)S(1)}, f32[2,256,16,128]{3,2,1,0:T(8,128)}, u32[]{:S(2)}) copy-start(f32[2,256,16,128]{3,2,1,0:T(8,128)} %refs_4_.3) | copy-start | bytes 12582916
  73.7 4.0 %copy-start.3 = (f32[256,16,128]{2,1,0:T(8,128)S(1)}, f32[256,16,128]{2,1,0:T(8,128)}, u32[]{:S(2)}) copy-start(f32[256,16,128]{2,1,0:T(8,128)} %refs_5_.3) | copy-start | bytes 6291460
  75.7 2.0 %collective-permute-start.19 = (f32[2,8,64,128]{3,2,1,0:T(8,128)S(1)}, f32[2,8,64,128]{3,2,1,0:T(8,128)S(1)}, u32[]{:S(2)}, u32[]{:S(2)}) collective-permute-start(f32[2,8,64,128]{3,2,1,0:T(8,128)S(1)} %get-tuple-element.79), channel_id=1, source_target_pairs={{0,1},{1,0},{2,3},{3,2},{4,5},{5,4},{6,7},{7,6},{8,9},{9,8},{10,11... | collective-permute-start | bytes 1572872 | tf_op jit(solution)/shard_map/ppermute | solution.py:515
  75.8 4.2 %collective-permute-start.16 = (f32[2,8,64,128]{3,2,1,0:T(8,128)S(1)}, f32[2,8,64,128]{3,2,1,0:T(8,128)S(1)}, u32[]{:S(2)}, u32[]{:S(2)}) collective-permute-start(f32[2,8,64,128]{3,2,1,0:T(8,128)S(1)} %get-tuple-element.71), channel_id=1, source_target_pairs={{0,1},{1,0},{2,3},{3,2},{4,5},{5,4},{6,7},{7,6},{8,9},{9,8},{10,11... | collective-permute-start | bytes 1572872 | tf_op jit(solution)/shard_map/ppermute | solution.py:515
  77.1 2.9 %collective-permute-start.17 = (f32[2,8,64,128]{3,2,1,0:T(8,128)S(1)}, f32[2,8,64,128]{3,2,1,0:T(8,128)S(1)}, u32[]{:S(2)}, u32[]{:S(2)}) collective-permute-start(f32[2,8,64,128]{3,2,1,0:T(8,128)S(1)} %get-tuple-element.72), channel_id=1, source_target_pairs={{0,1},{1,0},{2,3},{3,2},{4,5},{5,4},{6,7},{7,6},{8,9},{9,8},{10,11... | collective-permute-start | bytes 1572872 | tf_op jit(solution)/shard_map/ppermute | solution.py:515
  82.4 1.3 %collective-permute-start.20 = (f32[4,128]{1,0:T(4,128)S(1)}, f32[4,128]{1,0:T(4,128)S(1)}, u32[]{:S(2)}, u32[]{:S(2)}) collective-permute-start(f32[4,128]{1,0:T(4,128)S(1)} %add.6), channel_id=1, source_target_pairs={{0,1},{1,0},{2,3},{3,2},{4,5},{5,4},{6,7},{7,6},{8,9},{9,8},{10,11... | collective-permute-start | bytes 6152 | tf_op jit(solution)/shard_map/ppermute | solution.py:530

commit v8 on v7

--- a/solution.py
+++ b/solution.py
@@ -14,7 +14,7 @@
 bf16 = jnp.bfloat16
 YB = 8
 KB = 64
-XC = 32
+XC = 16
 CHUNKS = 2
 
 

time: 102 us -> 103 us (level)
  no operation moved by 1% of the time
where the time goes in v8:
time: 103 us; the launch traced here: 102 us
  starting transfers between devices  49.5 us (48%)
  Pallas kernels  23.8 us (23%)
  blocking collectives  16 us (16%)
  waiting for transfers between devices  11.5 us (11%)
  local copies, waits for them, and re-layouts  1.06 us (1%)
    ppermute x2, starting transfers between devices, on_device(): two = [lax.ppermute(s, 'px', pair) for s in one]  37.1 us
    all_to_all x1, blocking collectives, on_device(): lax.all_to_all(jnp.broadcast_to(sums[None], (ring, 4, w)), 'px', 0, 0, ti...  16 us
    ppermute x8, starting transfers between devices, on_device(): recv = lax.ppermute(s, 'px', route)  6.62 us
    pallas_call x2, Pallas kernels, on_device(): pl.pallas_call(functools.partial(inverse_x, h), in_specs=[VM] * (3 + 2 *...  4.68 us
    pallas_call x2, Pallas kernels, on_device(): pl.pallas_call(forward_x_first if first else functools.partial(forward_x,...  4.53 us
    ppermute x8, waiting for transfers between devices, on_device(): recv = lax.ppermute(s, 'px', route)  4.46 us
    pallas_call x2, Pallas kernels, on_device(): pl.pallas_call(functools.partial(forward_z, c), in_specs=[VM] * (4 + len(...  3.97 us
    ppermute x2, waiting for transfers between devices, on_device(): near = [lax.ppermute(s, 'px', pair) for s in sends]  3.84 us
  transfers between devices with their start and end apart: 21, of which 8 were waited for; matrix products, arithmetic and copies ran while one was open for 0% of the time, Pallas kernels for 15%

profile of v8, /device:TPU:86, one launch (start us, length us, event | category | flops | bytes accessed | tf_op | source)
XLA Modules:
  0.0 102.3 jit_solution(11820844811182568424)
XLA Ops:
  0.0 1.0 %copy-done.2 = bf16[2,256,256]{2,1,0:T(8,128)(2,1)S(1)} copy-done((bf16[2,256,256]{2,1,0:T(8,128)(2,1)S(1)}, bf16[2,256,256]{2,1,0:T(8,128)(2,1)}, u32[]{:S(2)}) %copy-start.2) | copy-done | bytes 262168
  1.0 3.5 %forward_x.2 = (f32[2,16,64,128]{3,2,1,0:T(8,128)S(1)}, f32[2,16,64,128]{3,2,1,0:T(8,128)S(1)}, bf16[2,2,512,1024]{3,2,1,0:T(8,128)(2,1)S(1)}) custom-call(bf16[2,256,256]{2,1,0:T(8,128)(2,1)S(1)} %copy-done.2, f32[2,256,16,128]{3,2,1,0:T(8,128)} %refs_4_.3), custom_call_target="tpu_custom_call" | custom-call | flops 805306368 | bytes 4194304 | tf_op jit(solution)/shard_map/forward_x/pallas_call | solution.py:417
  4.6 0.1 collective-permute-start
  4.7 1.0 forward_x.3
  5.7 0.6 collective-permute-start.8
  6.3 1.0 %collective-permute-done.recv = f32[2,16,64,128]{3,2,1,0:T(8,128)S(1)} collective-permute-done((f32[2,16,64,128]{3,2,1,0:T(8,128)S(1)}, f32[2,16,64,128]{3,2,1,0:T(8,128)S(1)}, u32[]{:S(2)}, u32[]{:S(2)}) %collective-permute-start) | collective-permute-done | bytes 1048608 | tf_op jit(solution)/shard_map/ppermute | solution.py:433
  7.4 1.7 %forward_z.2 = (f32[2,8,64,256]{3,2,1,0:T(8,128)S(1)}, f32[2,8,64,256]{3,2,1,0:T(8,128)S(1)}, f32[4,64,256]{2,1,0:T(8,128)S(1)}, f32[2,64,256]{2,1,0:T(8,128)S(1)}, f32[8,128]{1,0:T(8,128)S(1)}) custom-call(bf16[2,256,256]{2,1,0:T(8,128)(2,1)S(1)} %copy-done.2, f32[4,256,256]{2,1,0:T(8,128)S(1)} %copy-done, f32[2,16,64,128]{3,2,1,0:T(8,128)S(1)} %get-tuple-element.44.keep, ...), custom_call_target="tpu_custom_call" | custom-call | flops 805306368 | bytes 4194304 | tf_op jit(solution)/shard_map/forward_z/pallas_call | solution.py:436
  9.1 2.2 %collective-permute-start.1 = (f32[2,64,256]{2,1,0:T(8,128)S(1)}, f32[2,64,256]{2,1,0:T(8,128)S(1)}, u32[]{:S(2)}, u32[]{:S(2)}) collective-permute-start(f32[2,64,256]{2,1,0:T(8,128)S(1)} %get-tuple-element.47), channel_id=1, source_target_pairs={{0,2},{4,6},{8,10},{12,14},{16,18},{20,22},{24,26},{28,30},{30,28}... | collective-permute-start | bytes 393224 | tf_op jit(solution)/shard_map/ppermute | solution.py:481
  11.3 2.3 %forward_z.3 = (f32[2,8,64,256]{3,2,1,0:T(8,128)S(1)}, f32[2,8,64,256]{3,2,1,0:T(8,128)S(1)}, f32[4,64,256]{2,1,0:T(8,128)S(1)}, f32[2,64,256]{2,1,0:T(8,128)S(1)}, f32[8,128]{1,0:T(8,128)}) custom-call(bf16[2,256,256]{2,1,0:T(8,128)(2,1)S(1)} %copy-done.2, f32[4,256,256]{2,1,0:T(8,128)S(1)} %copy-done, f32[2,16,64,128]{3,2,1,0:T(8,128)S(1)} %get-tuple-element.57.keep, ...), custom_call_target="tpu_custom_call" | custom-call | flops 805306368 | bytes 4194304 | tf_op jit(solution)/shard_map/forward_z/pallas_call | solution.py:436
  13.6 0.0 collective-permute-start.9
  13.6 1.5 %collective-permute-done.1.recv.near = f32[2,64,256]{2,1,0:T(8,128)S(1)} collective-permute-done((f32[2,64,256]{2,1,0:T(8,128)S(1)}, f32[2,64,256]{2,1,0:T(8,128)S(1)}, u32[]{:S(2)}, u32[]{:S(2)}) %collective-permute-start.1) | collective-permute-done | bytes 131104 | tf_op jit(solution)/shard_map/ppermute | solution.py:481
  15.1 0.1 fold.10
  15.2 1.3 %collective-permute-start.2 = (f32[2,64,256]{2,1,0:T(8,128)S(1)}, f32[2,64,256]{2,1,0:T(8,128)S(1)}, u32[]{:S(2)}, u32[]{:S(2)}) collective-permute-start(f32[2,64,256]{2,1,0:T(8,128)S(1)} %get-tuple-element.48.now), channel_id=1, source_target_pairs={{2,6},{10,14},{18,22},{26,30},{28,24},{20,16},{12,8},{4,0},{3,7},{... | collective-permute-start | bytes 393224 | tf_op jit(solution)/shard_map/ppermute | solution.py:491
  16.5 2.3 %collective-permute-done.9.recv.near = f32[2,64,256]{2,1,0:T(8,128)S(1)} collective-permute-done((f32[2,64,256]{2,1,0:T(8,128)S(1)}, f32[2,64,256]{2,1,0:T(8,128)S(1)}, u32[]{:S(2)}, u32[]{:S(2)}) %collective-permute-start.9) | collective-permute-done | bytes 131104 | tf_op jit(solution)/shard_map/ppermute | solution.py:481
  18.8 0.6 fold.15
  19.5 1.3 %collective-permute-start.10 = (f32[2,64,256]{2,1,0:T(8,128)S(1)}, f32[2,64,256]{2,1,0:T(8,128)S(1)}, u32[]{:S(2)}, u32[]{:S(2)}) collective-permute-start(f32[2,64,256]{2,1,0:T(8,128)S(1)} %get-tuple-element.63.now), channel_id=1, source_target_pairs={{2,6},{10,14},{18,22},{26,30},{28,24},{20,16},{12,8},{4,0},{3,7},{... | collective-permute-start | bytes 393224 | tf_op jit(solution)/shard_map/ppermute | solution.py:491
  20.8 2.6 %collective-permute-done.2.refs_0_ = f32[2,64,256]{2,1,0:T(8,128)S(1)} collective-permute-done((f32[2,64,256]{2,1,0:T(8,128)S(1)}, f32[2,64,256]{2,1,0:T(8,128)S(1)}, u32[]{:S(2)}, u32[]{:S(2)}) %collective-permute-start.2) | collective-permute-done | bytes 131104 | tf_op jit(solution)/shard_map/ppermute | solution.py:491
  23.4 0.1 fold.11.now
  23.5 0.7 collective-permute-start.3
  24.1 1.4 %local_solve.2 = (f32[2,8,64,256]{3,2,1,0:T(8,128)S(1)}, f32[2,8,64,256]{3,2,1,0:T(8,128)S(1)}) custom-call(f32[4,256,256]{2,1,0:T(8,128)S(1)} %copy-done, f32[2,8,64,256]{3,2,1,0:T(8,128)S(1)} %get-tuple-element.49.f0, f32[2,8,64,256]{3,2,1,0:T(8,128)S(1)} %get-tuple-element.50.f1), custom_call_target="tpu_custom_call" | custom-call | flops 100663296 | bytes 8388608 | tf_op jit(solution)/shard_map/local_solve/pallas_call | solution.py:470
  25.5 1.8 %collective-permute-done.10.refs_0_ = f32[2,64,256]{2,1,0:T(8,128)S(1)} collective-permute-done((f32[2,64,256]{2,1,0:T(8,128)S(1)}, f32[2,64,256]{2,1,0:T(8,128)S(1)}, u32[]{:S(2)}, u32[]{:S(2)}) %collective-permute-start.10) | collective-permute-done | bytes 131104 | tf_op jit(solution)/shard_map/ppermute | solution.py:491
  27.3 0.1 fold.16.now
  27.4 0.7 collective-permute-start.11
  28.1 0.0 collective-permute-done.3.refs_0_
  28.1 0.1 fold.12.now
  28.2 0.7 collective-permute-start.4
  28.9 1.4 %local_solve.3 = (f32[2,8,64,256]{3,2,1,0:T(8,128)S(1)}, f32[2,8,64,256]{3,2,1,0:T(8,128)S(1)}) custom-call(f32[4,256,256]{2,1,0:T(8,128)S(1)} %copy-done, f32[2,8,64,256]{3,2,1,0:T(8,128)S(1)} %get-tuple-element.64.f0, f32[2,8,64,256]{3,2,1,0:T(8,128)S(1)} %get-tuple-element.65.f1), custom_call_target="tpu_custom_call" | custom-call | flops 100663296 | bytes 8388608 | tf_op jit(solution)/shard_map/local_solve/pallas_call | solution.py:470
  30.3 0.1 fold.17.now
  30.4 0.7 collective-permute-start.12
  31.1 0.0 collective-permute-done.4.refs_0_
  31.1 0.1 fold.13.now
  31.2 0.7 collective-permute-start.5
  31.9 0.0 collective-permute-done.12.refs_0_
  31.9 0.1 fold.18.now
  32.0 0.7 collective-permute-start.13
  32.7 0.0 collective-permute-done.5.refs_0_
  32.7 0.1 fold.14
  32.8 0.8 collective-permute-start.6
  33.6 0.0 collective-permute-done.13.refs_0_
  33.7 0.1 fold.19
  33.7 0.7 collective-permute-start.14
  34.4 0.0 collective-permute-done.6.one
  34.4 33.0 %collective-permute-start.7 = (f32[2,64,256]{2,1,0:T(8,128)S(1)}, f32[2,64,256]{2,1,0:T(8,128)S(1)}, u32[]{:S(2)}, u32[]{:S(2)}) collective-permute-start(f32[2,64,256]{2,1,0:T(8,128)S(1)} %collective-permute-done.6.one), channel_id=1, source_target_pairs={{0,2},{4,6},{8,10},{12,14},{16,18},{20,22},{24,26},{28,30},{30,28}... | collective-permute-start | bytes 393224 | tf_op jit(solution)/shard_map/ppermute | solution.py:496
  67.5 4.1 %collective-permute-start.15 = (f32[2,64,256]{2,1,0:T(8,128)S(1)}, f32[2,64,256]{2,1,0:T(8,128)S(1)}, u32[]{:S(2)}, u32[]{:S(2)}) collective-permute-start(f32[2,64,256]{2,1,0:T(8,128)S(1)} %collective-permute-done.14.one), channel_id=1, source_target_pairs={{0,2},{4,6},{8,10},{12,14},{16,18},{20,22},{24,26},{28,30},{30,28}... | collective-permute-start | bytes 393224 | tf_op jit(solution)/shard_map/ppermute | solution.py:496
  71.5 0.4 carries.2.fb
  71.9 0.8 inverse_z.6
  72.8 0.1 collective-permute-start.18
  72.9 0.8 inverse_z.4
  73.7 0.0 copy-start.1
  73.7 0.0 copy-start.3
  73.7 0.7 collective-permute-done.15.two
  74.5 0.4 carries.3.fb
  74.9 0.8 inverse_z.7
  75.7 0.1 collective-permute-start.19
  75.8 0.5 collective-permute-start.16
  76.3 0.8 inverse_z.5
  77.1 0.3 collective-permute-start.17
  77.4 0.3 collective-permute-done.19.refs_3_
  77.7 2.3 %inverse_x.3 = (f32[2,256,8,128]{3,2,1,0:T(8,128)S(1)}, f32[4,128]{1,0:T(4,128)S(1)}) custom-call(bf16[2,256,256]{2,1,0:T(8,128)(2,1)S(1)} %copy-done.2, f32[2,8,64,128]{3,2,1,0:T(8,128)S(1)} %get-tuple-element.75.refs_0_, f32[2,8,64,128]{3,2,1,0:T(8,128)S(1)} %get-tuple-element.77.refs_1_, f32[2,8,64,128]{3,2,1,0:T(8,128)S(1)} %collective-permute-done.18.refs_2_, ...), custom_call_target="tpu_custom_call" | custom-call | flops 805306368 | bytes 4194304 | tf_op jit(solution)/shard_map/inverse_x/pallas_call | solution.py:518
  80.1 2.3 %inverse_x.2 = (f32[2,256,8,128]{3,2,1,0:T(8,128)S(1)}, f32[4,128]{1,0:T(4,128)S(1)}) custom-call(bf16[2,256,256]{2,1,0:T(8,128)(2,1)S(1)} %copy-done.2, f32[2,8,64,128]{3,2,1,0:T(8,128)S(1)} %get-tuple-element.55.refs_0_, f32[2,8,64,128]{3,2,1,0:T(8,128)S(1)} %get-tuple-element.70.refs_1_, f32[2,8,64,128]{3,2,1,0:T(8,128)S(1)} %collective-permute-done.16.refs_2_, ...), custom_call_target="tpu_custom_call" | custom-call | flops 805306368 | bytes 4194304 | tf_op jit(solution)/shard_map/inverse_x/pallas_call | solution.py:518
  82.4 0.2 collective-permute-start.20
  82.7 1.0 %collective-permute-done.20 = f32[4,128]{1,0:T(4,128)S(1)} collective-permute-done((f32[4,128]{1,0:T(4,128)S(1)}, f32[4,128]{1,0:T(4,128)S(1)}, u32[]{:S(2)}, u32[]{:S(2)}) %collective-permute-start.20) | collective-permute-done | bytes 2080 | tf_op jit(solution)/shard_map/ppermute | solution.py:530
  83.7 16.0 %all_to_all.5.total = f32[16,4,128]{2,1,0:T(4,128)S(1)} all-to-all(f32[16,4,128]{2,1,0:T(4,128)S(1)} %broadcast_in_dim.2), channel_id=1, replica_groups=mesh['samples'=4,'px'=16,'py'=2] {'px'}, dimensions={0} | all-to-all | bytes 65536 | tf_op jit(solution)/shard_map/all_to_all | solution.py:531
  99.7 2.4 %finish.1 = f32[2,256,16,128]{3,2,1,0:T(8,128)} custom-call(f32[16,4,128]{2,1,0:T(4,128)S(1)} %all_to_all.5.total, f32[2,256,8,128]{3,2,1,0:T(8,128)S(1)} %get-tuple-element.81.ps0, f32[2,256,8,128]{3,2,1,0:T(8,128)S(1)} %get-tuple-element.82.ps1), custom_call_target="tpu_custom_call" | custom-call | flops 10000000 | bytes 8388608 | tf_op jit(solution)/shard_map/finish/pallas_call | solution.py:532
  (15 shorter events, 0.0 us)
Async XLA Ops:
  0.0 7.4 %copy-start = (f32[4,256,256]{2,1,0:T(8,128)S(1)}, f32[4,256,256]{2,1,0:T(8,128)}, u32[]{:S(2)}) copy-start(f32[4,256,256]{2,1,0:T(8,128)} %constant.5.clone.root) | copy-start | bytes 3145732
  0.0 1.0 %copy-start.2 = (bf16[2,256,256]{2,1,0:T(8,128)(2,1)S(1)}, bf16[2,256,256]{2,1,0:T(8,128)(2,1)}, u32[]{:S(2)}) copy-start(bf16[2,256,256]{2,1,0:T(8,128)(2,1)} %constant.4.clone.s_hbm.s_ref) | copy-start | bytes 786436
  4.6 2.8 %collective-permute-start = (f32[2,16,64,128]{3,2,1,0:T(8,128)S(1)}, f32[2,16,64,128]{3,2,1,0:T(8,128)S(1)}, u32[]{:S(2)}, u32[]{:S(2)}) collective-permute-start(f32[2,16,64,128]{3,2,1,0:T(8,128)S(1)} %get-tuple-element.45), channel_id=1, source_target_pairs={{0,1},{1,0},{2,3},{3,2},{4,5},{5,4},{6,7},{7,6},{8,9},{9,8},{10,11... | collective-permute-start | bytes 3145736 | tf_op jit(solution)/shard_map/ppermute | solution.py:433
  5.7 5.6 %collective-permute-start.8 = (f32[2,16,64,128]{3,2,1,0:T(8,128)S(1)}, f32[2,16,64,128]{3,2,1,0:T(8,128)S(1)}, u32[]{:S(2)}, u32[]{:S(2)}) collective-permute-start(f32[2,16,64,128]{3,2,1,0:T(8,128)S(1)} %get-tuple-element.58), channel_id=1, source_target_pairs={{0,1},{1,0},{2,3},{3,2},{4,5},{5,4},{6,7},{7,6},{8,9},{9,8},{10,11... | collective-permute-start | bytes 3145736 | tf_op jit(solution)/shard_map/ppermute | solution.py:433
  9.1 6.0 %collective-permute-start.1 = (f32[2,64,256]{2,1,0:T(8,128)S(1)}, f32[2,64,256]{2,1,0:T(8,128)S(1)}, u32[]{:S(2)}, u32[]{:S(2)}) collective-permute-start(f32[2,64,256]{2,1,0:T(8,128)S(1)} %get-tuple-element.47), channel_id=1, source_target_pairs={{0,2},{4,6},{8,10},{12,14},{16,18},{20,22},{24,26},{28,30},{30,28}... | collective-permute-start | bytes 393224 | tf_op jit(solution)/shard_map/ppermute | solution.py:481
  13.6 5.3 %collective-permute-start.9 = (f32[2,64,256]{2,1,0:T(8,128)S(1)}, f32[2,64,256]{2,1,0:T(8,128)S(1)}, u32[]{:S(2)}, u32[]{:S(2)}) collective-permute-start(f32[2,64,256]{2,1,0:T(8,128)S(1)} %get-tuple-element.61), channel_id=1, source_target_pairs={{0,2},{4,6},{8,10},{12,14},{16,18},{20,22},{24,26},{28,30},{30,28}... | collective-permute-start | bytes 393224 | tf_op jit(solution)/shard_map/ppermute | solution.py:481
  15.2 8.2 %collective-permute-start.2 = (f32[2,64,256]{2,1,0:T(8,128)S(1)}, f32[2,64,256]{2,1,0:T(8,128)S(1)}, u32[]{:S(2)}, u32[]{:S(2)}) collective-permute-start(f32[2,64,256]{2,1,0:T(8,128)S(1)} %get-tuple-element.48.now), channel_id=1, source_target_pairs={{2,6},{10,14},{18,22},{26,30},{28,24},{20,16},{12,8},{4,0},{3,7},{... | collective-permute-start | bytes 393224 | tf_op jit(solution)/shard_map/ppermute | solution.py:491
  19.5 7.9 %collective-permute-start.10 = (f32[2,64,256]{2,1,0:T(8,128)S(1)}, f32[2,64,256]{2,1,0:T(8,128)S(1)}, u32[]{:S(2)}, u32[]{:S(2)}) collective-permute-start(f32[2,64,256]{2,1,0:T(8,128)S(1)} %get-tuple-element.63.now), channel_id=1, source_target_pairs={{2,6},{10,14},{18,22},{26,30},{28,24},{20,16},{12,8},{4,0},{3,7},{... | collective-permute-start | bytes 393224 | tf_op jit(solution)/shard_map/ppermute | solution.py:491
  23.5 4.7 %collective-permute-start.3 = (f32[2,64,256]{2,1,0:T(8,128)S(1)}, f32[2,64,256]{2,1,0:T(8,128)S(1)}, u32[]{:S(2)}, u32[]{:S(2)}) collective-permute-start(f32[2,64,256]{2,1,0:T(8,128)S(1)} %fold.11.now), channel_id=1, source_target_pairs={{6,14},{24,16},{7,15},{25,17},{38,46},{56,48},{39,47},{57,49},{70,... | collective-permute-start | bytes 393224 | tf_op jit(solution)/shard_map/ppermute | solution.py:491
  27.4 2.9 %collective-permute-start.11 = (f32[2,64,256]{2,1,0:T(8,128)S(1)}, f32[2,64,256]{2,1,0:T(8,128)S(1)}, u32[]{:S(2)}, u32[]{:S(2)}) collective-permute-start(f32[2,64,256]{2,1,0:T(8,128)S(1)} %fold.16.now), channel_id=1, source_target_pairs={{6,14},{24,16},{7,15},{25,17},{38,46},{56,48},{39,47},{57,49},{70,... | collective-permute-start | bytes 393224 | tf_op jit(solution)/shard_map/ppermute | solution.py:491
  28.2 2.9 %collective-permute-start.4 = (f32[2,64,256]{2,1,0:T(8,128)S(1)}, f32[2,64,256]{2,1,0:T(8,128)S(1)}, u32[]{:S(2)}, u32[]{:S(2)}) collective-permute-start(f32[2,64,256]{2,1,0:T(8,128)S(1)} %fold.12.now), channel_id=1, source_target_pairs={{14,22},{16,8},{15,23},{17,9},{46,54},{48,40},{47,55},{49,41},{78,... | collective-permute-start | bytes 393224 | tf_op jit(solution)/shard_map/ppermute | solution.py:491
  30.4 1.5 %collective-permute-start.12 = (f32[2,64,256]{2,1,0:T(8,128)S(1)}, f32[2,64,256]{2,1,0:T(8,128)S(1)}, u32[]{:S(2)}, u32[]{:S(2)}) collective-permute-start(f32[2,64,256]{2,1,0:T(8,128)S(1)} %fold.17.now), channel_id=1, source_target_pairs={{14,22},{16,8},{15,23},{17,9},{46,54},{48,40},{47,55},{49,41},{78,... | collective-permute-start | bytes 393224 | tf_op jit(solution)/shard_map/ppermute | solution.py:491
  31.2 1.5 %collective-permute-start.5 = (f32[2,64,256]{2,1,0:T(8,128)S(1)}, f32[2,64,256]{2,1,0:T(8,128)S(1)}, u32[]{:S(2)}, u32[]{:S(2)}) collective-permute-start(f32[2,64,256]{2,1,0:T(8,128)S(1)} %fold.13.now), channel_id=1, source_target_pairs={{6,10},{14,18},{22,26},{24,20},{16,12},{8,4},{7,11},{15,19},{23,27... | collective-permute-start | bytes 393224 | tf_op jit(solution)/shard_map/ppermute | solution.py:491
  32.0 1.6 %collective-permute-start.13 = (f32[2,64,256]{2,1,0:T(8,128)S(1)}, f32[2,64,256]{2,1,0:T(8,128)S(1)}, u32[]{:S(2)}, u32[]{:S(2)}) collective-permute-start(f32[2,64,256]{2,1,0:T(8,128)S(1)} %fold.18.now), channel_id=1, source_target_pairs={{6,10},{14,18},{22,26},{24,20},{16,12},{8,4},{7,11},{15,19},{23,27... | collective-permute-start | bytes 393224 | tf_op jit(solution)/shard_map/ppermute | solution.py:491
  32.8 1.6 %collective-permute-start.6 = (f32[2,64,256]{2,1,0:T(8,128)S(1)}, f32[2,64,256]{2,1,0:T(8,128)S(1)}, u32[]{:S(2)}, u32[]{:S(2)}) collective-permute-start(f32[2,64,256]{2,1,0:T(8,128)S(1)} %fold.14), channel_id=1, source_target_pairs={{2,4},{6,8},{10,12},{14,16},{18,20},{22,24},{26,28},{28,26},{24,22... | collective-permute-start | bytes 393224 | tf_op jit(solution)/shard_map/ppermute | solution.py:495
  33.7 33.7 %collective-permute-start.14 = (f32[2,64,256]{2,1,0:T(8,128)S(1)}, f32[2,64,256]{2,1,0:T(8,128)S(1)}, u32[]{:S(2)}, u32[]{:S(2)}) collective-permute-start(f32[2,64,256]{2,1,0:T(8,128)S(1)} %fold.19), channel_id=1, source_target_pairs={{2,4},{6,8},{10,12},{14,16},{18,20},{22,24},{26,28},{28,26},{24,22... | collective-permute-start | bytes 393224 | tf_op jit(solution)/shard_map/ppermute | solution.py:495
  34.4 37.1 %collective-permute-start.7 = (f32[2,64,256]{2,1,0:T(8,128)S(1)}, f32[2,64,256]{2,1,0:T(8,128)S(1)}, u32[]{:S(2)}, u32[]{:S(2)}) collective-permute-start(f32[2,64,256]{2,1,0:T(8,128)S(1)} %collective-permute-done.6.one), channel_id=1, source_target_pairs={{0,2},{4,6},{8,10},{12,14},{16,18},{20,22},{24,26},{28,30},{30,28}... | collective-permute-start | bytes 393224 | tf_op jit(solution)/shard_map/ppermute | solution.py:496
  67.5 7.0 %collective-permute-start.15 = (f32[2,64,256]{2,1,0:T(8,128)S(1)}, f32[2,64,256]{2,1,0:T(8,128)S(1)}, u32[]{:S(2)}, u32[]{:S(2)}) collective-permute-start(f32[2,64,256]{2,1,0:T(8,128)S(1)} %collective-permute-done.14.one), channel_id=1, source_target_pairs={{0,2},{4,6},{8,10},{12,14},{16,18},{20,22},{24,26},{28,30},{30,28}... | collective-permute-start | bytes 393224 | tf_op jit(solution)/shard_map/ppermute | solution.py:496
  72.8 4.6 %collective-permute-start.18 = (f32[2,8,64,128]{3,2,1,0:T(8,128)S(1)}, f32[2,8,64,128]{3,2,1,0:T(8,128)S(1)}, u32[]{:S(2)}, u32[]{:S(2)}) collective-permute-start(f32[2,8,64,128]{3,2,1,0:T(8,128)S(1)} %get-tuple-element.78), channel_id=1, source_target_pairs={{0,1},{1,0},{2,3},{3,2},{4,5},{5,4},{6,7},{7,6},{8,9},{9,8},{10,11... | collective-permute-start | bytes 1572872 | tf_op jit(solution)/shard_map/ppermute | solution.py:515
  73.7 4.0 %copy-start.1 = (f32[2,256,16,128]{3,2,1,0:T(8,128)S(1)}, f32[2,256,16,128]{3,2,1,0:T(8,128)}, u32[]{:S(2)}) copy-start(f32[2,256,16,128]{3,2,1,0:T(8,128)} %refs_4_.3) | copy-start | bytes 12582916
  73.7 4.0 %copy-start.3 = (f32[256,16,128]{2,1,0:T(8,128)S(1)}, f32[256,16,128]{2,1,0:T(8,128)}, u32[]{:S(2)}) copy-start(f32[256,16,128]{2,1,0:T(8,128)} %refs_5_.3) | copy-start | bytes 6291460
  75.7 2.0 %collective-permute-start.19 = (f32[2,8,64,128]{3,2,1,0:T(8,128)S(1)}, f32[2,8,64,128]{3,2,1,0:T(8,128)S(1)}, u32[]{:S(2)}, u32[]{:S(2)}) collective-permute-start(f32[2,8,64,128]{3,2,1,0:T(8,128)S(1)} %get-tuple-element.79), channel_id=1, source_target_pairs={{0,1},{1,0},{2,3},{3,2},{4,5},{5,4},{6,7},{7,6},{8,9},{9,8},{10,11... | collective-permute-start | bytes 1572872 | tf_op jit(solution)/shard_map/ppermute | solution.py:515
  75.8 4.2 %collective-permute-start.16 = (f32[2,8,64,128]{3,2,1,0:T(8,128)S(1)}, f32[2,8,64,128]{3,2,1,0:T(8,128)S(1)}, u32[]{:S(2)}, u32[]{:S(2)}) collective-permute-start(f32[2,8,64,128]{3,2,1,0:T(8,128)S(1)} %get-tuple-element.71), channel_id=1, source_target_pairs={{0,1},{1,0},{2,3},{3,2},{4,5},{5,4},{6,7},{7,6},{8,9},{9,8},{10,11... | collective-permute-start | bytes 1572872 | tf_op jit(solution)/shard_map/ppermute | solution.py:515
  77.1 2.9 %collective-permute-start.17 = (f32[2,8,64,128]{3,2,1,0:T(8,128)S(1)}, f32[2,8,64,128]{3,2,1,0:T(8,128)S(1)}, u32[]{:S(2)}, u32[]{:S(2)}) collective-permute-start(f32[2,8,64,128]{3,2,1,0:T(8,128)S(1)} %get-tuple-element.72), channel_id=1, source_target_pairs={{0,1},{1,0},{2,3},{3,2},{4,5},{5,4},{6,7},{7,6},{8,9},{9,8},{10,11... | collective-permute-start | bytes 1572872 | tf_op jit(solution)/shard_map/ppermute | solution.py:515
  82.4 1.3 %collective-permute-start.20 = (f32[4,128]{1,0:T(4,128)S(1)}, f32[4,128]{1,0:T(4,128)S(1)}, u32[]{:S(2)}, u32[]{:S(2)}) collective-permute-start(f32[4,128]{1,0:T(4,128)S(1)} %add.6), channel_id=1, source_target_pairs={{0,1},{1,0},{2,3},{3,2},{4,5},{5,4},{6,7},{7,6},{8,9},{9,8},{10,11... | collective-permute-start | bytes 6152 | tf_op jit(solution)/shard_map/ppermute | solution.py:530
